TPU v7x, 512 devices: a whole 4x4x16 slice. The times are simulated.
512 devices in a mesh: contract: 32 (over z, y_lo), out: 16 (over y_hi, x, core).
Axes of the slice: x: 4, y: 4 (y_hi: 2, y_lo: 2; y = y_hi * 2 + y_lo), z: 16, core: 2. Of those that a mesh axis runs over, the one named last changes fastest.
Arguments:
- chol: bfloat16 [128, 1024, 640], P('out', 'contract'), may hold values from -1.1953125 to 1.1953125
- amplitudes: bfloat16 [128, 32768], P('out', 'contract'), may hold values from -0.0625 to 0.0625
- tile_pairs: int32 [64, 2], replicated, may hold values from 0 to 7, as said below
- partner: int32 [64], replicated, may hold values from 0 to 63, as said below
- pair_swap: int32 [128], replicated, may hold values from 0 to 127, as said below
Outputs:
- residual: float32 [64, 128, 256], P('out', 'contract')
Inputs may be any that keep to these rules, and one draw needn't show every extreme that they name: `tile_pairs`: each ordered pair of tiles of 0 to 7 stands at exactly one slot. partner[s] is the slot holding the pair of slot s reversed; a diagonal pair is its own partner. `pair_swap`: an involution without fixed points that maps each aligned block of 4 pairs into itself.
All inputs are finite; a program needn't handle non-finite values.
Results may differ from a plain program's by a relative error of at most 0.0029.
Values may be sent and summed in bfloat16 or wider, within the bound.
No kernel may reach another device: no remote copies, remote signals or barrier semaphores. Data moves between devices by JAX's collectives and lax.ppermute only.
A program may use at most 128 MiB of HBM per device.

v0:
```python
import jax
import jax.numpy as jnp
from jax import lax
from jax.sharding import Mesh
from jax.sharding import PartitionSpec as P

TS = 16
CONTRACT = ("contract_0", "contract_1")


def broadcast_by_axis(array, axes, root):
    array = jnp.where(lax.axis_index(axes) == root, array, jnp.zeros_like(array))
    for axis in axes:
        array = lax.psum(array, axis)
    return array


def cut_along(array, dim, count):
    before, after = (array.shape[:dim], array.shape[dim + 1 :])
    return jnp.moveaxis(array.reshape(*before, count, -1, *after), dim, 0)


def sum_at_owner(array, axis, dim):
    count = lax.axis_size(axis)
    parts = lax.all_to_all(cut_along(array, dim, count), axis, 0, 0, tiled=True)
    return jnp.sum(parts, axis=0)


def laid_out(parts, dim):
    lengths = list(parts.shape[1:])
    lengths[dim] *= parts.shape[0]
    return jnp.moveaxis(parts, 0, dim).reshape(lengths)


def sent_to_all(array, axis):
    count = lax.axis_size(axis)
    return lax.all_to_all(
        jnp.broadcast_to(array[None], (count, *array.shape)), axis, 0, 0, tiled=True
    )


def collect(array, axis, dim):
    return laid_out(sent_to_all(array, axis), dim)


def pick_tile(source, tile):
    return lax.dynamic_slice_in_dim(source, tile * TS, TS, 0)


def on_device(chol, amplitudes, tile_pairs, partner, pair_swap):
    out_count = lax.axis_size("out")
    con_count = lax.axis_size(CONTRACT)
    out_index = lax.axis_index("out")
    con_index = lax.axis_index(CONTRACT)
    local_window = broadcast_by_axis(chol, CONTRACT, 0)
    rows_all, window, amps_all = (
        lax.all_gather(chol, "out", axis=0, tiled=True),
        lax.all_gather(local_window, "out", axis=0, tiled=True),
        lax.all_gather(amplitudes, "out", axis=0, tiled=True),
    )
    slot_count = tile_pairs.shape[0] // out_count
    first = out_index * slot_count
    pairs = lax.dynamic_slice_in_dim(tile_pairs, first, slot_count, 0)
    left = jax.vmap(pick_tile, (None, 0))(rows_all, pairs[:, 0])
    right = jax.vmap(pick_tile, (None, 0))(window, pairs[:, 1])
    integral = jnp.einsum(
        "sacp,sbdp->sabcd", left, right, preferred_element_type=jnp.float32
    ).astype(jnp.bfloat16)
    flat = integral.reshape(slot_count * TS * TS, -1)
    occ_dev = amps_all.shape[0] // con_count
    ladder = sum_at_owner(
        lax.dot_general(
            amps_all, flat, (((1,), (1,)), ((), ())), preferred_element_type=jnp.float32
        ),
        CONTRACT,
        0,
    )
    ladder = jnp.transpose(ladder.reshape(occ_dev, slot_count, TS, TS), (1, 0, 2, 3))
    own_swap = (
        lax.dynamic_slice_in_dim(pair_swap, con_index * occ_dev, occ_dev, 0) - con_index * occ_dev
    )
    turned = jnp.transpose(jnp.take(ladder, own_swap, axis=1), (0, 1, 3, 2))
    turned = turned.reshape(slot_count, occ_dev, TS * TS)
    every = collect(turned, "out", 0)
    wanted = lax.dynamic_slice_in_dim(partner, first, slot_count, 0)
    mirror = jnp.take(every, wanted, axis=0)
    return ladder.reshape(slot_count, occ_dev, TS * TS) + mirror


def solution(mesh):
    torus = Mesh(
        mesh.devices.reshape(16, 2, mesh.shape["out"]), ("contract_0", "contract_1", "out")
    )
    in_specs = (P("out", CONTRACT, None), P("out", CONTRACT), P(), P(), P())
    out_specs = P("out", CONTRACT, None)
    return jax.shard_map(
        on_device, mesh=torus, in_specs=in_specs, out_specs=out_specs, check_vma=False
    )
```

profile of v0, /device:TPU:1, one launch (start us, length us, event | category | flops | bytes accessed | tf_op | source)
XLA Modules:
  0.0 417.8 jit_solution(8291045161352591324)
XLA Ops:
  7.4 1.7 broadcast_select_fusion
  9.2 133.9 %all-reduce.5.cloned.1.call-done = bf16[8,32,640]{2,1,0:T(8,128)(2,1)} async-done(((bf16[8,32,640]{2,1,0:T(8,128)(2,1)}), bf16[8,32,640]{2,1,0:T(8,128)(2,1)}) %all-reduce.5.cloned.1.call-update) | async-done | bytes 327696 | tf_op jit(solution)/shard_map/psum | solution.py:14
  143.1 0.0 all-gather.5.cloned.1.call-start
  143.1 0.5 all-gather.5.cloned.1.call-update
  143.7 55.1 %all-reduce.7.cloned.1.call-done = bf16[8,32,640]{2,1,0:T(8,128)(2,1)} async-done(((bf16[8,32,640]{2,1,0:T(8,128)(2,1)}), bf16[8,32,640]{2,1,0:T(8,128)(2,1)}) %all-reduce.7.cloned.1.call-update) | async-done | bytes 327696 | tf_op jit(solution)/shard_map/psum | solution.py:14
  198.8 0.1 constant_dynamic-slice_fusion
  198.9 25.7 %all_gather.11 = bf16[128,1024]{1,0:T(8,128)(2,1)S(1)} all-gather(bf16[8,1024]{1,0:T(8,128)(2,1)} %param.6), channel_id=1, replica_groups=mesh['contract_0'=16,'contract_1'=2,'out'=16] {'out'}, dimensions={0}, use_global_device_ids=true | all-gather | bytes 278528 | tf_op jit(solution)/shard_map/all_gather | solution.py:59
  224.6 4.9 %all-gather.5.cloned.1.call-done = bf16[128,32,640]{2,1,0:T(8,128)(2,1)} async-done(((bf16[8,32,640]{2,1,0:T(8,128)(2,1)}), bf16[128,32,640]{2,1,0:T(8,128)(2,1)}) %all-gather.5.cloned.1.call-update) | async-done | bytes 5242896 | tf_op jit(solution)/shard_map/all_gather | solution.py:57
  229.5 3.5 gather_fusion.1
  233.0 74.3 %all-gather.3.cloned.1.call-done = bf16[128,32,640]{2,1,0:T(8,128)(2,1)} async-done(((bf16[8,32,640]{2,1,0:T(8,128)(2,1)}), bf16[128,32,640]{2,1,0:T(8,128)(2,1)}) %all-gather.3.cloned.1.call-update) | async-done | bytes 5242896 | tf_op jit(solution)/shard_map/all_gather | solution.py:58
  307.3 4.9 %gather_fusion = bf16[4,16,32,640]{3,2,1,0:T(8,128)(2,1)} fusion(bf16[128,32,640]{2,1,0:T(8,128)(2,1)} %all-gather.3.cloned.1.call-done, s32[4]{0:T(128)S(1)} %get-tuple-element.9), kind=kCustom, calls=%fused_computation | custom fusion | bytes 5242928 | tf_op jit(solution)/shard_map/vmap()/gather | solution.py:47
  312.3 10.4 %convert_bitcast_fusion = bf16[4,16,16,32,32]{3,4,1,2,0:T(8,128)(2,1)} fusion(bf16[4,16,32,640]{3,2,1,0:T(8,128)(2,1)S(1)} %gather_fusion.1, bf16[4,16,32,640]{3,2,1,0:T(8,128)(2,1)} %gather_fusion), kind=kOutput, calls=%fused_computation.4 | convolution fusion | flops 1343225856 | bytes 7340032 | tf_op jit(solution)/shard_map/sacp,sbdp->sabcd/dot_general | solution.py:66
  322.6 11.5 %copy.9 = bf16[4,16,16,32,32]{4,3,2,1,0:T(8,128)(2,1)} copy(bf16[4,16,16,32,32]{3,4,1,2,0:T(8,128)(2,1)} %convert_bitcast_fusion) | data formatting | bytes 4194304 | tf_op jit(solution)/shard_map/convert_element_type | solution.py:68
  334.1 11.3 %reshape.26 = bf16[1024,1024]{1,0:T(8,128)(2,1)S(1)} reshape(bf16[4,16,16,32,32]{4,3,2,1,0:T(8,128)(2,1)} %copy.9) | data formatting | bytes 4194304 | tf_op jit(solution)/shard_map/reshape | solution.py:69
  345.4 0.8 convolution_bitcast_fusion
  346.3 0.9 reshape.27
  347.2 12.3 %all-to-all-start = ((f32[32,4,1024]{2,1,0:T(4,128)}), f32[32,4,1024]{2,1,0:T(4,128)S(1)}, u32[]{:S(2)}, u32[]{:S(2)}) async-start(f32[32,4,1024]{2,1,0:T(4,128)} %reshape.27), calls=%async_computation | async-start | bytes 1048576 | tf_op jit(solution)/shard_map/all_to_all | solution.py:25
  359.6 0.1 compare_and_fusion
  359.7 32.0 %all-to-all-done = f32[32,4,1024]{2,1,0:T(4,128)S(1)} async-done(((f32[32,4,1024]{2,1,0:T(4,128)}), f32[32,4,1024]{2,1,0:T(4,128)S(1)}, u32[]{:S(2)}, u32[]{:S(2)}) %all-to-all-start) | async-done | bytes 524320 | tf_op jit(solution)/shard_map/all_to_all | solution.py:25
  391.7 0.1 reduce_sum.9
  391.8 0.1 reshape.28
  391.9 0.6 gather_fusion.2
  392.5 0.1 select_bitcast_fusion
  392.6 0.1 copy.11
  392.7 0.1 broadcast_in_dim.41
  392.8 0.8 broadcast_in_dim.42
  393.5 6.8 %all-to-all-start.1 = ((f32[16,4,4,256]{3,2,1,0:T(4,128)}), f32[16,4,4,256]{3,2,1,0:T(4,128)S(1)}, u32[]{:S(2)}, u32[]{:S(2)}) async-start(f32[16,4,4,256]{3,2,1,0:T(4,128)} %broadcast_in_dim.42), calls=%async_computation.1 | async-start | bytes 524288 | tf_op jit(solution)/shard_map/all_to_all | solution.py:37
  400.4 0.1 compare_and_fusion.1
  400.5 0.1 reshape.63
  400.6 8.5 %all-to-all-done.1 = f32[16,4,4,256]{3,2,1,0:T(4,128)S(1)} async-done(((f32[16,4,4,256]{3,2,1,0:T(4,128)}), f32[16,4,4,256]{3,2,1,0:T(4,128)S(1)}, u32[]{:S(2)}, u32[]{:S(2)}) %all-to-all-start.1) | async-done | bytes 262176 | tf_op jit(solution)/shard_map/all_to_all | solution.py:37
  409.1 0.6 gather_fusion.3
  409.6 0.7 copy_add_fusion
  (15 shorter events, 0.2 us)
Async XLA Ops:
  7.4 191.4 %copy-start = (s32[64,2]{0,1:T(2,128)S(1)}, s32[64,2]{0,1:T(2,128)}, u32[]{:S(2)}) copy-start(s32[64,2]{0,1:T(2,128)} %param.7) | copy-start | bytes 1540
  7.4 135.7 %all-reduce.5.cloned.1.call-start = ((), (), s32[]{:S(2)}) async-start(), calls=%async_computation.2 | async-start | bytes 655360 | tf_op jit(solution)/shard_map/psum | solution.py:14
  9.1 189.6 %all-reduce.7.cloned.1.call-start = ((), (), s32[]{:S(2)}) async-start(), calls=%async_computation.3 | async-start | bytes 655360 | tf_op jit(solution)/shard_map/psum | solution.py:14
  143.1 86.4 %all-gather.5.cloned.1.call-start = ((), (), s32[]{:S(2)}) async-start(), calls=%async_computation.5 | async-start | bytes 5570560 | tf_op jit(solution)/shard_map/all_gather | solution.py:57
  143.6 163.7 %all-gather.3.cloned.1.call-start = ((), (), s32[]{:S(2)}) async-start(), calls=%async_computation.4 | async-start | bytes 5570560 | tf_op jit(solution)/shard_map/all_gather | solution.py:58
  345.4 14.1 %copy-start.1 = (s32[128]{0:T(128)S(1)}, s32[128]{0:T(128)}, u32[]{:S(2)}) copy-start(s32[128]{0:T(128)} %param.9) | copy-start | bytes 1540
  346.3 54.1 %copy-start.2 = (s32[64]{0:T(128)S(1)}, s32[64]{0:T(128)}, u32[]{:S(2)}) copy-start(s32[64]{0:T(128)} %param.8) | copy-start | bytes 772
  347.2 44.5 %all-to-all-start = ((f32[32,4,1024]{2,1,0:T(4,128)}), f32[32,4,1024]{2,1,0:T(4,128)S(1)}, u32[]{:S(2)}, u32[]{:S(2)}) async-start(f32[32,4,1024]{2,1,0:T(4,128)} %reshape.27), calls=%async_computation | async-start | bytes 1048576 | tf_op jit(solution)/shard_map/all_to_all | solution.py:25
  393.5 15.5 %all-to-all-start.1 = ((f32[16,4,4,256]{3,2,1,0:T(4,128)}), f32[16,4,4,256]{3,2,1,0:T(4,128)S(1)}, u32[]{:S(2)}, u32[]{:S(2)}) async-start(f32[16,4,4,256]{3,2,1,0:T(4,128)} %broadcast_in_dim.42), calls=%async_computation.1 | async-start | bytes 524288 | tf_op jit(solution)/shard_map/all_to_all | solution.py:37
Sparse Core Ops, SparseCore 0:
  10.5 132.4 all-reduce.4
  145.9 52.8 all-reduce.6
Sparse Core Ops, SparseCore 1:
  146.8 82.6 all-gather.4
  232.7 74.6 all-gather.2
where the time goes:
time: 419 us; the launch traced here: 418 us
  waiting for transfers between devices  309 us (74%)
  local copies, waits for them, and re-layouts  34.5 us (8%)
  blocking collectives  25.7 us (6%)
  starting transfers between devices  19.3 us (5%)
  between operations  15 us (4%)
  matrix products  11.2 us (3%)
    psum x2, waiting for transfers between devices, broadcast_by_axis(): array = lax.psum(array, axis)  189 us
    all_gather x1, waiting for transfers between devices, on_device(): lax.all_gather(local_window, 'out', axis=0, tiled=True)  74.3 us
    all_to_all x1, waiting for transfers between devices, sum_at_owner(): parts = lax.all_to_all(cut_along(array, dim, count), axis, 0, 0, tiled=True)  32 us
    all_gather x1, blocking collectives, on_device(): lax.all_gather(amplitudes, 'out', axis=0, tiled=True)  25.7 us
    all_to_all x1, starting transfers between devices, sum_at_owner(): parts = lax.all_to_all(cut_along(array, dim, count), axis, 0, 0, tiled=True)  12.3 us
    convert_element_type x1, local copies, waits for them, and re-layouts, on_device(): integral = jnp.einsum('sacp,sbdp->sabcd', left, right, preferred_element_...  11.5 us
    reshape x1, local copies, waits for them, and re-layouts, on_device(): flat = integral.reshape(slot_count * TS * TS, -1)  11.3 us
    dot_general x1, matrix products, on_device(): jnp.einsum('sacp,sbdp->sabcd', left, right, preferred_element_type=jnp.fl...  10.4 us
  transfers between devices with their start and end apart: 6, of which 6 were waited for; matrix products, arithmetic and copies ran while one was open for 1% of the time, Pallas kernels for 0%

commit v1 on v0

v1 whole, which is shorter than its diff:
```python
import functools

import jax
import jax.numpy as jnp
from jax import lax
from jax.experimental import pallas as pl
from jax.experimental.pallas import tpu as pltpu
from jax.sharding import Mesh
from jax.sharding import PartitionSpec as P

TS = 16
LANES = 128
CONTRACT = ("z", "yl")
OUT = ("yh", "x", "core")
PAIR = [(0, 1), (1, 0)]


def exchange(array, axes):
    return lax.all_to_all(array, axes, 0, 0, tiled=True)


def sent_to_all(array, axes):
    count = lax.axis_size(axes)
    return exchange(jnp.broadcast_to(array[None], (count, *array.shape)), axes)


def ladder_kernel(
    place_ref, near_ref, far_ref, amps_ref, amps_far_ref, own_ref, opposite_ref, out_ref, stack_ref
):
    core, x_here, yh = place_ref[0], place_ref[1], place_ref[2]
    _, ring, pair_rows, _ = near_ref.shape
    c_pairs = near_ref.shape[0] - 1
    a_dev = pair_rows // 2
    b_count, depth, _ = stack_ref.shape
    b_dev = b_count // 2
    d_count = own_ref.shape[0] // b_dev
    order = [lax.rem(x_here + ring - x, ring) for x in range(ring)]
    right = jnp.concatenate([own_ref[...], opposite_ref[...]], axis=0)
    for n in range(0, c_pairs, 2):
        left = jnp.concatenate(
            [ref[m, order[x]] for m in (n, n + 1) for ref in (near_ref, far_ref) for x in range(ring)],
            axis=0,
        )
        part = lax.dot_general(
            right, left, (((1,), (1,)), ((), ())), preferred_element_type=jnp.float32
        ).astype(jnp.bfloat16)
        part = part.reshape(b_count, d_count, 2 * LANES)
        for h in range(2):
            rows = (n + h) * d_count
            stack_ref[:, rows : rows + d_count, :] = part[:, :, h * LANES : (h + 1) * LANES]
    amps = jnp.concatenate(
        [amps_ref[q, :, :depth] for q in range(amps_ref.shape[0])]
        + [amps_far_ref[q, :, :depth] for q in range(amps_far_ref.shape[0])],
        axis=0,
    )
    blocks = amps.shape[0] // pair_rows
    odd = lax.rem(lax.broadcasted_iota(jnp.int32, (1, 1, LANES), 2) // a_dev, 2) == 1
    for q in range(b_count // 2):
        sums = []
        for b, step in ((2 * q, LANES - a_dev), (2 * q + 1, a_dev)):
            full = jnp.dot(amps, stack_ref[b], preferred_element_type=jnp.float32)
            full = full.reshape(blocks, 2, a_dev, LANES)
            mixed = jnp.where(odd, full[:, 1], full[:, 0]).reshape(blocks * a_dev, LANES)
            sums.append(mixed + pltpu.roll(mixed, step, 1))
        found = jnp.where(odd[0], sums[1], sums[0])
        found = pltpu.roll(found, core * (LANES // 2), 1)
        half = lax.rem(yh + q // (b_count // 4), 2)
        column = pl.multiple_of((half * (b_count // 4) + q % (b_count // 4)) * LANES, LANES)
        for block in range(blocks):
            other_yh, other_core, shift = block // (2 * ring), block // ring % 2, block % ring
            source = lax.rem(x_here + ring - shift, ring)
            place = (lax.rem(yh + other_yh, 2) * ring + source) * 2 + lax.rem(core + other_core, 2)
            for h in range(2):
                rows = found[block * a_dev + h * (a_dev // 2) : block * a_dev + (h + 1) * (a_dev // 2)]
                out_ref[2 * place + h, :, pl.ds(column, LANES)] = rows


def ladder_partials(place, near, far, amps, amps_far, own, opposite, i_count, con_count):
    b_count = 2 * near.shape[2] // 2
    d_count = own.shape[0] // (b_count // 2)
    depth = (near.shape[0] - 1) * d_count
    pairs = 2 * near.size * (2 * own.shape[0])
    return pl.pallas_call(
        ladder_kernel,
        out_shape=jax.ShapeDtypeStruct(
            (con_count, i_count // con_count, b_count * LANES // 2), jnp.float32
        ),
        in_specs=[pl.BlockSpec(memory_space=pltpu.SMEM)]
        + [pl.BlockSpec(memory_space=pltpu.VMEM)] * 6,
        out_specs=pl.BlockSpec(memory_space=pltpu.VMEM),
        scratch_shapes=[pltpu.VMEM((b_count, depth, LANES), jnp.bfloat16)],
        compiler_params=pltpu.CompilerParams(vmem_limit_bytes=20 * 1024 * 1024),
        cost_estimate=pl.CostEstimate(
            flops=2 * pairs, bytes_accessed=4 * near.size, transcendentals=0
        ),
    )(place, near, far, amps, amps_far, own, opposite)


def on_device(chol, amplitudes, tile_pairs, partner, pair_swap):
    out_count = lax.axis_size(OUT)
    con_count = lax.axis_size(CONTRACT)
    ring = lax.axis_size("x")
    a_dev, c_dev, p_size = chol.shape
    i_dev = amplitudes.shape[0]
    i_count = i_dev * out_count
    half = c_dev // 2
    pair_rows = 2 * a_dev

    with jax.named_scope("pack"):
        rows = jnp.transpose(chol.reshape(a_dev, 2, half, p_size), (2, 1, 0, 3))
        extra = jnp.transpose(amplitudes.reshape(i_dev, 2, -1), (1, 0, 2)).reshape(1, pair_rows, -1)
        extra = jnp.pad(extra, ((0, 0), (0, 0), (0, p_size - extra.shape[2])))
        packed = jnp.concatenate([rows.reshape(half, pair_rows, p_size), extra], axis=0)
    with jax.named_scope("ring"):
        near = [packed] + [
            lax.ppermute(packed, "x", [(x, (x + shift) % ring) for x in range(ring)])
            for shift in range(1, ring)
        ]
        near = jnp.stack(near, axis=1)

    with jax.named_scope("scatter"):
        slices = exchange(chol.reshape(con_count, -1, p_size), CONTRACT)
    with jax.named_scope("spread"):
        own = sent_to_all(slices[0], CONTRACT).reshape(a_dev * c_dev, p_size)

    with jax.named_scope("cores"):
        far = lax.ppermute(near, "core", PAIR)
    with jax.named_scope("amps"):
        amps = jnp.concatenate([near[half], far[half]], axis=0)
        amps_far = lax.ppermute(amps, "yh", PAIR)
    with jax.named_scope("window"):
        opposite = lax.ppermute(own, "yh", PAIR)

    place = jnp.stack([lax.axis_index("core"), lax.axis_index("x"), lax.axis_index("yh")])
    partial = ladder_partials(
        place, near, far, amps, amps_far, own, opposite, i_count, con_count
    )
    ladder = jnp.sum(exchange(partial, CONTRACT), axis=0)

    occ_dev = i_count // con_count
    ladder = ladder.reshape(occ_dev, 2, a_dev // 2, 2, ring, 2, a_dev)
    ladder = jnp.transpose(ladder, (4, 1, 0, 3, 6, 2, 5)).reshape(2 * ring, occ_dev, TS * a_dev)
    every = sent_to_all(ladder, OUT).reshape(-1, occ_dev, TS * a_dev)

    slot_count = tile_pairs.shape[0] // out_count
    first = lax.axis_index(OUT) * slot_count
    pairs = lax.dynamic_slice_in_dim(tile_pairs, first, slot_count, 0)

    def whole_tiles(a_tile, b_tile):
        holder = (a_tile // ring * ring + b_tile % ring) * 2
        inner = a_tile % ring * 2 + b_tile // ring
        spots = (holder[:, None] + jnp.arange(2)) * (2 * ring) + inner[:, None]
        found = jnp.take(every, spots.reshape(-1), axis=0, mode="clip")
        return found.reshape(slot_count, 2, occ_dev, TS, a_dev)

    own_swap = lax.dynamic_slice_in_dim(
        pair_swap, lax.axis_index(CONTRACT) * occ_dev, occ_dev, 0
    ) - lax.axis_index(CONTRACT) * occ_dev
    straight = jnp.transpose(whole_tiles(pairs[:, 0], pairs[:, 1]), (0, 2, 3, 1, 4))
    mirror = whole_tiles(pairs[:, 1], pairs[:, 0])
    mirror = jnp.take(mirror, own_swap, axis=2, mode="clip")
    mirror = jnp.transpose(mirror, (0, 2, 1, 4, 3))
    residual = straight.reshape(slot_count, occ_dev, TS, TS) + mirror.reshape(
        slot_count, occ_dev, TS, TS
    )
    return residual.reshape(slot_count, occ_dev, TS * TS)


def solution(mesh):
    torus = Mesh(mesh.devices.reshape(16, 2, 2, 4, 2), ("z", "yl", "yh", "x", "core"))
    in_specs = (P(OUT, CONTRACT, None), P(OUT, CONTRACT), P(), P(), P())
    out_specs = P(OUT, CONTRACT, None)
    return jax.shard_map(
        on_device, mesh=torus, in_specs=in_specs, out_specs=out_specs, check_vma=False
    )
```

time: 419 us -> 162 us (0.39)
  waiting for transfers between devices: 309 us -> 85.9 us
  starting transfers between devices: 19.3 us -> 61.5 us
  local copies, waits for them, and re-layouts: 34.5 us -> 7.11 us
  blocking collectives: 25.7 us -> 0 us
  between operations: 15 us -> 0.24 us
  matrix products: 11.2 us -> 0 us
  Pallas kernels: 0 us -> 4.89 us
    psum x2 -> x0, waiting for transfers between devices: 189 us -> none  [broadcast_by_axis(): array = lax.psum(array, axis)]
    all_gather x2 -> x0, waiting for transfers between devices: 79.2 us -> none  [the longest x1 74.3 us: on_device(): lax.all_gather(local_window, 'out', axis=0, tiled=True)]
    all_gather x1 -> x0, blocking collectives: 25.7 us -> none  [on_device(): lax.all_gather(amplitudes, 'out', axis=0, tiled=True)]
    all_to_all x2 -> x4, starting transfers between devices: 19.2 us -> 43 us  [exchange(): return lax.all_to_all(array, axes, 0, 0, tiled=True)]
    ppermute x0 -> x6, waiting for transfers between devices: none -> 23.4 us  [the longest x3 16 us: on_device(): lax.ppermute(packed, 'x', [(x, (x + shift) % ring) for x in range(ring)])]
    all_to_all x2 -> x4, waiting for transfers between devices: 40.5 us -> 62.5 us  [exchange(): return lax.all_to_all(array, axes, 0, 0, tiled=True)]
    ppermute x0 -> x6, starting transfers between devices: none -> 18.5 us  [the longest x3 9.33 us: on_device(): lax.ppermute(packed, 'x', [(x, (x + shift) % ring) for x in range(ring)])]
    convert_element_type x1 -> x0, local copies, waits for them, and re-layouts: 11.5 us -> none  [on_device(): integral = jnp.einsum('sacp,sbdp->sabcd', left, right, preferred_element_...]
  transfers between devices with their start and end apart: 6 -> 10, of which waited for: 6 -> 7; matrix products, arithmetic and copies ran while one was open for 1% -> 2% of each run, Pallas kernels for 0% -> 0%
where the time goes in v1:
time: 162 us
  waiting for transfers between devices  85.9 us (53%)
  starting transfers between devices  61.5 us (38%)
  local copies, waits for them, and re-layouts  7.11 us (4%)
  Pallas kernels  4.89 us (3%)
  other arithmetic  2.01 us (1%)
    all_to_all x4, waiting for transfers between devices, exchange(): return lax.all_to_all(array, axes, 0, 0, tiled=True)  62.5 us
    all_to_all x4, starting transfers between devices, exchange(): return lax.all_to_all(array, axes, 0, 0, tiled=True)  43 us
    ppermute x3, waiting for transfers between devices, on_device(): lax.ppermute(packed, 'x', [(x, (x + shift) % ring) for x in range(ring)])  16 us
    ppermute x3, starting transfers between devices, on_device(): lax.ppermute(packed, 'x', [(x, (x + shift) % ring) for x in range(ring)])  9.33 us
    ppermute x1, waiting for transfers between devices, on_device(): amps_far = lax.ppermute(amps, 'yh', PAIR)  7.45 us
    pallas_call x1, Pallas kernels, ladder_partials(): pl.pallas_call(ladder_kernel, out_shape=jax.ShapeDtypeStruct((con_count,...  4.89 us
    ppermute x1, starting transfers between devices, on_device(): opposite = lax.ppermute(own, 'yh', PAIR)  4.52 us
  transfers between devices with their start and end apart: 10, of which 7 were waited for; matrix products, arithmetic and copies ran while one was open for 2% of the time, Pallas kernels for 0%

profile of v1, /device:TPU:1, one launch (start us, length us, event | category | flops | bytes accessed | tf_op | source)
XLA Modules:
  0.0 161.7 jit_solution(15078797542734576242)
XLA Ops:
  0.0 17.2 %all-to-all-start = ((bf16[32,8,640]{2,1,0:T(8,128)(2,1)}), bf16[32,8,640]{2,1,0:T(8,128)(2,1)S(1)}, u32[]{:S(2)}, u32[]{:S(2)}) async-start(bf16[32,8,640]{2,1,0:T(8,128)(2,1)} %bitcast.55), calls=%async_computation | async-start | bytes 655360 | tf_op jit(solution)/shard_map/scatter/all_to_all | solution.py:19
  17.2 1.1 copy.32
  18.3 0.8 fusion.2
  19.1 4.4 %collective-permute-start.2 = (bf16[17,16,640]{2,1,0:T(8,128)(2,1)S(1)}, bf16[17,16,640]{2,1,0:T(8,128)(2,1)S(1)}, u32[]{:S(2)}, u32[]{:S(2)}) collective-permute-start(bf16[17,16,640]{2,1,0:T(8,128)(2,1)S(1)} %get-tuple-element.12), channel_id=1, source_target_pairs={{0,6},{2,0},{4,2},{6,4},{1,7},{3,1},{5,3},{7,5},{8,14},{10,8},{12,... | collective-permute-start | bytes 1044488 | tf_op jit(solution)/shard_map/ring/ppermute | solution.py:116
  23.5 2.4 %collective-permute-start.1 = (bf16[17,16,640]{2,1,0:T(8,128)(2,1)S(1)}, bf16[17,16,640]{2,1,0:T(8,128)(2,1)S(1)}, u32[]{:S(2)}, u32[]{:S(2)}) collective-permute-start(bf16[17,16,640]{2,1,0:T(8,128)(2,1)S(1)} %get-tuple-element.12), channel_id=1, source_target_pairs={{0,4},{2,6},{4,0},{6,2},{1,5},{3,7},{5,1},{7,3},{8,12},{10,14},{12... | collective-permute-start | bytes 1044488 | tf_op jit(solution)/shard_map/ring/ppermute | solution.py:116
  25.9 2.5 %collective-permute-start = (bf16[17,16,640]{2,1,0:T(8,128)(2,1)S(1)}, bf16[17,16,640]{2,1,0:T(8,128)(2,1)S(1)}, u32[]{:S(2)}, u32[]{:S(2)}) collective-permute-start(bf16[17,16,640]{2,1,0:T(8,128)(2,1)S(1)} %get-tuple-element.12), channel_id=1, source_target_pairs={{0,2},{2,4},{4,6},{6,0},{1,3},{3,5},{5,7},{7,1},{8,10},{10,12},{12... | collective-permute-start | bytes 1044488 | tf_op jit(solution)/shard_map/ring/ppermute | solution.py:116
  28.4 2.4 %collective-permute-done.2 = bf16[17,16,640]{2,1,0:T(8,128)(2,1)S(1)} collective-permute-done((bf16[17,16,640]{2,1,0:T(8,128)(2,1)S(1)}, bf16[17,16,640]{2,1,0:T(8,128)(2,1)S(1)}, u32[]{:S(2)}, u32[]{:S(2)}) %collective-permute-start.2) | collective-permute-done | bytes 348192 | tf_op jit(solution)/shard_map/ring/ppermute | solution.py:116
  30.8 4.6 %collective-permute-done.1 = bf16[17,16,640]{2,1,0:T(8,128)(2,1)S(1)} collective-permute-done((bf16[17,16,640]{2,1,0:T(8,128)(2,1)S(1)}, bf16[17,16,640]{2,1,0:T(8,128)(2,1)S(1)}, u32[]{:S(2)}, u32[]{:S(2)}) %collective-permute-start.1) | collective-permute-done | bytes 348192 | tf_op jit(solution)/shard_map/ring/ppermute | solution.py:116
  35.4 9.0 %collective-permute-done = bf16[17,16,640]{2,1,0:T(8,128)(2,1)S(1)} collective-permute-done((bf16[17,16,640]{2,1,0:T(8,128)(2,1)S(1)}, bf16[17,16,640]{2,1,0:T(8,128)(2,1)S(1)}, u32[]{:S(2)}, u32[]{:S(2)}) %collective-permute-start) | collective-permute-done | bytes 348192 | tf_op jit(solution)/shard_map/ring/ppermute | solution.py:116
  44.4 0.2 pad_maximum_fusion.near_ref
  44.6 2.4 %collective-permute-start.3 = (bf16[17,4,16,640]{3,2,1,0:T(8,128)(2,1)S(1)}, bf16[17,4,16,640]{3,2,1,0:T(8,128)(2,1)S(1)}, u32[]{:S(2)}, u32[]{:S(2)}) collective-permute-start(bf16[17,4,16,640]{3,2,1,0:T(8,128)(2,1)S(1)} %pad_maximum_fusion.near_ref), channel_id=1, source_target_pairs={{0,1},{1,0},{2,3},{3,2},{4,5},{5,4},{6,7},{7,6},{8,9},{9,8},{10,11... | collective-permute-start | bytes 4177928 | tf_op jit(solution)/shard_map/cores/ppermute | solution.py:127
  47.0 0.7 broadcast_in_dim.28
  47.8 12.5 %all-to-all-start.1 = ((bf16[32,8,640]{2,1,0:T(8,128)(2,1)}), bf16[32,8,640]{2,1,0:T(8,128)(2,1)S(1)}, u32[]{:S(2)}, u32[]{:S(2)}) async-start(bf16[32,8,640]{2,1,0:T(8,128)(2,1)} %broadcast_in_dim.28), calls=%async_computation.1 | async-start | bytes 655360 | tf_op jit(solution)/shard_map/spread/all_to_all | solution.py:19
  60.3 23.7 %all-to-all-done.1 = bf16[32,8,640]{2,1,0:T(8,128)(2,1)S(1)} async-done(((bf16[32,8,640]{2,1,0:T(8,128)(2,1)}), bf16[32,8,640]{2,1,0:T(8,128)(2,1)S(1)}, u32[]{:S(2)}, u32[]{:S(2)}) %all-to-all-start.1) | async-done | bytes 327712 | tf_op jit(solution)/shard_map/spread/all_to_all | solution.py:19
  84.0 4.5 %collective-permute-start.5 = (bf16[256,640]{1,0:T(8,128)(2,1)S(1)}, bf16[256,640]{1,0:T(8,128)(2,1)}, u32[]{:S(2)}, u32[]{:S(2)}) collective-permute-start(bf16[256,640]{1,0:T(8,128)(2,1)S(1)} %bitcast.52), channel_id=1, source_target_pairs={{0,8},{8,0},{1,9},{9,1},{2,10},{10,2},{3,11},{11,3},{4,12},{12,4},... | collective-permute-start | bytes 983048 | tf_op jit(solution)/shard_map/window/ppermute | solution.py:132
  88.6 2.3 %collective-permute-start.4 = (bf16[8,16,640]{2,1,0:T(8,128)(2,1)S(1)}, bf16[8,16,640]{2,1,0:T(8,128)(2,1)S(1)}, u32[]{:S(2)}, u32[]{:S(2)}) collective-permute-start(bf16[8,16,640]{2,1,0:T(8,128)(2,1)S(1)} %pad_maximum_fusion.1.amps_ref), channel_id=1, source_target_pairs={{0,8},{8,0},{1,9},{9,1},{2,10},{10,2},{3,11},{11,3},{4,12},{12,4},... | collective-permute-start | bytes 491528 | tf_op jit(solution)/shard_map/amps/ppermute | solution.py:130
  91.0 7.4 %collective-permute-done.4.amps_far_ref = bf16[8,16,640]{2,1,0:T(8,128)(2,1)S(1)} collective-permute-done((bf16[8,16,640]{2,1,0:T(8,128)(2,1)S(1)}, bf16[8,16,640]{2,1,0:T(8,128)(2,1)S(1)}, u32[]{:S(2)}, u32[]{:S(2)}) %collective-permute-start.4) | collective-permute-done | bytes 163872 | tf_op jit(solution)/shard_map/amps/ppermute | solution.py:130
  98.4 4.9 %shard_map.46 = f32[32,4,1024]{2,1,0:T(4,128)} custom-call(s32[3]{0:T(128)S(1)} %pad_add_fusion.place_ref, bf16[17,4,16,640]{3,2,1,0:T(8,128)(2,1)S(1)} %pad_maximum_fusion.near_ref, bf16[17,4,16,640]{3,2,1,0:T(8,128)(2,1)S(1)} %collective-permute-done.3.far_ref, bf16[8,16,640]{2,1,0:T(8,128)(2,1)S(1)} %pad_maximum_fusion.1.amps_ref, ...), custom_call_target="tpu_custom_call" | custom-call | flops 1426063360 | bytes 2785280 | tf_op jit(solution)/shard_map/pallas_call | solution.py:83
  103.3 5.5 %all-to-all-start.2 = ((f32[32,4,1024]{2,1,0:T(4,128)}), f32[32,4,1024]{2,1,0:T(4,128)S(1)}, u32[]{:S(2)}, u32[]{:S(2)}) async-start(f32[32,4,1024]{2,1,0:T(4,128)} %shard_map.46), calls=%async_computation.2 | async-start | bytes 1048576 | tf_op jit(solution)/shard_map/all_to_all | solution.py:19
  109.1 30.2 %all-to-all-done.2 = f32[32,4,1024]{2,1,0:T(4,128)S(1)} async-done(((f32[32,4,1024]{2,1,0:T(4,128)}), f32[32,4,1024]{2,1,0:T(4,128)S(1)}, u32[]{:S(2)}, u32[]{:S(2)}) %all-to-all-start.2) | async-done | bytes 524320 | tf_op jit(solution)/shard_map/all_to_all | solution.py:19
  139.4 0.4 reshape.130
  139.9 0.9 copy.21
  140.7 0.2 copy.22
  140.9 0.8 broadcast_in_dim.30
  141.7 7.9 %all-to-all-start.3 = ((f32[16,8,4,128]{3,2,1,0:T(4,128)}), f32[16,8,4,128]{3,2,1,0:T(4,128)S(1)}, u32[]{:S(2)}, u32[]{:S(2)}) async-start(f32[16,8,4,128]{3,2,1,0:T(4,128)} %broadcast_in_dim.30), calls=%async_computation.3 | async-start | bytes 524288 | tf_op jit(solution)/shard_map/all_to_all | solution.py:19
  149.7 8.5 %all-to-all-done.3 = f32[16,8,4,128]{3,2,1,0:T(4,128)S(1)} async-done(((f32[16,8,4,128]{3,2,1,0:T(4,128)}), f32[16,8,4,128]{3,2,1,0:T(4,128)S(1)}, u32[]{:S(2)}, u32[]{:S(2)}) %all-to-all-start.3) | async-done | bytes 262176 | tf_op jit(solution)/shard_map/all_to_all | solution.py:19
  158.2 0.6 gather_fusion
  159.1 0.4 reshape.133
  159.5 0.6 gather_fusion.1
  160.1 0.2 reshape.163
  160.3 0.6 gather_fusion.2
  161.0 0.6 copy_add_fusion
  (29 shorter events, 1.2 us)
Async XLA Ops:
  0.0 108.8 %copy-start = (s32[64,2]{0,1:T(2,128)S(1)}, s32[64,2]{0,1:T(2,128)}, u32[]{:S(2)}) copy-start(s32[64,2]{0,1:T(2,128)} %param.7) | copy-start | bytes 1540
  0.0 47.0 %all-to-all-start = ((bf16[32,8,640]{2,1,0:T(8,128)(2,1)}), bf16[32,8,640]{2,1,0:T(8,128)(2,1)S(1)}, u32[]{:S(2)}, u32[]{:S(2)}) async-start(bf16[32,8,640]{2,1,0:T(8,128)(2,1)} %bitcast.55), calls=%async_computation | async-start | bytes 655360 | tf_op jit(solution)/shard_map/scatter/all_to_all | solution.py:19
  19.1 11.7 %collective-permute-start.2 = (bf16[17,16,640]{2,1,0:T(8,128)(2,1)S(1)}, bf16[17,16,640]{2,1,0:T(8,128)(2,1)S(1)}, u32[]{:S(2)}, u32[]{:S(2)}) collective-permute-start(bf16[17,16,640]{2,1,0:T(8,128)(2,1)S(1)} %get-tuple-element.12), channel_id=1, source_target_pairs={{0,6},{2,0},{4,2},{6,4},{1,7},{3,1},{5,3},{7,5},{8,14},{10,8},{12,... | collective-permute-start | bytes 1044488 | tf_op jit(solution)/shard_map/ring/ppermute | solution.py:116
  23.5 11.9 %collective-permute-start.1 = (bf16[17,16,640]{2,1,0:T(8,128)(2,1)S(1)}, bf16[17,16,640]{2,1,0:T(8,128)(2,1)S(1)}, u32[]{:S(2)}, u32[]{:S(2)}) collective-permute-start(bf16[17,16,640]{2,1,0:T(8,128)(2,1)S(1)} %get-tuple-element.12), channel_id=1, source_target_pairs={{0,4},{2,6},{4,0},{6,2},{1,5},{3,7},{5,1},{7,3},{8,12},{10,14},{12... | collective-permute-start | bytes 1044488 | tf_op jit(solution)/shard_map/ring/ppermute | solution.py:116
  25.9 18.5 %collective-permute-start = (bf16[17,16,640]{2,1,0:T(8,128)(2,1)S(1)}, bf16[17,16,640]{2,1,0:T(8,128)(2,1)S(1)}, u32[]{:S(2)}, u32[]{:S(2)}) collective-permute-start(bf16[17,16,640]{2,1,0:T(8,128)(2,1)S(1)} %get-tuple-element.12), channel_id=1, source_target_pairs={{0,2},{2,4},{4,6},{6,0},{1,3},{3,5},{5,7},{7,1},{8,10},{10,12},{12... | collective-permute-start | bytes 1044488 | tf_op jit(solution)/shard_map/ring/ppermute | solution.py:116
  44.6 44.0 %collective-permute-start.3 = (bf16[17,4,16,640]{3,2,1,0:T(8,128)(2,1)S(1)}, bf16[17,4,16,640]{3,2,1,0:T(8,128)(2,1)S(1)}, u32[]{:S(2)}, u32[]{:S(2)}) collective-permute-start(bf16[17,4,16,640]{3,2,1,0:T(8,128)(2,1)S(1)} %pad_maximum_fusion.near_ref), channel_id=1, source_target_pairs={{0,1},{1,0},{2,3},{3,2},{4,5},{5,4},{6,7},{7,6},{8,9},{9,8},{10,11... | collective-permute-start | bytes 4177928 | tf_op jit(solution)/shard_map/cores/ppermute | solution.py:127
  47.8 36.2 %all-to-all-start.1 = ((bf16[32,8,640]{2,1,0:T(8,128)(2,1)}), bf16[32,8,640]{2,1,0:T(8,128)(2,1)S(1)}, u32[]{:S(2)}, u32[]{:S(2)}) async-start(bf16[32,8,640]{2,1,0:T(8,128)(2,1)} %broadcast_in_dim.28), calls=%async_computation.1 | async-start | bytes 655360 | tf_op jit(solution)/shard_map/spread/all_to_all | solution.py:19
  84.0 14.4 %collective-permute-start.5 = (bf16[256,640]{1,0:T(8,128)(2,1)S(1)}, bf16[256,640]{1,0:T(8,128)(2,1)}, u32[]{:S(2)}, u32[]{:S(2)}) collective-permute-start(bf16[256,640]{1,0:T(8,128)(2,1)S(1)} %bitcast.52), channel_id=1, source_target_pairs={{0,8},{8,0},{1,9},{9,1},{2,10},{10,2},{3,11},{11,3},{4,12},{12,4},... | collective-permute-start | bytes 983048 | tf_op jit(solution)/shard_map/window/ppermute | solution.py:132
  88.6 9.8 %collective-permute-start.4 = (bf16[8,16,640]{2,1,0:T(8,128)(2,1)S(1)}, bf16[8,16,640]{2,1,0:T(8,128)(2,1)S(1)}, u32[]{:S(2)}, u32[]{:S(2)}) collective-permute-start(bf16[8,16,640]{2,1,0:T(8,128)(2,1)S(1)} %pad_maximum_fusion.1.amps_ref), channel_id=1, source_target_pairs={{0,8},{8,0},{1,9},{9,1},{2,10},{10,2},{3,11},{11,3},{4,12},{12,4},... | collective-permute-start | bytes 491528 | tf_op jit(solution)/shard_map/amps/ppermute | solution.py:130
  103.3 36.0 %all-to-all-start.2 = ((f32[32,4,1024]{2,1,0:T(4,128)}), f32[32,4,1024]{2,1,0:T(4,128)S(1)}, u32[]{:S(2)}, u32[]{:S(2)}) async-start(f32[32,4,1024]{2,1,0:T(4,128)} %shard_map.46), calls=%async_computation.2 | async-start | bytes 1048576 | tf_op jit(solution)/shard_map/all_to_all | solution.py:19
  109.1 40.4 %copy-start.1 = (s32[128]{0:T(128)S(1)}, s32[128]{0:T(128)}, u32[]{:S(2)}) copy-start(s32[128]{0:T(128)} %param.8) | copy-start | bytes 1540
  141.7 16.6 %all-to-all-start.3 = ((f32[16,8,4,128]{3,2,1,0:T(4,128)}), f32[16,8,4,128]{3,2,1,0:T(4,128)S(1)}, u32[]{:S(2)}, u32[]{:S(2)}) async-start(f32[16,8,4,128]{3,2,1,0:T(4,128)} %broadcast_in_dim.30), calls=%async_computation.3 | async-start | bytes 524288 | tf_op jit(solution)/shard_map/all_to_all | solution.py:19

commit v2 on v1

v2 whole, which is shorter than its diff:
```python
import jax
import jax.numpy as jnp
from jax import lax
from jax.experimental import pallas as pl
from jax.experimental.pallas import tpu as pltpu
from jax.sharding import Mesh
from jax.sharding import PartitionSpec as P

TS = 16
LANES = 128
CONTRACT = ("z", "yl")
OUT = ("yh", "x", "core")
PAIR = [(0, 1), (1, 0)]


def exchange(array, axes):
    return lax.all_to_all(array, axes, 0, 0, tiled=True)


def sent_to_all(array, axes):
    count = lax.axis_size(axes)
    return exchange(jnp.broadcast_to(array[None], (count, *array.shape)), axes)


def ladder_kernel(
    place_ref, near_ref, far_ref, amps_ref, amps_far_ref, right_ref, out_ref, stack_ref
):
    core, yh = place_ref[0], place_ref[1]
    b_count, depth, _ = stack_ref.shape
    ring, pair_rows = near_ref.shape[0], amps_ref.shape[1]
    c_pairs = near_ref.shape[1] // pair_rows - 1
    a_dev = pair_rows // 2
    d_count = right_ref.shape[0] // b_count
    right = right_ref[...]
    for n in range(0, c_pairs, 2):
        left = jnp.concatenate(
            [
                ref[x, m * pair_rows : (m + 1) * pair_rows, :]
                for m in (n, n + 1)
                for ref in (near_ref, far_ref)
                for x in range(ring)
            ],
            axis=0,
        )
        part = lax.dot_general(
            right, left, (((1,), (1,)), ((), ())), preferred_element_type=jnp.float32
        ).astype(jnp.bfloat16)
        part = part.reshape(b_count, d_count, 2 * LANES)
        for h in range(2):
            rows = (n + h) * d_count
            stack_ref[:, rows : rows + d_count, :] = part[:, :, h * LANES : (h + 1) * LANES]
    amps = jnp.concatenate(
        [amps_ref[q, :, :depth] for q in range(amps_ref.shape[0])]
        + [amps_far_ref[q, :, :depth] for q in range(amps_far_ref.shape[0])],
        axis=0,
    )
    blocks = amps.shape[0] // pair_rows
    odd = lax.rem(lax.broadcasted_iota(jnp.int32, (1, 1, LANES), 2) // a_dev, 2) == 1
    for q in range(b_count // 2):
        sums = []
        for b, step in ((2 * q, LANES - a_dev), (2 * q + 1, a_dev)):
            full = jnp.dot(amps, stack_ref[b], preferred_element_type=jnp.float32)
            full = full.reshape(blocks, 2, a_dev, LANES)
            mixed = jnp.where(odd, full[:, 1], full[:, 0]).reshape(blocks * a_dev, LANES)
            sums.append(mixed + pltpu.roll(mixed, step, 1))
        found = jnp.where(odd[0], sums[1], sums[0])
        found = pltpu.roll(found, core * (LANES // 2), 1)
        found = found.astype(out_ref.dtype)
        for block in range(blocks):
            other_yh, other_core, x = block // (2 * ring), block // ring % 2, block % ring
            place = (lax.rem(yh + other_yh, 2) * ring + x) * 2 + lax.rem(core + other_core, 2)
            for h in range(2):
                rows = found[block * a_dev + h * (a_dev // 2) : block * a_dev + (h + 1) * (a_dev // 2)]
                out_ref[2 * place + h, :, q * LANES : (q + 1) * LANES] = rows


def ladder_partials(place, near, far, amps, amps_far, right, i_count, con_count):
    b_count = amps.shape[1]
    depth = (near.shape[1] // b_count - 1) * (right.shape[0] // b_count)
    pairs = 2 * near.size * right.shape[0]
    return pl.pallas_call(
        ladder_kernel,
        out_shape=jax.ShapeDtypeStruct(
            (con_count, i_count // con_count, b_count * LANES // 2), jnp.bfloat16
        ),
        in_specs=[pl.BlockSpec(memory_space=pltpu.SMEM)]
        + [pl.BlockSpec(memory_space=pltpu.VMEM)] * 5,
        out_specs=pl.BlockSpec(memory_space=pltpu.VMEM),
        scratch_shapes=[pltpu.VMEM((b_count, depth, LANES), jnp.bfloat16)],
        compiler_params=pltpu.CompilerParams(vmem_limit_bytes=12 * 1024 * 1024),
        cost_estimate=pl.CostEstimate(
            flops=2 * pairs, bytes_accessed=4 * near.size, transcendentals=0
        ),
    )(place, near, far, amps, amps_far, right)


def on_device(chol, amplitudes, tile_pairs, partner, pair_swap):
    out_count = lax.axis_size(OUT)
    con_count = lax.axis_size(CONTRACT)
    ring = lax.axis_size("x")
    a_dev, c_dev, p_size = chol.shape
    i_dev = amplitudes.shape[0]
    i_count = i_dev * out_count
    half = c_dev // 2
    pair_rows = 2 * a_dev

    rows = jnp.transpose(chol.reshape(a_dev, 2, half, p_size), (2, 1, 0, 3))
    extra = jnp.transpose(amplitudes.reshape(i_dev, 2, -1), (1, 0, 2)).reshape(1, pair_rows, -1)
    extra = jnp.pad(extra, ((0, 0), (0, 0), (0, p_size - extra.shape[2])))
    packed = jnp.concatenate([rows.reshape(half, pair_rows, p_size), extra], axis=0)
    near = sent_to_all(packed.reshape(-1, p_size), "x")

    z, yl = lax.axis_index("z"), lax.axis_index("yl")
    depth_z = lax.axis_size("z")
    window = chol.reshape(2, -1, p_size)
    piece = jnp.where(yl == 0, window[0], lax.ppermute(window[1], CONTRACT, [(0, 1)]))
    got = sum(lax.ppermute(piece, "z", [(0, to)]) for to in (8, 12, 4))
    piece = jnp.where(z == 0, piece, got)
    got = sum(
        lax.ppermute(
            piece, "z", [(at, (at + step) % depth_z) for at in range(0, depth_z, 4)]
        )
        for step in (2, 1, -1)
    )
    piece = jnp.where(z % 4 == 0, piece, got)
    right = sent_to_all(piece, ("yh", "yl")).reshape(-1, p_size)

    far = lax.ppermute(near, "core", PAIR)
    amps = jnp.concatenate([near[:, -pair_rows:], far[:, -pair_rows:]], axis=0)
    amps_far = lax.ppermute(amps, "yh", PAIR)

    place = jnp.stack([lax.axis_index("core"), lax.axis_index("yh")])
    partial = ladder_partials(place, near, far, amps, amps_far, right, i_count, con_count)
    ladder = jnp.sum(exchange(partial, CONTRACT).astype(jnp.float32), axis=0)

    occ_dev = i_count // con_count
    ladder = ladder.reshape(occ_dev, 2, a_dev // 2, 2, ring, 2, a_dev)
    ladder = jnp.transpose(ladder, (4, 1, 0, 3, 6, 2, 5)).reshape(2 * ring, occ_dev, TS * a_dev)
    every = sent_to_all(ladder, OUT).reshape(-1, occ_dev, TS * a_dev)

    slot_count = tile_pairs.shape[0] // out_count
    first = lax.axis_index(OUT) * slot_count
    pairs = lax.dynamic_slice_in_dim(tile_pairs, first, slot_count, 0)

    def whole_tiles(a_tile, b_tile):
        holder = (a_tile // ring * ring + b_tile % ring) * 2
        inner = a_tile % ring * 2 + b_tile // ring
        spots = (holder[:, None] + jnp.arange(2)) * (2 * ring) + inner[:, None]
        found = jnp.take(every, spots.reshape(-1), axis=0, mode="clip")
        return found.reshape(slot_count, 2, occ_dev, TS, a_dev)

    own_swap = lax.dynamic_slice_in_dim(
        pair_swap, lax.axis_index(CONTRACT) * occ_dev, occ_dev, 0
    ) - lax.axis_index(CONTRACT) * occ_dev
    straight = jnp.transpose(whole_tiles(pairs[:, 0], pairs[:, 1]), (0, 2, 3, 1, 4))
    mirror = whole_tiles(pairs[:, 1], pairs[:, 0])
    mirror = jnp.take(mirror, own_swap, axis=2, mode="clip")
    mirror = jnp.transpose(mirror, (0, 2, 1, 4, 3))
    residual = straight.reshape(slot_count, occ_dev, TS, TS) + mirror.reshape(
        slot_count, occ_dev, TS, TS
    )
    return residual.reshape(slot_count, occ_dev, TS * TS)


def solution(mesh):
    torus = Mesh(mesh.devices.reshape(16, 2, 2, 4, 2), ("z", "yl", "yh", "x", "core"))
    in_specs = (P(OUT, CONTRACT, None), P(OUT, CONTRACT), P(), P(), P())
    out_specs = P(OUT, CONTRACT, None)

    return jax.shard_map(
        on_device, mesh=torus, in_specs=in_specs, out_specs=out_specs, check_vma=False
    )
```

time: 162 us -> 136 us (0.84)
  waiting for transfers between devices: 85.9 us -> 50.5 us
  starting transfers between devices: 61.5 us -> 66.8 us
  local copies, waits for them, and re-layouts: 7.11 us -> 10.9 us
    all_to_all x4, waiting for transfers between devices: 62.5 us -> 39.1 us  [exchange(): return lax.all_to_all(array, axes, 0, 0, tiled=True)]
    all_to_all x4, starting transfers between devices: 43 us -> 27.5 us  [exchange(): return lax.all_to_all(array, axes, 0, 0, tiled=True)]
    ppermute x4 -> x7, starting transfers between devices: 13.8 us -> 25.8 us  [the longest x3 18.7 us: on_device(): got = sum((lax.ppermute(piece, 'z', [(0, to)]) for to in (8, 12, 4)))]
    ppermute x4 -> x7, waiting for transfers between devices: 16 us -> 7.59 us  [the longest x3 3.82 us: on_device(): lax.ppermute(piece, 'z', [(at, (at + step) % depth_z) for at in range(0,...]
    ppermute x1, starting transfers between devices: 2.4 us -> 8.58 us  [on_device(): far = lax.ppermute(near, 'core', PAIR)]
    ppermute x1, waiting for transfers between devices: 7.45 us -> 3.81 us  [on_device(): amps_far = lax.ppermute(amps, 'yh', PAIR)]
    ppermute x1, starting transfers between devices: 2.26 us -> 4.88 us  [on_device(): amps_far = lax.ppermute(amps, 'yh', PAIR)]
    unnamed x4 -> x10, local copies, waits for them, and re-layouts: 0.01 us -> 2.45 us
  transfers between devices with their start and end apart: 10 -> 13, of which waited for: 7 -> 10; matrix products, arithmetic and copies ran while one was open for 2% -> 2% of each run, Pallas kernels for 0% -> 0%
where the time goes in v2:
time: 136 us
  starting transfers between devices  66.8 us (49%)
  waiting for transfers between devices  50.5 us (37%)
  local copies, waits for them, and re-layouts  10.9 us (8%)
  Pallas kernels  4.33 us (3%)
  other arithmetic  2.86 us (2%)
    all_to_all x4, waiting for transfers between devices, exchange(): return lax.all_to_all(array, axes, 0, 0, tiled=True)  39.1 us
    all_to_all x4, starting transfers between devices, exchange(): return lax.all_to_all(array, axes, 0, 0, tiled=True)  27.5 us
    ppermute x3, starting transfers between devices, on_device(): got = sum((lax.ppermute(piece, 'z', [(0, to)]) for to in (8, 12, 4)))  18.7 us
    ppermute x1, starting transfers between devices, on_device(): far = lax.ppermute(near, 'core', PAIR)  8.58 us
    ppermute x1, starting transfers between devices, on_device(): amps_far = lax.ppermute(amps, 'yh', PAIR)  4.88 us
    pallas_call x1, Pallas kernels, ladder_partials(): pl.pallas_call(ladder_kernel, out_shape=jax.ShapeDtypeStruct((con_count,...  4.33 us
    ppermute x3, starting transfers between devices, on_device(): lax.ppermute(piece, 'z', [(at, (at + step) % depth_z) for at in range(0,...  3.9 us
    ppermute x3, waiting for transfers between devices, on_device(): lax.ppermute(piece, 'z', [(at, (at + step) % depth_z) for at in range(0,...  3.82 us
  transfers between devices with their start and end apart: 13, of which 10 were waited for; matrix products, arithmetic and copies ran while one was open for 2% of the time, Pallas kernels for 0%

profile of v2, /device:TPU:1, one launch (start us, length us, event | category | flops | bytes accessed | tf_op | source)
XLA Modules:
  0.0 135.6 jit_solution(15255581239852663225)
XLA Ops:
  0.0 1.1 copy.21
  1.1 0.8 fusion.1
  1.9 1.2 broadcast_in_dim.17
  3.1 5.0 %all-to-all-start = ((bf16[4,272,640]{2,1,0:T(8,128)(2,1)}), bf16[4,272,640]{2,1,0:T(8,128)(2,1)S(1)}, u32[]{:S(2)}, u32[]{:S(2)}) async-start(bf16[4,272,640]{2,1,0:T(8,128)(2,1)} %broadcast_in_dim.17), calls=%async_computation | async-start | bytes 2785280 | tf_op jit(solution)/shard_map/all_to_all | solution.py:17
  8.1 3.2 %collective-permute-start.2 = (bf16[128,640]{1,0:T(8,128)(2,1)S(1)}, bf16[128,640]{1,0:T(8,128)(2,1)S(1)}, u32[]{:S(2)}, u32[]{:S(2)}) collective-permute-start(bf16[128,640]{1,0:T(8,128)(2,1)S(1)} %bitcast.47), channel_id=1, source_target_pairs={{0,16},{1,17},{2,18},{3,19},{4,20},{5,21},{6,22},{7,23},{8,24},{9,... | collective-permute-start | bytes 491528 | tf_op jit(solution)/shard_map/ppermute | solution.py:116
  11.3 9.8 %all-to-all-done.near_ref = bf16[4,272,640]{2,1,0:T(8,128)(2,1)S(1)} async-done(((bf16[4,272,640]{2,1,0:T(8,128)(2,1)}), bf16[4,272,640]{2,1,0:T(8,128)(2,1)S(1)}, u32[]{:S(2)}, u32[]{:S(2)}) %all-to-all-start) | async-done | bytes 1392672 | tf_op jit(solution)/shard_map/all_to_all | solution.py:17
  21.1 8.6 %collective-permute-start = (bf16[4,272,640]{2,1,0:T(8,128)(2,1)S(1)}, bf16[4,272,640]{2,1,0:T(8,128)(2,1)S(1)}, u32[]{:S(2)}, u32[]{:S(2)}) collective-permute-start(bf16[4,272,640]{2,1,0:T(8,128)(2,1)S(1)} %all-to-all-done.near_ref), channel_id=1, source_target_pairs={{0,1},{1,0},{2,3},{3,2},{4,5},{5,4},{6,7},{7,6},{8,9},{9,8},{10,11... | collective-permute-start | bytes 4177928 | tf_op jit(solution)/shard_map/ppermute | solution.py:128
  29.7 15.4 %collective-permute-start.3 = (bf16[128,640]{1,0:T(8,128)(2,1)S(1)}, bf16[128,640]{1,0:T(8,128)(2,1)S(1)}, u32[]{:S(2)}, u32[]{:S(2)}) collective-permute-start(bf16[128,640]{1,0:T(8,128)(2,1)S(1)} %bitcast_select_fusion), channel_id=1, source_target_pairs={{0,256},{1,257},{2,258},{3,259},{4,260},{5,261},{6,262},{7,263},{8... | collective-permute-start | bytes 491528 | tf_op jit(solution)/shard_map/ppermute | solution.py:117
  45.2 1.3 collective-permute-start.4
  46.5 1.9 %collective-permute-start.5 = (bf16[128,640]{1,0:T(8,128)(2,1)S(1)}, bf16[128,640]{1,0:T(8,128)(2,1)}, u32[]{:S(2)}, u32[]{:S(2)}) collective-permute-start(bf16[128,640]{1,0:T(8,128)(2,1)S(1)} %bitcast_select_fusion), channel_id=1, source_target_pairs={{0,128},{1,129},{2,130},{3,131},{4,132},{5,133},{6,134},{7,135},{8... | collective-permute-start | bytes 491528 | tf_op jit(solution)/shard_map/ppermute | solution.py:117
  48.7 1.3 collective-permute-done.4
  50.0 2.2 %collective-permute-done.5 = bf16[128,640]{1,0:T(8,128)(2,1)} collective-permute-done((bf16[128,640]{1,0:T(8,128)(2,1)S(1)}, bf16[128,640]{1,0:T(8,128)(2,1)}, u32[]{:S(2)}, u32[]{:S(2)}) %collective-permute-start.5) | collective-permute-done | bytes 163872 | tf_op jit(solution)/shard_map/ppermute | solution.py:117
  52.2 1.0 add_select_fusion.1
  53.2 1.3 collective-permute-start.6
  54.5 1.3 collective-permute-start.7
  55.8 1.3 collective-permute-start.8
  57.4 3.5 %collective-permute-done.7 = bf16[128,640]{1,0:T(8,128)(2,1)S(1)} collective-permute-done((bf16[128,640]{1,0:T(8,128)(2,1)S(1)}, bf16[128,640]{1,0:T(8,128)(2,1)S(1)}, u32[]{:S(2)}, u32[]{:S(2)}) %collective-permute-start.7) | collective-permute-done | bytes 163872 | tf_op jit(solution)/shard_map/ppermute | solution.py:120
  61.0 0.9 broadcast_in_dim.18
  61.9 4.2 %all-to-all-start.1 = ((bf16[4,128,640]{2,1,0:T(8,128)(2,1)}), bf16[4,128,640]{2,1,0:T(8,128)(2,1)S(1)}, u32[]{:S(2)}, u32[]{:S(2)}) async-start(bf16[4,128,640]{2,1,0:T(8,128)(2,1)} %broadcast_in_dim.18), calls=%async_computation.1 | async-start | bytes 1310720 | tf_op jit(solution)/shard_map/all_to_all | solution.py:17
  66.1 1.1 copy-done.1
  67.2 4.9 %collective-permute-start.1 = (bf16[8,16,640]{2,1,0:T(8,128)(2,1)S(1)}, bf16[8,16,640]{2,1,0:T(8,128)(2,1)S(1)}, u32[]{:S(2)}, u32[]{:S(2)}) collective-permute-start(bf16[8,16,640]{2,1,0:T(8,128)(2,1)S(1)} %pad_maximum_fusion.amps_ref), channel_id=1, source_target_pairs={{0,8},{8,0},{1,9},{9,1},{2,10},{10,2},{3,11},{11,3},{4,12},{12,4},... | collective-permute-start | bytes 491528 | tf_op jit(solution)/shard_map/ppermute | solution.py:130
  72.2 2.8 %all-to-all-done.1 = bf16[4,128,640]{2,1,0:T(8,128)(2,1)S(1)} async-done(((bf16[4,128,640]{2,1,0:T(8,128)(2,1)}), bf16[4,128,640]{2,1,0:T(8,128)(2,1)S(1)}, u32[]{:S(2)}, u32[]{:S(2)}) %all-to-all-start.1) | async-done | bytes 655392 | tf_op jit(solution)/shard_map/all_to_all | solution.py:17
  75.0 3.8 %collective-permute-done.1.amps_far_ref = bf16[8,16,640]{2,1,0:T(8,128)(2,1)S(1)} collective-permute-done((bf16[8,16,640]{2,1,0:T(8,128)(2,1)S(1)}, bf16[8,16,640]{2,1,0:T(8,128)(2,1)S(1)}, u32[]{:S(2)}, u32[]{:S(2)}) %collective-permute-start.1) | collective-permute-done | bytes 163872 | tf_op jit(solution)/shard_map/ppermute | solution.py:130
  78.8 1.3 copy-done.2
  80.2 4.3 %shard_map.46 = bf16[32,4,1024]{2,1,0:T(4,128)(2,1)} custom-call(s32[2]{0:T(128)S(1)} %pad_add_fusion.place_ref, bf16[4,272,640]{2,1,0:T(8,128)(2,1)S(1)} %all-to-all-done.near_ref, bf16[4,272,640]{2,1,0:T(8,128)(2,1)S(1)} %copy-done.2, bf16[8,16,640]{2,1,0:T(8,128)(2,1)S(1)} %pad_maximum_fusion.amps_ref, ...), custom_call_target="tpu_custom_call" | custom-call | flops 1426063360 | bytes 2785280 | tf_op jit(solution)/shard_map/pallas_call | solution.py:81
  84.5 9.8 %all-to-all-start.2 = ((bf16[32,4,1024]{2,1,0:T(4,128)(2,1)}), bf16[32,4,1024]{2,1,0:T(4,128)(2,1)S(1)}, u32[]{:S(2)}, u32[]{:S(2)}) async-start(bf16[32,4,1024]{2,1,0:T(4,128)(2,1)} %shard_map.46), calls=%async_computation.2 | async-start | bytes 524288 | tf_op jit(solution)/shard_map/all_to_all | solution.py:17
  94.7 17.9 %all-to-all-done.2 = bf16[32,4,1024]{2,1,0:T(4,128)(2,1)S(1)} async-done(((bf16[32,4,1024]{2,1,0:T(4,128)(2,1)}), bf16[32,4,1024]{2,1,0:T(4,128)(2,1)S(1)}, u32[]{:S(2)}, u32[]{:S(2)}) %all-to-all-start.2) | async-done | bytes 262176 | tf_op jit(solution)/shard_map/all_to_all | solution.py:17
  113.1 0.9 copy.10
  114.2 0.8 broadcast_in_dim.37
  114.9 8.6 %all-to-all-start.3 = ((f32[16,8,4,128]{3,2,1,0:T(4,128)}), f32[16,8,4,128]{3,2,1,0:T(4,128)S(1)}, u32[]{:S(2)}, u32[]{:S(2)}) async-start(f32[16,8,4,128]{3,2,1,0:T(4,128)} %broadcast_in_dim.37), calls=%async_computation.3 | async-start | bytes 524288 | tf_op jit(solution)/shard_map/all_to_all | solution.py:17
  123.7 8.5 %all-to-all-done.3 = f32[16,8,4,128]{3,2,1,0:T(4,128)S(1)} async-done(((f32[16,8,4,128]{3,2,1,0:T(4,128)}), f32[16,8,4,128]{3,2,1,0:T(4,128)S(1)}, u32[]{:S(2)}, u32[]{:S(2)}) %all-to-all-start.3) | async-done | bytes 262176 | tf_op jit(solution)/shard_map/all_to_all | solution.py:17
  135.0 0.6 copy_add_fusion
  (44 shorter events, 4.8 us)
Async XLA Ops:
  0.0 94.3 %copy-start = (s32[64,2]{0,1:T(2,128)S(1)}, s32[64,2]{0,1:T(2,128)}, u32[]{:S(2)}) copy-start(s32[64,2]{0,1:T(2,128)} %param.7) | copy-start | bytes 1540
  3.1 5.0 %copy-start.3 = (bf16[8,32,640]{2,1,0:T(8,128)(2,1)S(1)}, bf16[8,32,640]{2,1,0:T(8,128)(2,1)}, u32[]{:S(2)}) copy-start(bf16[8,32,640]{2,1,0:T(8,128)(2,1)} %param.5) | copy-start | bytes 983044
  3.1 18.0 %all-to-all-start = ((bf16[4,272,640]{2,1,0:T(8,128)(2,1)}), bf16[4,272,640]{2,1,0:T(8,128)(2,1)S(1)}, u32[]{:S(2)}, u32[]{:S(2)}) async-start(bf16[4,272,640]{2,1,0:T(8,128)(2,1)} %broadcast_in_dim.17), calls=%async_computation | async-start | bytes 2785280 | tf_op jit(solution)/shard_map/all_to_all | solution.py:17
  8.1 21.6 %collective-permute-start.2 = (bf16[128,640]{1,0:T(8,128)(2,1)S(1)}, bf16[128,640]{1,0:T(8,128)(2,1)S(1)}, u32[]{:S(2)}, u32[]{:S(2)}) collective-permute-start(bf16[128,640]{1,0:T(8,128)(2,1)S(1)} %bitcast.47), channel_id=1, source_target_pairs={{0,16},{1,17},{2,18},{3,19},{4,20},{5,21},{6,22},{7,23},{8,24},{9,... | collective-permute-start | bytes 491528 | tf_op jit(solution)/shard_map/ppermute | solution.py:116
  21.1 45.0 %collective-permute-start = (bf16[4,272,640]{2,1,0:T(8,128)(2,1)S(1)}, bf16[4,272,640]{2,1,0:T(8,128)(2,1)S(1)}, u32[]{:S(2)}, u32[]{:S(2)}) collective-permute-start(bf16[4,272,640]{2,1,0:T(8,128)(2,1)S(1)} %all-to-all-done.near_ref), channel_id=1, source_target_pairs={{0,1},{1,0},{2,3},{3,2},{4,5},{5,4},{6,7},{7,6},{8,9},{9,8},{10,11... | collective-permute-start | bytes 4177928 | tf_op jit(solution)/shard_map/ppermute | solution.py:128
  29.7 19.0 %collective-permute-start.3 = (bf16[128,640]{1,0:T(8,128)(2,1)S(1)}, bf16[128,640]{1,0:T(8,128)(2,1)S(1)}, u32[]{:S(2)}, u32[]{:S(2)}) collective-permute-start(bf16[128,640]{1,0:T(8,128)(2,1)S(1)} %bitcast_select_fusion), channel_id=1, source_target_pairs={{0,256},{1,257},{2,258},{3,259},{4,260},{5,261},{6,262},{7,263},{8... | collective-permute-start | bytes 491528 | tf_op jit(solution)/shard_map/ppermute | solution.py:117
  45.2 4.8 %collective-permute-start.4 = (bf16[128,640]{1,0:T(8,128)(2,1)S(1)}, bf16[128,640]{1,0:T(8,128)(2,1)S(1)}, u32[]{:S(2)}, u32[]{:S(2)}) collective-permute-start(bf16[128,640]{1,0:T(8,128)(2,1)S(1)} %bitcast_select_fusion), channel_id=1, source_target_pairs={{0,384},{1,385},{2,386},{3,387},{4,388},{5,389},{6,390},{7,391},{8... | collective-permute-start | bytes 491528 | tf_op jit(solution)/shard_map/ppermute | solution.py:117
  46.5 5.7 %collective-permute-start.5 = (bf16[128,640]{1,0:T(8,128)(2,1)S(1)}, bf16[128,640]{1,0:T(8,128)(2,1)}, u32[]{:S(2)}, u32[]{:S(2)}) collective-permute-start(bf16[128,640]{1,0:T(8,128)(2,1)S(1)} %bitcast_select_fusion), channel_id=1, source_target_pairs={{0,128},{1,129},{2,130},{3,131},{4,132},{5,133},{6,134},{7,135},{8... | collective-permute-start | bytes 491528 | tf_op jit(solution)/shard_map/ppermute | solution.py:117
  53.2 4.2 %collective-permute-start.6 = (bf16[128,640]{1,0:T(8,128)(2,1)S(1)}, bf16[128,640]{1,0:T(8,128)(2,1)S(1)}, u32[]{:S(2)}, u32[]{:S(2)}) collective-permute-start(bf16[128,640]{1,0:T(8,128)(2,1)S(1)} %add_select_fusion.1), channel_id=1, source_target_pairs={{0,64},{128,192},{256,320},{384,448},{1,65},{129,193},{257,321},{3... | collective-permute-start | bytes 491528 | tf_op jit(solution)/shard_map/ppermute | solution.py:120
  54.5 6.4 %collective-permute-start.7 = (bf16[128,640]{1,0:T(8,128)(2,1)S(1)}, bf16[128,640]{1,0:T(8,128)(2,1)S(1)}, u32[]{:S(2)}, u32[]{:S(2)}) collective-permute-start(bf16[128,640]{1,0:T(8,128)(2,1)S(1)} %add_select_fusion.1), channel_id=1, source_target_pairs={{0,32},{128,160},{256,288},{384,416},{1,33},{129,161},{257,289},{3... | collective-permute-start | bytes 491528 | tf_op jit(solution)/shard_map/ppermute | solution.py:120
  55.8 5.1 %collective-permute-start.8 = (bf16[128,640]{1,0:T(8,128)(2,1)S(1)}, bf16[128,640]{1,0:T(8,128)(2,1)S(1)}, u32[]{:S(2)}, u32[]{:S(2)}) collective-permute-start(bf16[128,640]{1,0:T(8,128)(2,1)S(1)} %add_select_fusion.1), channel_id=1, source_target_pairs={{0,480},{128,96},{256,224},{384,352},{1,481},{129,97},{257,225},{3... | collective-permute-start | bytes 491528 | tf_op jit(solution)/shard_map/ppermute | solution.py:120
  61.9 13.1 %all-to-all-start.1 = ((bf16[4,128,640]{2,1,0:T(8,128)(2,1)}), bf16[4,128,640]{2,1,0:T(8,128)(2,1)S(1)}, u32[]{:S(2)}, u32[]{:S(2)}) async-start(bf16[4,128,640]{2,1,0:T(8,128)(2,1)} %broadcast_in_dim.18), calls=%async_computation.1 | async-start | bytes 1310720 | tf_op jit(solution)/shard_map/all_to_all | solution.py:17
  66.1 1.1 copy-start.1
  67.2 11.6 %collective-permute-start.1 = (bf16[8,16,640]{2,1,0:T(8,128)(2,1)S(1)}, bf16[8,16,640]{2,1,0:T(8,128)(2,1)S(1)}, u32[]{:S(2)}, u32[]{:S(2)}) collective-permute-start(bf16[8,16,640]{2,1,0:T(8,128)(2,1)S(1)} %pad_maximum_fusion.amps_ref), channel_id=1, source_target_pairs={{0,8},{8,0},{1,9},{9,1},{2,10},{10,2},{3,11},{11,3},{4,12},{12,4},... | collective-permute-start | bytes 491528 | tf_op jit(solution)/shard_map/ppermute | solution.py:130
  78.8 1.3 copy-start.2
  84.5 28.0 %all-to-all-start.2 = ((bf16[32,4,1024]{2,1,0:T(4,128)(2,1)}), bf16[32,4,1024]{2,1,0:T(4,128)(2,1)S(1)}, u32[]{:S(2)}, u32[]{:S(2)}) async-start(bf16[32,4,1024]{2,1,0:T(4,128)(2,1)} %shard_map.46), calls=%async_computation.2 | async-start | bytes 524288 | tf_op jit(solution)/shard_map/all_to_all | solution.py:17
  94.3 29.1 %copy-start.4 = (s32[128]{0:T(128)S(1)}, s32[128]{0:T(128)}, u32[]{:S(2)}) copy-start(s32[128]{0:T(128)} %param.8) | copy-start | bytes 1540
  114.9 17.3 %all-to-all-start.3 = ((f32[16,8,4,128]{3,2,1,0:T(4,128)}), f32[16,8,4,128]{3,2,1,0:T(4,128)S(1)}, u32[]{:S(2)}, u32[]{:S(2)}) async-start(f32[16,8,4,128]{3,2,1,0:T(4,128)} %broadcast_in_dim.37), calls=%async_computation.3 | async-start | bytes 524288 | tf_op jit(solution)/shard_map/all_to_all | solution.py:17

commit v3 on v2

v3 whole, which is shorter than its diff:
```python
import functools

import jax
import jax.numpy as jnp
from jax import lax
from jax.experimental import pallas as pl
from jax.experimental.pallas import tpu as pltpu
from jax.sharding import Mesh
from jax.sharding import PartitionSpec as P

TS = 16
LANES = 128
CONTRACT = ("z", "yl")
OUT = ("yh", "x", "core")
PAIR = [(0, 1), (1, 0)]


def exchange(array, axes):
    return lax.all_to_all(array, axes, 0, 0, tiled=True)


def sent_to_all(array, axes):
    count = lax.axis_size(axes)
    return exchange(jnp.broadcast_to(array[None], (count, *array.shape)), axes)


def ladder_kernel(place_ref, near_ref, far_ref, right_ref, out_ref, stack_ref):
    core, yh = place_ref[0], place_ref[1]
    b_count, depth, _ = stack_ref.shape
    ring, pair_rows = near_ref.shape[0], b_count
    c_pairs = near_ref.shape[1] // pair_rows - 2
    a_dev = pair_rows // 2
    d_count = right_ref.shape[0] // b_count
    right = right_ref[...]
    for n in range(0, c_pairs, 2):
        left = jnp.concatenate(
            [
                ref[x, m * pair_rows : (m + 1) * pair_rows, :]
                for m in (n, n + 1)
                for x in range(ring)
                for ref in (near_ref, far_ref)
            ],
            axis=0,
        )
        part = lax.dot_general(
            right, left, (((1,), (1,)), ((), ())), preferred_element_type=jnp.float32
        ).astype(jnp.bfloat16)
        part = part.reshape(b_count, d_count, 2 * LANES)
        for h in range(2):
            rows = (n + h) * d_count
            stack_ref[:, rows : rows + d_count, :] = part[:, :, h * LANES : (h + 1) * LANES]
    amps = jnp.concatenate(
        [
            ref[x, m * pair_rows : (m + 1) * pair_rows, :depth]
            for m in (c_pairs, c_pairs + 1)
            for ref in (near_ref, far_ref)
            for x in range(ring)
        ],
        axis=0,
    )
    blocks = 4 * ring
    odd = lax.rem(lax.broadcasted_iota(jnp.int32, (1, 1, LANES), 2) // a_dev, 2) == 1
    for q in range(b_count // 2):
        sums = []
        for b, step in ((2 * q, LANES - a_dev), (2 * q + 1, a_dev)):
            full = jnp.dot(amps, stack_ref[b], preferred_element_type=jnp.float32)
            full = full.reshape(blocks, 2, a_dev, LANES)
            mixed = jnp.where(odd, full[:, 1], full[:, 0]).reshape(blocks * a_dev, LANES)
            sums.append(mixed + pltpu.roll(mixed, step, 1))
        found = jnp.where(odd[0], sums[1], sums[0]).astype(out_ref.dtype)
        for block in range(blocks):
            other_yh, other_core, x = block // (2 * ring), block // ring % 2, block % ring
            place = (lax.rem(yh + other_yh, 2) * ring + x) * 2 + lax.rem(core + other_core, 2)
            for h in range(2):
                rows = found[block * a_dev + h * (a_dev // 2) : block * a_dev + (h + 1) * (a_dev // 2)]
                out_ref[2 * place + h, :, q * LANES : (q + 1) * LANES] = rows


def in_vmem(count):
    return [pl.BlockSpec(memory_space=pltpu.VMEM)] * count


def ladder_partials(place, near, far, right, b_count, i_count, con_count):
    depth = (near.shape[1] // b_count - 2) * (right.shape[0] // b_count)
    pairs = 2 * near.size * right.shape[0]
    return pl.pallas_call(
        ladder_kernel,
        out_shape=jax.ShapeDtypeStruct(
            (con_count, i_count // con_count, b_count * LANES // 2), jnp.bfloat16
        ),
        in_specs=[pl.BlockSpec(memory_space=pltpu.SMEM)] + in_vmem(3),
        out_specs=pl.BlockSpec(memory_space=pltpu.VMEM),
        scratch_shapes=[pltpu.VMEM((b_count, depth, LANES), jnp.bfloat16)],
        compiler_params=pltpu.CompilerParams(vmem_limit_bytes=12 * 1024 * 1024),
        cost_estimate=pl.CostEstimate(
            flops=2 * pairs, bytes_accessed=4 * near.size, transcendentals=0
        ),
    )(place, near, far, right)


def total_kernel(parts_ref, out_ref):
    total = parts_ref[0].astype(jnp.float32)
    for k in range(1, parts_ref.shape[0]):
        total = total + parts_ref[k].astype(jnp.float32)
    for o in range(out_ref.shape[0]):
        out_ref[o] = total


def totals(parts, copies):
    return pl.pallas_call(
        total_kernel,
        out_shape=jax.ShapeDtypeStruct((copies, *parts.shape[1:]), jnp.float32),
        in_specs=in_vmem(1),
        out_specs=pl.BlockSpec(memory_space=pltpu.VMEM),
        compiler_params=pltpu.CompilerParams(vmem_limit_bytes=4 * 1024 * 1024),
        cost_estimate=pl.CostEstimate(
            flops=parts.size, bytes_accessed=4 * parts.size, transcendentals=0
        ),
    )(parts)


def residual_kernel(ring, pairs_ref, swap_ref, every_ref, out_ref):
    slots, occ, width = out_ref.shape
    group = LANES // ring
    chunks = every_ref.shape[2] // LANES // 2
    lane_group = lax.broadcasted_iota(jnp.int32, (1, LANES), 1) // group

    def half_tile(a_tile, b_tile, c):
        holder = (a_tile // ring * ring + lax.rem(b_tile, ring)) * 2 + c
        first = b_tile // ring * (chunks * LANES)
        found = jnp.zeros((occ, LANES), jnp.float32)
        for m in range(chunks):
            block = every_ref[holder, :, pl.ds(pl.multiple_of(first + m * LANES, LANES), LANES)]
            shift = lax.rem((m + ring - lax.rem(a_tile, ring)) * group, LANES)
            found = jnp.where(lane_group == m, pltpu.roll(block, shift, 1), found)
        return found

    def tiles(role):
        return jnp.concatenate(
            [
                jnp.concatenate(
                    [half_tile(pairs_ref[s, role], pairs_ref[s, 1 - role], c) for c in range(2)],
                    axis=1,
                )
                for s in range(slots)
            ],
            axis=0,
        )

    def placed(rows, spot):
        column = lax.broadcasted_iota(jnp.int32, (width, width), 1)
        chosen = (column == spot).astype(jnp.float32)
        return jnp.dot(
            rows, chosen, preferred_element_type=jnp.float32, precision=lax.Precision.HIGHEST
        )

    lane = lax.broadcasted_iota(jnp.int32, (width, width), 0)
    core_b = lane // LANES
    core_a = lax.rem(lane // (group // 2) + core_b, 2)
    a = core_a * (TS // 2) + lax.rem(lane, TS // 2)
    b = core_b * (TS // 2) + lax.rem(lane, LANES) // group * 2 + lax.rem(lane // (TS // 2), 2)
    straight = placed(tiles(0), a * TS + b)
    mirror = placed(tiles(1), b * TS + a)
    row = lax.broadcasted_iota(jnp.int32, (slots * occ, slots * occ), 0)
    column = lax.broadcasted_iota(jnp.int32, (slots * occ, slots * occ), 1)
    source = row // occ * occ
    for i in range(occ):
        source = source + jnp.where(lax.rem(row, occ) == i, swap_ref[i], 0)
    turned = jnp.dot(
        (column == source).astype(jnp.float32),
        mirror,
        preferred_element_type=jnp.float32,
        precision=lax.Precision.HIGHEST,
    )
    total = straight + turned
    for s in range(slots):
        out_ref[s] = total[s * occ : (s + 1) * occ]


def residual_tiles(pairs, swap, every, ring):
    slots, occ = pairs.shape[0], swap.shape[0]
    return pl.pallas_call(
        functools.partial(residual_kernel, ring),
        out_shape=jax.ShapeDtypeStruct((slots, occ, TS * TS), jnp.float32),
        in_specs=[pl.BlockSpec(memory_space=pltpu.SMEM)] * 2 + in_vmem(1),
        out_specs=pl.BlockSpec(memory_space=pltpu.VMEM),
        compiler_params=pltpu.CompilerParams(vmem_limit_bytes=8 * 1024 * 1024),
        cost_estimate=pl.CostEstimate(
            flops=100 * every.size, bytes_accessed=4 * every.size, transcendentals=0
        ),
    )(pairs, swap, every)


def on_device(chol, amplitudes, tile_pairs, partner, pair_swap):
    out_count = lax.axis_size(OUT)
    con_count = lax.axis_size(CONTRACT)
    ring = lax.axis_size("x")
    a_dev, c_dev, p_size = chol.shape
    i_dev = amplitudes.shape[0]
    i_count = i_dev * out_count
    half = c_dev // 2
    pair_rows = 2 * a_dev

    other_amps = lax.ppermute(amplitudes, "yh", PAIR)
    rows = jnp.transpose(chol.reshape(a_dev, 2, half, p_size), (2, 1, 0, 3))
    extra = jnp.stack([amplitudes, other_amps], axis=0).reshape(2, i_dev, 2, -1)
    extra = jnp.transpose(extra, (0, 2, 1, 3)).reshape(2, pair_rows, -1)
    extra = jnp.pad(extra, ((0, 0), (0, 0), (0, p_size - extra.shape[2])))
    packed = jnp.concatenate([rows.reshape(half, pair_rows, p_size), extra], axis=0)
    near = sent_to_all(packed.reshape(-1, p_size), "x")

    z, yl = lax.axis_index("z"), lax.axis_index("yl")
    depth_z = lax.axis_size("z")
    window = chol.reshape(2, -1, p_size)
    piece = jnp.where(yl == 0, window[0], lax.ppermute(window[1], CONTRACT, [(0, 1)]))
    got = sum(lax.ppermute(piece, "z", [(0, to)]) for to in (8, 12, 4))
    piece = jnp.where(z == 0, piece, got)
    got = sum(
        lax.ppermute(
            piece, "z", [(at, (at + step) % depth_z) for at in range(0, depth_z, 4)]
        )
        for step in (2, 1, -1)
    )
    piece = jnp.where(z % 4 == 0, piece, got)
    right = sent_to_all(piece, ("yh", "yl")).reshape(-1, p_size)

    far = lax.ppermute(near, "core", PAIR)
    place = jnp.stack([lax.axis_index("core"), lax.axis_index("yh")])
    partial = ladder_partials(place, near, far, right, 2 * a_dev, i_count, con_count)
    every = exchange(totals(exchange(partial, CONTRACT), out_count), OUT)

    slot_count, occ_dev = tile_pairs.shape[0] // out_count, i_count // con_count
    first = lax.axis_index(OUT) * slot_count
    pairs = lax.dynamic_slice_in_dim(tile_pairs, first, slot_count, 0)
    first = lax.axis_index(CONTRACT) * occ_dev
    swap = lax.dynamic_slice_in_dim(pair_swap, first, occ_dev, 0) - first
    return residual_tiles(pairs, swap, every, ring)


def solution(mesh):
    torus = Mesh(mesh.devices.reshape(16, 2, 2, 4, 2), ("z", "yl", "yh", "x", "core"))
    in_specs = (P(OUT, CONTRACT, None), P(OUT, CONTRACT), P(), P(), P())
    out_specs = P(OUT, CONTRACT, None)

    return jax.shard_map(
        on_device, mesh=torus, in_specs=in_specs, out_specs=out_specs, check_vma=False
    )
```

time: 136 us -> 136 us (level)
  blocking collectives: 0 us -> 31.5 us
  waiting for transfers between devices: 50.5 us -> 35.7 us
  starting transfers between devices: 66.8 us -> 56.3 us
  local copies, waits for them, and re-layouts: 10.9 us -> 3.45 us
  Pallas kernels: 4.33 us -> 7.18 us
  other arithmetic: 2.86 us -> 1.02 us
    all_to_all x0 -> x1, blocking collectives: none -> 31.5 us  [exchange(): return lax.all_to_all(array, axes, 0, 0, tiled=True)]
    all_to_all x4 -> x3, waiting for transfers between devices: 39.1 us -> 26.9 us  [exchange(): return lax.all_to_all(array, axes, 0, 0, tiled=True)]
    all_to_all x4 -> x3, starting transfers between devices: 27.5 us -> 16.9 us  [exchange(): return lax.all_to_all(array, axes, 0, 0, tiled=True)]
    ppermute x1, waiting for transfers between devices: 3.81 us -> 0.24 us  [on_device(): other_amps = lax.ppermute(amplitudes, 'yh', PAIR)]
    pallas_call x0 -> x2, Pallas kernels: none -> 2.75 us  [the longest x1 1.98 us: residual_tiles(): pl.pallas_call(functools.partial(residual_kernel, ring), out_shape=jax.Sh...]
    unnamed x10 -> x7, local copies, waits for them, and re-layouts: 2.45 us -> 0.11 us
    ppermute x3, starting transfers between devices: 18.7 us -> 16.8 us  [on_device(): got = sum((lax.ppermute(piece, 'z', [(0, to)]) for to in (8, 12, 4)))]
    gather x4 -> x0, local copies, waits for them, and re-layouts: 1.74 us -> none  [the longest x3 1.15 us: whole_tiles(): found = jnp.take(every, spots.reshape(-1), axis=0, mode='clip')]
  transfers between devices with their start and end apart: 13 -> 12, of which waited for: 10 -> 8; matrix products, arithmetic and copies ran while one was open for 2% -> 2% of each run, Pallas kernels for 0% -> 0%
where the time goes in v3:
time: 136 us; the launch traced here: 135 us
  starting transfers between devices  56.3 us (41%)
  waiting for transfers between devices  35.7 us (26%)
  blocking collectives  31.5 us (23%)
  Pallas kernels  7.18 us (5%)
  local copies, waits for them, and re-layouts  3.45 us (3%)
    all_to_all x1, blocking collectives, exchange(): return lax.all_to_all(array, axes, 0, 0, tiled=True)  31.5 us
    all_to_all x3, waiting for transfers between devices, exchange(): return lax.all_to_all(array, axes, 0, 0, tiled=True)  26.9 us
    all_to_all x3, starting transfers between devices, exchange(): return lax.all_to_all(array, axes, 0, 0, tiled=True)  16.9 us
    ppermute x3, starting transfers between devices, on_device(): got = sum((lax.ppermute(piece, 'z', [(0, to)]) for to in (8, 12, 4)))  16.8 us
    ppermute x1, starting transfers between devices, on_device(): far = lax.ppermute(near, 'core', PAIR)  9.73 us
    ppermute x1, starting transfers between devices, on_device(): other_amps = lax.ppermute(amplitudes, 'yh', PAIR)  5.76 us
    ppermute x3, waiting for transfers between devices, on_device(): lax.ppermute(piece, 'z', [(at, (at + step) % depth_z) for at in range(0,...  5.13 us
    pallas_call x1, Pallas kernels, ladder_partials(): pl.pallas_call(ladder_kernel, out_shape=jax.ShapeDtypeStruct((con_count,...  4.43 us
  transfers between devices with their start and end apart: 12, of which 8 were waited for; matrix products, arithmetic and copies ran while one was open for 2% of the time, Pallas kernels for 0%

profile of v3, /device:TPU:1, one launch (start us, length us, event | category | flops | bytes accessed | tf_op | source)
XLA Modules:
  0.0 135.3 jit_solution(4355519788700273433)
XLA Ops:
  0.0 5.8 %collective-permute-start = (bf16[8,1024]{1,0:T(8,128)(2,1)}, bf16[8,1024]{1,0:T(8,128)(2,1)S(1)}, u32[]{:S(2)}, u32[]{:S(2)}) collective-permute-start(bf16[8,1024]{1,0:T(8,128)(2,1)} %param.6), channel_id=1, source_target_pairs={{0,8},{8,0},{1,9},{9,1},{2,10},{10,2},{3,11},{11,3},{4,12},{12,4},... | collective-permute-start | bytes 49160 | tf_op jit(solution)/shard_map/ppermute | solution.py:204
  5.8 1.1 copy.11
  6.9 0.2 collective-permute-done
  7.1 0.7 maximum_bitcast_fusion
  7.9 1.2 broadcast_in_dim.14
  9.1 4.2 %all-to-all-start = ((bf16[4,288,640]{2,1,0:T(8,128)(2,1)}), bf16[4,288,640]{2,1,0:T(8,128)(2,1)S(1)}, u32[]{:S(2)}, u32[]{:S(2)}) async-start(bf16[4,288,640]{2,1,0:T(8,128)(2,1)} %broadcast_in_dim.14), calls=%async_computation | async-start | bytes 2949120 | tf_op jit(solution)/shard_map/all_to_all | solution.py:19
  13.3 3.2 %collective-permute-start.2 = (bf16[128,640]{1,0:T(8,128)(2,1)S(1)}, bf16[128,640]{1,0:T(8,128)(2,1)S(1)}, u32[]{:S(2)}, u32[]{:S(2)}) collective-permute-start(bf16[128,640]{1,0:T(8,128)(2,1)S(1)} %bitcast.23), channel_id=1, source_target_pairs={{0,16},{1,17},{2,18},{3,19},{4,20},{5,21},{6,22},{7,23},{8,24},{9,... | collective-permute-start | bytes 491528 | tf_op jit(solution)/shard_map/ppermute | solution.py:215
  16.6 9.5 %all-to-all-done.near_ref = bf16[4,288,640]{2,1,0:T(8,128)(2,1)S(1)} async-done(((bf16[4,288,640]{2,1,0:T(8,128)(2,1)}), bf16[4,288,640]{2,1,0:T(8,128)(2,1)S(1)}, u32[]{:S(2)}, u32[]{:S(2)}) %all-to-all-start) | async-done | bytes 1474592 | tf_op jit(solution)/shard_map/all_to_all | solution.py:19
  26.1 9.7 %collective-permute-start.1 = (bf16[4,288,640]{2,1,0:T(8,128)(2,1)S(1)}, bf16[4,288,640]{2,1,0:T(8,128)(2,1)}, u32[]{:S(2)}, u32[]{:S(2)}) collective-permute-start(bf16[4,288,640]{2,1,0:T(8,128)(2,1)S(1)} %all-to-all-done.near_ref), channel_id=1, source_target_pairs={{0,1},{1,0},{2,3},{3,2},{4,5},{5,4},{6,7},{7,6},{8,9},{9,8},{10,11... | collective-permute-start | bytes 4423688 | tf_op jit(solution)/shard_map/ppermute | solution.py:227
  35.9 8.8 %collective-permute-start.5 = (bf16[128,640]{1,0:T(8,128)(2,1)S(1)}, bf16[128,640]{1,0:T(8,128)(2,1)S(1)}, u32[]{:S(2)}, u32[]{:S(2)}) collective-permute-start(bf16[128,640]{1,0:T(8,128)(2,1)S(1)} %bitcast_select_fusion), channel_id=1, source_target_pairs={{0,128},{1,129},{2,130},{3,131},{4,132},{5,133},{6,134},{7,135},{8... | collective-permute-start | bytes 491528 | tf_op jit(solution)/shard_map/ppermute | solution.py:216
  44.7 4.3 %collective-permute-start.4 = (bf16[128,640]{1,0:T(8,128)(2,1)S(1)}, bf16[128,640]{1,0:T(8,128)(2,1)S(1)}, u32[]{:S(2)}, u32[]{:S(2)}) collective-permute-start(bf16[128,640]{1,0:T(8,128)(2,1)S(1)} %bitcast_select_fusion), channel_id=1, source_target_pairs={{0,384},{1,385},{2,386},{3,387},{4,388},{5,389},{6,390},{7,391},{8... | collective-permute-start | bytes 491528 | tf_op jit(solution)/shard_map/ppermute | solution.py:216
  49.0 3.7 %collective-permute-start.3 = (bf16[128,640]{1,0:T(8,128)(2,1)S(1)}, bf16[128,640]{1,0:T(8,128)(2,1)S(1)}, u32[]{:S(2)}, u32[]{:S(2)}) collective-permute-start(bf16[128,640]{1,0:T(8,128)(2,1)S(1)} %bitcast_select_fusion), channel_id=1, source_target_pairs={{0,256},{1,257},{2,258},{3,259},{4,260},{5,261},{6,262},{7,263},{8... | collective-permute-start | bytes 491528 | tf_op jit(solution)/shard_map/ppermute | solution.py:216
  52.7 3.5 %collective-permute-done.3 = bf16[128,640]{1,0:T(8,128)(2,1)S(1)} collective-permute-done((bf16[128,640]{1,0:T(8,128)(2,1)S(1)}, bf16[128,640]{1,0:T(8,128)(2,1)S(1)}, u32[]{:S(2)}, u32[]{:S(2)}) %collective-permute-start.3) | collective-permute-done | bytes 163872 | tf_op jit(solution)/shard_map/ppermute | solution.py:216
  56.2 1.3 collective-permute-start.8
  57.5 1.3 collective-permute-start.7
  58.9 1.3 collective-permute-start.6
  60.2 0.3 collective-permute-done.8
  60.5 1.3 collective-permute-done.7
  61.8 3.5 %collective-permute-done.6 = bf16[128,640]{1,0:T(8,128)(2,1)S(1)} collective-permute-done((bf16[128,640]{1,0:T(8,128)(2,1)S(1)}, bf16[128,640]{1,0:T(8,128)(2,1)S(1)}, u32[]{:S(2)}, u32[]{:S(2)}) %collective-permute-start.6) | collective-permute-done | bytes 163872 | tf_op jit(solution)/shard_map/ppermute | solution.py:219
  65.3 0.9 broadcast_in_dim.15
  66.3 4.2 %all-to-all-start.1 = ((bf16[4,128,640]{2,1,0:T(8,128)(2,1)}), bf16[4,128,640]{2,1,0:T(8,128)(2,1)S(1)}, u32[]{:S(2)}, u32[]{:S(2)}) async-start(bf16[4,128,640]{2,1,0:T(8,128)(2,1)} %broadcast_in_dim.15), calls=%async_computation.1 | async-start | bytes 1310720 | tf_op jit(solution)/shard_map/all_to_all | solution.py:19
  70.4 0.1 pad_add_fusion.place_ref
  70.5 8.9 %all-to-all-done.1 = bf16[4,128,640]{2,1,0:T(8,128)(2,1)S(1)} async-done(((bf16[4,128,640]{2,1,0:T(8,128)(2,1)}), bf16[4,128,640]{2,1,0:T(8,128)(2,1)S(1)}, u32[]{:S(2)}, u32[]{:S(2)}) %all-to-all-start.1) | async-done | bytes 655392 | tf_op jit(solution)/shard_map/all_to_all | solution.py:19
  79.4 4.4 %shard_map.46 = bf16[32,4,1024]{2,1,0:T(4,128)(2,1)S(1)} custom-call(s32[2]{0:T(128)S(1)} %pad_add_fusion.place_ref, bf16[4,288,640]{2,1,0:T(8,128)(2,1)S(1)} %all-to-all-done.near_ref, bf16[4,288,640]{2,1,0:T(8,128)(2,1)} %collective-permute-done.1.far_ref, bf16[512,640]{1,0:T(8,128)(2,1)S(1)} %bitcast.19), custom_call_target="tpu_custom_call" | custom-call | flops 1509949440 | bytes 2949120 | tf_op jit(solution)/shard_map/pallas_call | solution.py:86
  83.8 31.5 %all_to_all.20.parts_ref = bf16[32,4,1024]{2,1,0:T(4,128)(2,1)S(1)} all-to-all(bf16[32,4,1024]{2,1,0:T(4,128)(2,1)S(1)} %shard_map.46), channel_id=1, replica_groups=mesh['z'=16,'yl'=2,'yh'=2,'x'=4,'core'=2] {'z','yl'}, dimensions={0} | all-to-all | bytes 524288 | tf_op jit(solution)/shard_map/all_to_all | solution.py:19
  115.3 0.8 shard_map.47
  116.1 8.5 %all-to-all-start.3 = ((f32[16,4,1024]{2,1,0:T(4,128)}), f32[16,4,1024]{2,1,0:T(4,128)S(1)}, u32[]{:S(2)}, u32[]{:S(2)}) async-start(f32[16,4,1024]{2,1,0:T(4,128)} %shard_map.47), calls=%async_computation.3 | async-start | bytes 524288 | tf_op jit(solution)/shard_map/all_to_all | solution.py:19
  124.6 0.1 constant_dynamic-slice_fusion
  124.7 0.1 copy.9.pairs_ref
  124.8 0.1 dynamic-slice_subtract_fusion.swap_ref
  124.8 8.4 %all-to-all-done.3.every_ref = f32[16,4,1024]{2,1,0:T(4,128)S(1)} async-done(((f32[16,4,1024]{2,1,0:T(4,128)}), f32[16,4,1024]{2,1,0:T(4,128)S(1)}, u32[]{:S(2)}, u32[]{:S(2)}) %all-to-all-start.3) | async-done | bytes 262176 | tf_op jit(solution)/shard_map/all_to_all | solution.py:19
  133.3 2.0 %shard_map.48 = f32[4,4,256]{2,1,0:T(4,128)} custom-call(s32[4,2]{1,0:T(4,128)S(1)} %copy.9.pairs_ref, s32[4]{0:T(128)S(1)} %dynamic-slice_subtract_fusion.swap_ref, f32[16,4,1024]{2,1,0:T(4,128)S(1)} %all-to-all-done.3.every_ref), custom_call_target="tpu_custom_call" | custom-call | flops 6553600 | bytes 262144 | tf_op jit(solution)/shard_map/pallas_call | solution.py:182
  (15 shorter events, 0.2 us)
Async XLA Ops:
  0.0 124.6 %copy-start = (s32[64,2]{0,1:T(2,128)S(1)}, s32[64,2]{0,1:T(2,128)}, u32[]{:S(2)}) copy-start(s32[64,2]{0,1:T(2,128)} %param.7) | copy-start | bytes 1540
  0.0 7.1 %collective-permute-start = (bf16[8,1024]{1,0:T(8,128)(2,1)}, bf16[8,1024]{1,0:T(8,128)(2,1)S(1)}, u32[]{:S(2)}, u32[]{:S(2)}) collective-permute-start(bf16[8,1024]{1,0:T(8,128)(2,1)} %param.6), channel_id=1, source_target_pairs={{0,8},{8,0},{1,9},{9,1},{2,10},{10,2},{3,11},{11,3},{4,12},{12,4},... | collective-permute-start | bytes 49160 | tf_op jit(solution)/shard_map/ppermute | solution.py:204
  9.1 4.2 %copy-start.1 = (bf16[8,32,640]{2,1,0:T(8,128)(2,1)S(1)}, bf16[8,32,640]{2,1,0:T(8,128)(2,1)}, u32[]{:S(2)}) copy-start(bf16[8,32,640]{2,1,0:T(8,128)(2,1)} %param.5) | copy-start | bytes 983044
  9.1 17.0 %all-to-all-start = ((bf16[4,288,640]{2,1,0:T(8,128)(2,1)}), bf16[4,288,640]{2,1,0:T(8,128)(2,1)S(1)}, u32[]{:S(2)}, u32[]{:S(2)}) async-start(bf16[4,288,640]{2,1,0:T(8,128)(2,1)} %broadcast_in_dim.14), calls=%async_computation | async-start | bytes 2949120 | tf_op jit(solution)/shard_map/all_to_all | solution.py:19
  13.3 22.5 %collective-permute-start.2 = (bf16[128,640]{1,0:T(8,128)(2,1)S(1)}, bf16[128,640]{1,0:T(8,128)(2,1)S(1)}, u32[]{:S(2)}, u32[]{:S(2)}) collective-permute-start(bf16[128,640]{1,0:T(8,128)(2,1)S(1)} %bitcast.23), channel_id=1, source_target_pairs={{0,16},{1,17},{2,18},{3,19},{4,20},{5,21},{6,22},{7,23},{8,24},{9,... | collective-permute-start | bytes 491528 | tf_op jit(solution)/shard_map/ppermute | solution.py:215
  26.1 53.3 %collective-permute-start.1 = (bf16[4,288,640]{2,1,0:T(8,128)(2,1)S(1)}, bf16[4,288,640]{2,1,0:T(8,128)(2,1)}, u32[]{:S(2)}, u32[]{:S(2)}) collective-permute-start(bf16[4,288,640]{2,1,0:T(8,128)(2,1)S(1)} %all-to-all-done.near_ref), channel_id=1, source_target_pairs={{0,1},{1,0},{2,3},{3,2},{4,5},{5,4},{6,7},{7,6},{8,9},{9,8},{10,11... | collective-permute-start | bytes 4423688 | tf_op jit(solution)/shard_map/ppermute | solution.py:227
  35.9 16.8 %collective-permute-start.5 = (bf16[128,640]{1,0:T(8,128)(2,1)S(1)}, bf16[128,640]{1,0:T(8,128)(2,1)S(1)}, u32[]{:S(2)}, u32[]{:S(2)}) collective-permute-start(bf16[128,640]{1,0:T(8,128)(2,1)S(1)} %bitcast_select_fusion), channel_id=1, source_target_pairs={{0,128},{1,129},{2,130},{3,131},{4,132},{5,133},{6,134},{7,135},{8... | collective-permute-start | bytes 491528 | tf_op jit(solution)/shard_map/ppermute | solution.py:216
  44.7 8.0 %collective-permute-start.4 = (bf16[128,640]{1,0:T(8,128)(2,1)S(1)}, bf16[128,640]{1,0:T(8,128)(2,1)S(1)}, u32[]{:S(2)}, u32[]{:S(2)}) collective-permute-start(bf16[128,640]{1,0:T(8,128)(2,1)S(1)} %bitcast_select_fusion), channel_id=1, source_target_pairs={{0,384},{1,385},{2,386},{3,387},{4,388},{5,389},{6,390},{7,391},{8... | collective-permute-start | bytes 491528 | tf_op jit(solution)/shard_map/ppermute | solution.py:216
  49.0 7.2 %collective-permute-start.3 = (bf16[128,640]{1,0:T(8,128)(2,1)S(1)}, bf16[128,640]{1,0:T(8,128)(2,1)S(1)}, u32[]{:S(2)}, u32[]{:S(2)}) collective-permute-start(bf16[128,640]{1,0:T(8,128)(2,1)S(1)} %bitcast_select_fusion), channel_id=1, source_target_pairs={{0,256},{1,257},{2,258},{3,259},{4,260},{5,261},{6,262},{7,263},{8... | collective-permute-start | bytes 491528 | tf_op jit(solution)/shard_map/ppermute | solution.py:216
  56.2 4.2 %collective-permute-start.8 = (bf16[128,640]{1,0:T(8,128)(2,1)S(1)}, bf16[128,640]{1,0:T(8,128)(2,1)S(1)}, u32[]{:S(2)}, u32[]{:S(2)}) collective-permute-start(bf16[128,640]{1,0:T(8,128)(2,1)S(1)} %add_select_fusion.1), channel_id=1, source_target_pairs={{0,480},{128,96},{256,224},{384,352},{1,481},{129,97},{257,225},{3... | collective-permute-start | bytes 491528 | tf_op jit(solution)/shard_map/ppermute | solution.py:219
  57.5 4.2 %collective-permute-start.7 = (bf16[128,640]{1,0:T(8,128)(2,1)S(1)}, bf16[128,640]{1,0:T(8,128)(2,1)S(1)}, u32[]{:S(2)}, u32[]{:S(2)}) collective-permute-start(bf16[128,640]{1,0:T(8,128)(2,1)S(1)} %add_select_fusion.1), channel_id=1, source_target_pairs={{0,32},{128,160},{256,288},{384,416},{1,33},{129,161},{257,289},{3... | collective-permute-start | bytes 491528 | tf_op jit(solution)/shard_map/ppermute | solution.py:219
  58.9 6.4 %collective-permute-start.6 = (bf16[128,640]{1,0:T(8,128)(2,1)S(1)}, bf16[128,640]{1,0:T(8,128)(2,1)S(1)}, u32[]{:S(2)}, u32[]{:S(2)}) collective-permute-start(bf16[128,640]{1,0:T(8,128)(2,1)S(1)} %add_select_fusion.1), channel_id=1, source_target_pairs={{0,64},{128,192},{256,320},{384,448},{1,65},{129,193},{257,321},{3... | collective-permute-start | bytes 491528 | tf_op jit(solution)/shard_map/ppermute | solution.py:219
  66.3 13.1 %all-to-all-start.1 = ((bf16[4,128,640]{2,1,0:T(8,128)(2,1)}), bf16[4,128,640]{2,1,0:T(8,128)(2,1)S(1)}, u32[]{:S(2)}, u32[]{:S(2)}) async-start(bf16[4,128,640]{2,1,0:T(8,128)(2,1)} %broadcast_in_dim.15), calls=%async_computation.1 | async-start | bytes 1310720 | tf_op jit(solution)/shard_map/all_to_all | solution.py:19
  83.8 40.9 %copy-start.2 = (s32[128]{0:T(128)S(1)}, s32[128]{0:T(128)}, u32[]{:S(2)}) copy-start(s32[128]{0:T(128)} %param.8) | copy-start | bytes 1540
  116.1 17.2 %all-to-all-start.3 = ((f32[16,4,1024]{2,1,0:T(4,128)}), f32[16,4,1024]{2,1,0:T(4,128)S(1)}, u32[]{:S(2)}, u32[]{:S(2)}) async-start(f32[16,4,1024]{2,1,0:T(4,128)} %shard_map.47), calls=%async_computation.3 | async-start | bytes 524288 | tf_op jit(solution)/shard_map/all_to_all | solution.py:19

commit v4 on v3

--- a/solution.py
+++ b/solution.py
@@ -13,6 +13,7 @@
 CONTRACT = ("z", "yl")
 OUT = ("yh", "x", "core")
 PAIR = [(0, 1), (1, 0)]
+RELAYS = (5, 11)
 
 
 def exchange(array, axes):
@@ -24,8 +25,12 @@
     return exchange(jnp.broadcast_to(array[None], (count, *array.shape)), axes)
 
 
-def ladder_kernel(place_ref, near_ref, far_ref, right_ref, out_ref, stack_ref):
-    core, yh = place_ref[0], place_ref[1]
+def ladder_kernel(place_ref, near_ref, far_ref, *refs):
+    *quarter_refs, out_ref, stack_ref, right_ref = refs
+    core, yh, own = place_ref[0], place_ref[1], place_ref[2]
+    size = quarter_refs[0].shape[0]
+    for q, ref in enumerate(quarter_refs):
+        right_ref[pl.ds(pl.multiple_of((own ^ q) * size, size), size), :] = ref[...]
     b_count, depth, _ = stack_ref.shape
     ring, pair_rows = near_ref.shape[0], b_count
     c_pairs = near_ref.shape[1] // pair_rows - 2
@@ -80,22 +85,26 @@
     return [pl.BlockSpec(memory_space=pltpu.VMEM)] * count
 
 
-def ladder_partials(place, near, far, right, b_count, i_count, con_count):
-    depth = (near.shape[1] // b_count - 2) * (right.shape[0] // b_count)
-    pairs = 2 * near.size * right.shape[0]
+def ladder_partials(place, near, far, quarters, b_count, i_count, con_count):
+    right = (len(quarters) * quarters[0].shape[0], quarters[0].shape[1])
+    depth = (near.shape[1] // b_count - 2) * (right[0] // b_count)
+    pairs = 2 * near.size * right[0]
     return pl.pallas_call(
         ladder_kernel,
         out_shape=jax.ShapeDtypeStruct(
             (con_count, i_count // con_count, b_count * LANES // 2), jnp.bfloat16
         ),
-        in_specs=[pl.BlockSpec(memory_space=pltpu.SMEM)] + in_vmem(3),
+        in_specs=[pl.BlockSpec(memory_space=pltpu.SMEM)] + in_vmem(2 + len(quarters)),
         out_specs=pl.BlockSpec(memory_space=pltpu.VMEM),
-        scratch_shapes=[pltpu.VMEM((b_count, depth, LANES), jnp.bfloat16)],
+        scratch_shapes=[
+            pltpu.VMEM((b_count, depth, LANES), jnp.bfloat16),
+            pltpu.VMEM(right, jnp.bfloat16),
+        ],
         compiler_params=pltpu.CompilerParams(vmem_limit_bytes=12 * 1024 * 1024),
         cost_estimate=pl.CostEstimate(
             flops=2 * pairs, bytes_accessed=4 * near.size, transcendentals=0
         ),
-    )(place, near, far, right)
+    )(place, near, far, *quarters)
 
 
 def total_kernel(parts_ref, out_ref):
@@ -209,24 +218,28 @@
     packed = jnp.concatenate([rows.reshape(half, pair_rows, p_size), extra], axis=0)
     near = sent_to_all(packed.reshape(-1, p_size), "x")
 
-    z, yl = lax.axis_index("z"), lax.axis_index("yl")
+    z, yl, yh = lax.axis_index("z"), lax.axis_index("yl"), lax.axis_index("yh")
     depth_z = lax.axis_size("z")
     window = chol.reshape(2, -1, p_size)
     piece = jnp.where(yl == 0, window[0], lax.ppermute(window[1], CONTRACT, [(0, 1)]))
-    got = sum(lax.ppermute(piece, "z", [(0, to)]) for to in (8, 12, 4))
+    got = sum(lax.ppermute(piece, "z", [(0, to)]) for to in RELAYS)
     piece = jnp.where(z == 0, piece, got)
-    got = sum(
-        lax.ppermute(
-            piece, "z", [(at, (at + step) % depth_z) for at in range(0, depth_z, 4)]
-        )
-        for step in (2, 1, -1)
-    )
-    piece = jnp.where(z % 4 == 0, piece, got)
-    right = sent_to_all(piece, ("yh", "yl")).reshape(-1, p_size)
+    reach = {}
+    for to in range(depth_z):
+        if to and to not in RELAYS:
+            steps = [((to - at + depth_z // 2) % depth_z - depth_z // 2, at) for at in (0, *RELAYS)]
+            step, at = min(steps, key=lambda pair: abs(pair[0]))
+            reach.setdefault(step, []).append((at, to))
+    got = sum(lax.ppermute(piece, "z", reach[step]) for step in sorted(reach, key=abs, reverse=True))
+    sender = functools.reduce(jnp.logical_or, [z == at for at in (0, *RELAYS)])
+    piece = jnp.where(sender, piece, got)
+    quarters = [piece] + [
+        lax.ppermute(piece, ("yl", "yh"), [(at, at ^ q) for at in range(4)]) for q in (2, 1, 3)
+    ]
 
     far = lax.ppermute(near, "core", PAIR)
-    place = jnp.stack([lax.axis_index("core"), lax.axis_index("yh")])
-    partial = ladder_partials(place, near, far, right, 2 * a_dev, i_count, con_count)
+    place = jnp.stack([lax.axis_index("core"), yh, 2 * yh + yl])
+    partial = ladder_partials(place, near, far, quarters, 2 * a_dev, i_count, con_count)
     every = exchange(totals(exchange(partial, CONTRACT), out_count), OUT)
 
     slot_count, occ_dev = tile_pairs.shape[0] // out_count, i_count // con_count

time: 136 us -> 143 us (1.051)
  waiting for transfers between devices: 35.7 us -> 27.1 us
  starting transfers between devices: 56.3 us -> 64.8 us
  blocking collectives: 31.5 us -> 37.5 us
  other arithmetic: 1.02 us -> 3.13 us
    ppermute x6 -> x10, starting transfers between devices: 20.7 us -> 33.9 us  [the longest x2 16.1 us: on_device(): got = sum((lax.ppermute(piece, 'z', [(0, to)]) for to in RELAYS))]
    all_to_all x3 -> x2, waiting for transfers between devices: 26.9 us -> 18 us  [exchange(): return lax.all_to_all(array, axes, 0, 0, tiled=True)]
    all_to_all x1, blocking collectives: 31.5 us -> 37.5 us  [exchange(): return lax.all_to_all(array, axes, 0, 0, tiled=True)]
    all_to_all x3 -> x2, starting transfers between devices: 16.9 us -> 12.3 us  [exchange(): return lax.all_to_all(array, axes, 0, 0, tiled=True)]
    ppermute x6 -> x10, waiting for transfers between devices: 8.62 us -> 8.86 us  [the longest x3 4.53 us: on_device(): lax.ppermute(piece, ('yl', 'yh'), [(at, at ^ q) for at in range(4)])]
  transfers between devices with their start and end apart: 12 -> 15, of which waited for: 8 -> 9; matrix products, arithmetic and copies ran while one was open for 2% -> 3% of each run, Pallas kernels for 0% -> 0%
where the time goes in v4:
time: 143 us
  starting transfers between devices  64.8 us (45%)
  blocking collectives  37.5 us (26%)
  waiting for transfers between devices  27.1 us (19%)
  Pallas kernels  6.69 us (5%)
  local copies, waits for them, and re-layouts  3.2 us (2%)
  other arithmetic  3.13 us (2%)
    all_to_all x1, blocking collectives, exchange(): return lax.all_to_all(array, axes, 0, 0, tiled=True)  37.5 us
    all_to_all x2, waiting for transfers between devices, exchange(): return lax.all_to_all(array, axes, 0, 0, tiled=True)  18 us
    ppermute x2, starting transfers between devices, on_device(): got = sum((lax.ppermute(piece, 'z', [(0, to)]) for to in RELAYS))  16.1 us
    all_to_all x2, starting transfers between devices, exchange(): return lax.all_to_all(array, axes, 0, 0, tiled=True)  12.3 us
    ppermute x3, starting transfers between devices, on_device(): lax.ppermute(piece, ('yl', 'yh'), [(at, at ^ q) for at in range(4)])  9.95 us
    ppermute x1, starting transfers between devices, on_device(): far = lax.ppermute(near, 'core', PAIR)  9.73 us
    ppermute x5, starting transfers between devices, on_device(): lax.ppermute(piece, 'z', reach[step])  7.83 us
    ppermute x1, starting transfers between devices, on_device(): other_amps = lax.ppermute(amplitudes, 'yh', PAIR)  5.76 us
  transfers between devices with their start and end apart: 15, of which 9 were waited for; matrix products, arithmetic and copies ran while one was open for 3% of the time, Pallas kernels for 0%

profile of v4, /device:TPU:1, one launch (start us, length us, event | category | flops | bytes accessed | tf_op | source)
XLA Modules:
  0.0 142.6 jit_solution(18174043061760223945)
XLA Ops:
  0.0 5.8 %collective-permute-start = (bf16[8,1024]{1,0:T(8,128)(2,1)}, bf16[8,1024]{1,0:T(8,128)(2,1)S(1)}, u32[]{:S(2)}, u32[]{:S(2)}) collective-permute-start(bf16[8,1024]{1,0:T(8,128)(2,1)} %param.6), channel_id=1, source_target_pairs={{0,8},{8,0},{1,9},{9,1},{2,10},{10,2},{3,11},{11,3},{4,12},{12,4},... | collective-permute-start | bytes 49160 | tf_op jit(solution)/shard_map/ppermute | solution.py:213
  5.8 1.1 copy.11
  7.1 0.7 maximum_bitcast_fusion
  7.9 1.3 broadcast_in_dim.8
  9.1 4.2 %all-to-all-start = ((bf16[4,288,640]{2,1,0:T(8,128)(2,1)}), bf16[4,288,640]{2,1,0:T(8,128)(2,1)S(1)}, u32[]{:S(2)}, u32[]{:S(2)}) async-start(bf16[4,288,640]{2,1,0:T(8,128)(2,1)} %broadcast_in_dim.8), calls=%async_computation | async-start | bytes 2949120 | tf_op jit(solution)/shard_map/all_to_all | solution.py:20
  13.3 3.2 %collective-permute-start.2 = (bf16[128,640]{1,0:T(8,128)(2,1)S(1)}, bf16[128,640]{1,0:T(8,128)(2,1)S(1)}, u32[]{:S(2)}, u32[]{:S(2)}) collective-permute-start(bf16[128,640]{1,0:T(8,128)(2,1)S(1)} %bitcast.22), channel_id=1, source_target_pairs={{0,16},{1,17},{2,18},{3,19},{4,20},{5,21},{6,22},{7,23},{8,24},{9,... | collective-permute-start | bytes 491528 | tf_op jit(solution)/shard_map/ppermute | solution.py:224
  16.6 9.5 %all-to-all-done.near_ref = bf16[4,288,640]{2,1,0:T(8,128)(2,1)S(1)} async-done(((bf16[4,288,640]{2,1,0:T(8,128)(2,1)}), bf16[4,288,640]{2,1,0:T(8,128)(2,1)S(1)}, u32[]{:S(2)}, u32[]{:S(2)}) %all-to-all-start) | async-done | bytes 1474592 | tf_op jit(solution)/shard_map/all_to_all | solution.py:20
  26.1 9.7 %collective-permute-start.1 = (bf16[4,288,640]{2,1,0:T(8,128)(2,1)S(1)}, bf16[4,288,640]{2,1,0:T(8,128)(2,1)S(1)}, u32[]{:S(2)}, u32[]{:S(2)}) collective-permute-start(bf16[4,288,640]{2,1,0:T(8,128)(2,1)S(1)} %all-to-all-done.near_ref), channel_id=1, source_target_pairs={{0,1},{1,0},{2,3},{3,2},{4,5},{5,4},{6,7},{7,6},{8,9},{9,8},{10,11... | collective-permute-start | bytes 4423688 | tf_op jit(solution)/shard_map/ppermute | solution.py:240
  35.8 0.7 copy-done.2
  36.5 14.1 %collective-permute-start.4 = (bf16[128,640]{1,0:T(8,128)(2,1)S(1)}, bf16[128,640]{1,0:T(8,128)(2,1)S(1)}, u32[]{:S(2)}, u32[]{:S(2)}) collective-permute-start(bf16[128,640]{1,0:T(8,128)(2,1)S(1)} %bitcast_select_fusion), channel_id=1, source_target_pairs={{0,352},{1,353},{2,354},{3,355},{4,356},{5,357},{6,358},{7,359},{8... | collective-permute-start | bytes 491528 | tf_op jit(solution)/shard_map/ppermute | solution.py:225
  50.7 2.0 %collective-permute-start.3 = (bf16[128,640]{1,0:T(8,128)(2,1)S(1)}, bf16[128,640]{1,0:T(8,128)(2,1)}, u32[]{:S(2)}, u32[]{:S(2)}) collective-permute-start(bf16[128,640]{1,0:T(8,128)(2,1)S(1)} %bitcast_select_fusion), channel_id=1, source_target_pairs={{0,160},{1,161},{2,162},{3,163},{4,164},{5,165},{6,166},{7,167},{8... | collective-permute-start | bytes 491528 | tf_op jit(solution)/shard_map/ppermute | solution.py:225
  52.6 1.6 %collective-permute-done.4 = bf16[128,640]{1,0:T(8,128)(2,1)S(1)} collective-permute-done((bf16[128,640]{1,0:T(8,128)(2,1)S(1)}, bf16[128,640]{1,0:T(8,128)(2,1)S(1)}, u32[]{:S(2)}, u32[]{:S(2)}) %collective-permute-start.4) | collective-permute-done | bytes 163872 | tf_op jit(solution)/shard_map/ppermute | solution.py:225
  54.2 1.3 collective-permute-done.3
  55.5 1.0 add_select_fusion.1
  56.4 1.3 collective-permute-start.9
  57.8 1.3 collective-permute-start.8
  59.1 2.0 %collective-permute-start.7 = (bf16[128,640]{1,0:T(8,128)(2,1)S(1)}, bf16[128,640]{1,0:T(8,128)(2,1)}, u32[]{:S(2)}, u32[]{:S(2)}) collective-permute-start(bf16[128,640]{1,0:T(8,128)(2,1)S(1)} %add_select_fusion.1), channel_id=1, source_target_pairs={{160,96},{352,288},{0,448},{161,97},{353,289},{1,449},{162,98},{35... | collective-permute-start | bytes 491528 | tf_op jit(solution)/shard_map/ppermute | solution.py:233
  61.0 2.0 %collective-permute-start.6 = (bf16[128,640]{1,0:T(8,128)(2,1)S(1)}, bf16[128,640]{1,0:T(8,128)(2,1)}, u32[]{:S(2)}, u32[]{:S(2)}) collective-permute-start(bf16[128,640]{1,0:T(8,128)(2,1)S(1)} %add_select_fusion.1), channel_id=1, source_target_pairs={{0,64},{160,224},{352,416},{1,65},{161,225},{353,417},{2,66},{162,... | collective-permute-start | bytes 491528 | tf_op jit(solution)/shard_map/ppermute | solution.py:233
  63.0 1.3 collective-permute-start.5
  64.4 1.4 collective-permute-done.6
  65.8 1.2 add_select_fusion.refs_0_
  67.0 5.5 %collective-permute-start.12 = (bf16[128,640]{1,0:T(8,128)(2,1)S(1)}, bf16[128,640]{1,0:T(8,128)(2,1)S(1)}, u32[]{:S(2)}, u32[]{:S(2)}) collective-permute-start(bf16[128,640]{1,0:T(8,128)(2,1)S(1)} %add_select_fusion.refs_0_), channel_id=1, source_target_pairs={{0,24},{8,16},{16,8},{24,0},{1,25},{9,17},{17,9},{25,1},{2,26},{10... | collective-permute-start | bytes 491528 | tf_op jit(solution)/shard_map/ppermute | solution.py:237
  72.6 2.3 %collective-permute-start.11 = (bf16[128,640]{1,0:T(8,128)(2,1)S(1)}, bf16[128,640]{1,0:T(8,128)(2,1)S(1)}, u32[]{:S(2)}, u32[]{:S(2)}) collective-permute-start(bf16[128,640]{1,0:T(8,128)(2,1)S(1)} %add_select_fusion.refs_0_), channel_id=1, source_target_pairs={{0,8},{8,0},{16,24},{24,16},{1,9},{9,1},{17,25},{25,17},{2,10},{10... | collective-permute-start | bytes 491528 | tf_op jit(solution)/shard_map/ppermute | solution.py:237
  74.8 2.1 %collective-permute-start.10 = (bf16[128,640]{1,0:T(8,128)(2,1)S(1)}, bf16[128,640]{1,0:T(8,128)(2,1)}, u32[]{:S(2)}, u32[]{:S(2)}) collective-permute-start(bf16[128,640]{1,0:T(8,128)(2,1)S(1)} %add_select_fusion.refs_0_), channel_id=1, source_target_pairs={{0,16},{8,24},{16,0},{24,8},{1,17},{9,25},{17,1},{25,9},{2,18},{10... | collective-permute-start | bytes 491528 | tf_op jit(solution)/shard_map/ppermute | solution.py:237
  77.1 3.1 %collective-permute-done.11.refs_2_ = bf16[128,640]{1,0:T(8,128)(2,1)S(1)} collective-permute-done((bf16[128,640]{1,0:T(8,128)(2,1)S(1)}, bf16[128,640]{1,0:T(8,128)(2,1)S(1)}, u32[]{:S(2)}, u32[]{:S(2)}) %collective-permute-start.11) | collective-permute-done | bytes 163872 | tf_op jit(solution)/shard_map/ppermute | solution.py:237
  80.1 1.5 %collective-permute-done.10.refs_1_ = bf16[128,640]{1,0:T(8,128)(2,1)} collective-permute-done((bf16[128,640]{1,0:T(8,128)(2,1)S(1)}, bf16[128,640]{1,0:T(8,128)(2,1)}, u32[]{:S(2)}, u32[]{:S(2)}) %collective-permute-start.10) | collective-permute-done | bytes 163872 | tf_op jit(solution)/shard_map/ppermute | solution.py:237
  81.6 4.0 %shard_map.46 = bf16[32,4,1024]{2,1,0:T(4,128)(2,1)S(1)} custom-call(s32[3]{0:T(128)S(1)} %pad_add_fusion.place_ref, bf16[4,288,640]{2,1,0:T(8,128)(2,1)S(1)} %all-to-all-done.near_ref, bf16[4,288,640]{2,1,0:T(8,128)(2,1)S(1)} %collective-permute-done.1.far_ref, bf16[128,640]{1,0:T(8,128)(2,1)S(1)} %add_select_fusion.refs_0_, ...), custom_call_target="tpu_custom_call" | custom-call | flops 1509949440 | bytes 2949120 | tf_op jit(solution)/shard_map/pallas_call | solution.py:92
  85.6 37.5 %all_to_all.15.parts_ref = bf16[32,4,1024]{2,1,0:T(4,128)(2,1)S(1)} all-to-all(bf16[32,4,1024]{2,1,0:T(4,128)(2,1)S(1)} %shard_map.46), channel_id=1, replica_groups=mesh['z'=16,'yl'=2,'yh'=2,'x'=4,'core'=2] {'z','yl'}, dimensions={0} | all-to-all | bytes 524288 | tf_op jit(solution)/shard_map/all_to_all | solution.py:20
  123.1 0.8 shard_map.47
  123.9 8.1 %all-to-all-start.2 = ((f32[16,4,1024]{2,1,0:T(4,128)}), f32[16,4,1024]{2,1,0:T(4,128)S(1)}, u32[]{:S(2)}, u32[]{:S(2)}) async-start(f32[16,4,1024]{2,1,0:T(4,128)} %shard_map.47), calls=%async_computation.2 | async-start | bytes 524288 | tf_op jit(solution)/shard_map/all_to_all | solution.py:20
  132.2 8.4 %all-to-all-done.2.every_ref = f32[16,4,1024]{2,1,0:T(4,128)S(1)} async-done(((f32[16,4,1024]{2,1,0:T(4,128)}), f32[16,4,1024]{2,1,0:T(4,128)S(1)}, u32[]{:S(2)}, u32[]{:S(2)}) %all-to-all-start.2) | async-done | bytes 262176 | tf_op jit(solution)/shard_map/all_to_all | solution.py:20
  140.6 2.0 %shard_map.48 = f32[4,4,256]{2,1,0:T(4,128)} custom-call(s32[4,2]{1,0:T(4,128)S(1)} %copy.9.pairs_ref, s32[4]{0:T(128)S(1)} %dynamic-slice_subtract_fusion.swap_ref, f32[16,4,1024]{2,1,0:T(4,128)S(1)} %all-to-all-done.2.every_ref), custom_call_target="tpu_custom_call" | custom-call | flops 6553600 | bytes 262144 | tf_op jit(solution)/shard_map/pallas_call | solution.py:191
  (24 shorter events, 0.8 us)
Async XLA Ops:
  0.0 131.9 %copy-start = (s32[64,2]{0,1:T(2,128)S(1)}, s32[64,2]{0,1:T(2,128)}, u32[]{:S(2)}) copy-start(s32[64,2]{0,1:T(2,128)} %param.7) | copy-start | bytes 1540
  0.0 7.1 %collective-permute-start = (bf16[8,1024]{1,0:T(8,128)(2,1)}, bf16[8,1024]{1,0:T(8,128)(2,1)S(1)}, u32[]{:S(2)}, u32[]{:S(2)}) collective-permute-start(bf16[8,1024]{1,0:T(8,128)(2,1)} %param.6), channel_id=1, source_target_pairs={{0,8},{8,0},{1,9},{9,1},{2,10},{10,2},{3,11},{11,3},{4,12},{12,4},... | collective-permute-start | bytes 49160 | tf_op jit(solution)/shard_map/ppermute | solution.py:213
  9.1 4.2 %copy-start.1 = (bf16[8,32,640]{2,1,0:T(8,128)(2,1)S(1)}, bf16[8,32,640]{2,1,0:T(8,128)(2,1)}, u32[]{:S(2)}) copy-start(bf16[8,32,640]{2,1,0:T(8,128)(2,1)} %param.5) | copy-start | bytes 983044
  9.1 17.0 %all-to-all-start = ((bf16[4,288,640]{2,1,0:T(8,128)(2,1)}), bf16[4,288,640]{2,1,0:T(8,128)(2,1)S(1)}, u32[]{:S(2)}, u32[]{:S(2)}) async-start(bf16[4,288,640]{2,1,0:T(8,128)(2,1)} %broadcast_in_dim.8), calls=%async_computation | async-start | bytes 2949120 | tf_op jit(solution)/shard_map/all_to_all | solution.py:20
  13.3 22.5 %collective-permute-start.2 = (bf16[128,640]{1,0:T(8,128)(2,1)S(1)}, bf16[128,640]{1,0:T(8,128)(2,1)S(1)}, u32[]{:S(2)}, u32[]{:S(2)}) collective-permute-start(bf16[128,640]{1,0:T(8,128)(2,1)S(1)} %bitcast.22), channel_id=1, source_target_pairs={{0,16},{1,17},{2,18},{3,19},{4,20},{5,21},{6,22},{7,23},{8,24},{9,... | collective-permute-start | bytes 491528 | tf_op jit(solution)/shard_map/ppermute | solution.py:224
  26.1 55.5 %collective-permute-start.1 = (bf16[4,288,640]{2,1,0:T(8,128)(2,1)S(1)}, bf16[4,288,640]{2,1,0:T(8,128)(2,1)S(1)}, u32[]{:S(2)}, u32[]{:S(2)}) collective-permute-start(bf16[4,288,640]{2,1,0:T(8,128)(2,1)S(1)} %all-to-all-done.near_ref), channel_id=1, source_target_pairs={{0,1},{1,0},{2,3},{3,2},{4,5},{5,4},{6,7},{7,6},{8,9},{9,8},{10,11... | collective-permute-start | bytes 4423688 | tf_op jit(solution)/shard_map/ppermute | solution.py:240
  35.8 0.7 copy-start.2
  36.5 17.6 %collective-permute-start.4 = (bf16[128,640]{1,0:T(8,128)(2,1)S(1)}, bf16[128,640]{1,0:T(8,128)(2,1)S(1)}, u32[]{:S(2)}, u32[]{:S(2)}) collective-permute-start(bf16[128,640]{1,0:T(8,128)(2,1)S(1)} %bitcast_select_fusion), channel_id=1, source_target_pairs={{0,352},{1,353},{2,354},{3,355},{4,356},{5,357},{6,358},{7,359},{8... | collective-permute-start | bytes 491528 | tf_op jit(solution)/shard_map/ppermute | solution.py:225
  50.7 4.8 %collective-permute-start.3 = (bf16[128,640]{1,0:T(8,128)(2,1)S(1)}, bf16[128,640]{1,0:T(8,128)(2,1)}, u32[]{:S(2)}, u32[]{:S(2)}) collective-permute-start(bf16[128,640]{1,0:T(8,128)(2,1)S(1)} %bitcast_select_fusion), channel_id=1, source_target_pairs={{0,160},{1,161},{2,162},{3,163},{4,164},{5,165},{6,166},{7,167},{8... | collective-permute-start | bytes 491528 | tf_op jit(solution)/shard_map/ppermute | solution.py:225
  56.4 6.5 %collective-permute-start.9 = (bf16[128,640]{1,0:T(8,128)(2,1)S(1)}, bf16[128,640]{1,0:T(8,128)(2,1)S(1)}, u32[]{:S(2)}, u32[]{:S(2)}) collective-permute-start(bf16[128,640]{1,0:T(8,128)(2,1)S(1)} %add_select_fusion.1), channel_id=1, source_target_pairs={{160,128},{352,320},{0,480},{161,129},{353,321},{1,481},{162,130},... | collective-permute-start | bytes 491528 | tf_op jit(solution)/shard_map/ppermute | solution.py:233
  57.8 6.5 %collective-permute-start.8 = (bf16[128,640]{1,0:T(8,128)(2,1)S(1)}, bf16[128,640]{1,0:T(8,128)(2,1)S(1)}, u32[]{:S(2)}, u32[]{:S(2)}) collective-permute-start(bf16[128,640]{1,0:T(8,128)(2,1)S(1)} %add_select_fusion.1), channel_id=1, source_target_pairs={{0,32},{160,192},{352,384},{1,33},{161,193},{353,385},{2,34},{162,... | collective-permute-start | bytes 491528 | tf_op jit(solution)/shard_map/ppermute | solution.py:233
  59.1 5.3 %collective-permute-start.7 = (bf16[128,640]{1,0:T(8,128)(2,1)S(1)}, bf16[128,640]{1,0:T(8,128)(2,1)}, u32[]{:S(2)}, u32[]{:S(2)}) collective-permute-start(bf16[128,640]{1,0:T(8,128)(2,1)S(1)} %add_select_fusion.1), channel_id=1, source_target_pairs={{160,96},{352,288},{0,448},{161,97},{353,289},{1,449},{162,98},{35... | collective-permute-start | bytes 491528 | tf_op jit(solution)/shard_map/ppermute | solution.py:233
  61.0 4.7 %collective-permute-start.6 = (bf16[128,640]{1,0:T(8,128)(2,1)S(1)}, bf16[128,640]{1,0:T(8,128)(2,1)}, u32[]{:S(2)}, u32[]{:S(2)}) collective-permute-start(bf16[128,640]{1,0:T(8,128)(2,1)S(1)} %add_select_fusion.1), channel_id=1, source_target_pairs={{0,64},{160,224},{352,416},{1,65},{161,225},{353,417},{2,66},{162,... | collective-permute-start | bytes 491528 | tf_op jit(solution)/shard_map/ppermute | solution.py:233
  63.0 2.8 %collective-permute-start.5 = (bf16[128,640]{1,0:T(8,128)(2,1)S(1)}, bf16[128,640]{1,0:T(8,128)(2,1)}, u32[]{:S(2)}, u32[]{:S(2)}) collective-permute-start(bf16[128,640]{1,0:T(8,128)(2,1)S(1)} %add_select_fusion.1), channel_id=1, source_target_pairs={{160,256},{161,257},{162,258},{163,259},{164,260},{165,261},{166,2... | collective-permute-start | bytes 491528 | tf_op jit(solution)/shard_map/ppermute | solution.py:233
  64.3 1.5 %copy-start.3 = (bf16[128,640]{1,0:T(8,128)(2,1)}, bf16[128,640]{1,0:T(8,128)(2,1)S(1)}, u32[]{:S(2)}) copy-start(bf16[128,640]{1,0:T(8,128)(2,1)S(1)} %collective-permute-done.8) | copy-start | bytes 491524
  67.0 10.1 %collective-permute-start.12 = (bf16[128,640]{1,0:T(8,128)(2,1)S(1)}, bf16[128,640]{1,0:T(8,128)(2,1)S(1)}, u32[]{:S(2)}, u32[]{:S(2)}) collective-permute-start(bf16[128,640]{1,0:T(8,128)(2,1)S(1)} %add_select_fusion.refs_0_), channel_id=1, source_target_pairs={{0,24},{8,16},{16,8},{24,0},{1,25},{9,17},{17,9},{25,1},{2,26},{10... | collective-permute-start | bytes 491528 | tf_op jit(solution)/shard_map/ppermute | solution.py:237
  72.6 7.6 %collective-permute-start.11 = (bf16[128,640]{1,0:T(8,128)(2,1)S(1)}, bf16[128,640]{1,0:T(8,128)(2,1)S(1)}, u32[]{:S(2)}, u32[]{:S(2)}) collective-permute-start(bf16[128,640]{1,0:T(8,128)(2,1)S(1)} %add_select_fusion.refs_0_), channel_id=1, source_target_pairs={{0,8},{8,0},{16,24},{24,16},{1,9},{9,1},{17,25},{25,17},{2,10},{10... | collective-permute-start | bytes 491528 | tf_op jit(solution)/shard_map/ppermute | solution.py:237
  74.8 6.8 %collective-permute-start.10 = (bf16[128,640]{1,0:T(8,128)(2,1)S(1)}, bf16[128,640]{1,0:T(8,128)(2,1)}, u32[]{:S(2)}, u32[]{:S(2)}) collective-permute-start(bf16[128,640]{1,0:T(8,128)(2,1)S(1)} %add_select_fusion.refs_0_), channel_id=1, source_target_pairs={{0,16},{8,24},{16,0},{24,8},{1,17},{9,25},{17,1},{25,9},{2,18},{10... | collective-permute-start | bytes 491528 | tf_op jit(solution)/shard_map/ppermute | solution.py:237
  85.6 46.6 %copy-start.4 = (s32[128]{0:T(128)S(1)}, s32[128]{0:T(128)}, u32[]{:S(2)}) copy-start(s32[128]{0:T(128)} %param.8) | copy-start | bytes 1540
  123.9 16.8 %all-to-all-start.2 = ((f32[16,4,1024]{2,1,0:T(4,128)}), f32[16,4,1024]{2,1,0:T(4,128)S(1)}, u32[]{:S(2)}, u32[]{:S(2)}) async-start(f32[16,4,1024]{2,1,0:T(4,128)} %shard_map.47), calls=%async_computation.2 | async-start | bytes 524288 | tf_op jit(solution)/shard_map/all_to_all | solution.py:20

commit v5 on v4

--- a/solution.py
+++ b/solution.py
@@ -13,7 +13,8 @@
 CONTRACT = ("z", "yl")
 OUT = ("yh", "x", "core")
 PAIR = [(0, 1), (1, 0)]
-RELAYS = (5, 11)
+LONG, MIDDLE = [(0, 3), (0, 13)], [(3, 6), (13, 10)]
+SENDERS = (0, 3, 6, 10, 13)
 
 
 def exchange(array, axes):
@@ -156,32 +157,39 @@
             axis=0,
         )
 
-    def placed(rows, spot):
+    def thirds(rows):
+        high = rows.astype(jnp.bfloat16)
+        rest = rows - high.astype(jnp.float32)
+        middle = rest.astype(jnp.bfloat16)
+        low = (rest - middle.astype(jnp.float32)).astype(jnp.bfloat16)
+        return high, middle, low
+
+    def placed(parts, spot):
         column = lax.broadcasted_iota(jnp.int32, (width, width), 1)
-        chosen = (column == spot).astype(jnp.float32)
-        return jnp.dot(
-            rows, chosen, preferred_element_type=jnp.float32, precision=lax.Precision.HIGHEST
+        chosen = (column == spot).astype(jnp.float32).astype(jnp.bfloat16)
+        found = jnp.dot(
+            jnp.concatenate(parts, axis=0), chosen, preferred_element_type=jnp.float32
         )
+        high, middle, low = (found[n * slots * occ : (n + 1) * slots * occ] for n in range(3))
+        return high + middle + low
 
     lane = lax.broadcasted_iota(jnp.int32, (width, width), 0)
     core_b = lane // LANES
     core_a = lax.rem(lane // (group // 2) + core_b, 2)
     a = core_a * (TS // 2) + lax.rem(lane, TS // 2)
     b = core_b * (TS // 2) + lax.rem(lane, LANES) // group * 2 + lax.rem(lane // (TS // 2), 2)
-    straight = placed(tiles(0), a * TS + b)
-    mirror = placed(tiles(1), b * TS + a)
+    straight = placed(thirds(tiles(0)), a * TS + b)
     row = lax.broadcasted_iota(jnp.int32, (slots * occ, slots * occ), 0)
     column = lax.broadcasted_iota(jnp.int32, (slots * occ, slots * occ), 1)
     source = row // occ * occ
     for i in range(occ):
         source = source + jnp.where(lax.rem(row, occ) == i, swap_ref[i], 0)
-    turned = jnp.dot(
-        (column == source).astype(jnp.float32),
-        mirror,
-        preferred_element_type=jnp.float32,
-        precision=lax.Precision.HIGHEST,
-    )
-    total = straight + turned
+    chosen = (column == source).astype(jnp.float32).astype(jnp.bfloat16)
+    swapped = [
+        jnp.dot(chosen, part, preferred_element_type=jnp.float32).astype(jnp.bfloat16)
+        for part in thirds(tiles(1))
+    ]
+    total = straight + placed(swapped, b * TS + a)
     for s in range(slots):
         out_ref[s] = total[s * occ : (s + 1) * occ]
 
@@ -222,16 +230,20 @@
     depth_z = lax.axis_size("z")
     window = chol.reshape(2, -1, p_size)
     piece = jnp.where(yl == 0, window[0], lax.ppermute(window[1], CONTRACT, [(0, 1)]))
-    got = sum(lax.ppermute(piece, "z", [(0, to)]) for to in RELAYS)
+    got = sum(lax.ppermute(piece, "z", [hop]) for hop in LONG)
     piece = jnp.where(z == 0, piece, got)
+    got = lax.ppermute(piece, "z", MIDDLE)
+    piece = jnp.where(functools.reduce(jnp.logical_or, [z == to for _, to in MIDDLE]), got, piece)
     reach = {}
     for to in range(depth_z):
-        if to and to not in RELAYS:
-            steps = [((to - at + depth_z // 2) % depth_z - depth_z // 2, at) for at in (0, *RELAYS)]
+        if to not in SENDERS:
+            steps = [((to - at + depth_z // 2) % depth_z - depth_z // 2, at) for at in SENDERS]
             step, at = min(steps, key=lambda pair: abs(pair[0]))
             reach.setdefault(step, []).append((at, to))
-    got = sum(lax.ppermute(piece, "z", reach[step]) for step in sorted(reach, key=abs, reverse=True))
-    sender = functools.reduce(jnp.logical_or, [z == at for at in (0, *RELAYS)])
+    steps = sorted(reach, key=abs, reverse=True)
+    got = lax.ppermute(piece, "z", reach[steps[0]])
+    got = sum((lax.ppermute(piece, "z", reach[step]) for step in steps[1:]), got)
+    sender = functools.reduce(jnp.logical_or, [z == at for at in SENDERS])
     piece = jnp.where(sender, piece, got)
     quarters = [piece] + [
         lax.ppermute(piece, ("yl", "yh"), [(at, at ^ q) for at in range(4)]) for q in (2, 1, 3)

time: 143 us -> 141 us (0.986)
  starting transfers between devices: 64.8 us -> 60.4 us
  blocking collectives: 37.5 us -> 39.2 us
    ppermute x5 -> x2, starting transfers between devices: 7.83 us -> 2.6 us  [on_device(): lax.ppermute(piece, 'z', reach[step])]
    all_to_all x2, starting transfers between devices: 12.3 us -> 14 us  [exchange(): return lax.all_to_all(array, axes, 0, 0, tiled=True)]
    all_to_all x1, blocking collectives: 37.5 us -> 39.2 us  [exchange(): return lax.all_to_all(array, axes, 0, 0, tiled=True)]
    ppermute x2 -> x4, starting transfers between devices: 16.1 us -> 16 us  [the longest x2 14 us: on_device(): got = sum((lax.ppermute(piece, 'z', [hop]) for hop in LONG))]
    ppermute x2 -> x4, waiting for transfers between devices: 2.86 us -> 2.87 us  [the longest x2 2.86 us: on_device(): got = sum((lax.ppermute(piece, 'z', [hop]) for hop in LONG))]
  transfers between devices with their start and end apart: 15 -> 14, of which waited for: 9 -> 9; matrix products, arithmetic and copies ran while one was open for 3% -> 3% of each run, Pallas kernels for 0% -> 0%
where the time goes in v5:
time: 141 us; the launch traced here: 140 us
  starting transfers between devices  60.4 us (43%)
  blocking collectives  39.2 us (28%)
  waiting for transfers between devices  27.7 us (20%)
  Pallas kernels  6.35 us (5%)
  local copies, waits for them, and re-layouts  3.22 us (2%)
  other arithmetic  2.99 us (2%)
    all_to_all x1, blocking collectives, exchange(): return lax.all_to_all(array, axes, 0, 0, tiled=True)  39.2 us
    all_to_all x2, waiting for transfers between devices, exchange(): return lax.all_to_all(array, axes, 0, 0, tiled=True)  18 us
    all_to_all x2, starting transfers between devices, exchange(): return lax.all_to_all(array, axes, 0, 0, tiled=True)  14 us
    ppermute x2, starting transfers between devices, on_device(): got = sum((lax.ppermute(piece, 'z', [hop]) for hop in LONG))  14 us
    ppermute x1, starting transfers between devices, on_device(): far = lax.ppermute(near, 'core', PAIR)  9.73 us
    ppermute x3, starting transfers between devices, on_device(): lax.ppermute(piece, ('yl', 'yh'), [(at, at ^ q) for at in range(4)])  9.05 us
    ppermute x1, starting transfers between devices, on_device(): other_amps = lax.ppermute(amplitudes, 'yh', PAIR)  5.76 us
    ppermute x3, waiting for transfers between devices, on_device(): lax.ppermute(piece, ('yl', 'yh'), [(at, at ^ q) for at in range(4)])  4.97 us
  transfers between devices with their start and end apart: 14, of which 9 were waited for; matrix products, arithmetic and copies ran while one was open for 3% of the time, Pallas kernels for 0%

profile of v5, /device:TPU:1, one launch (start us, length us, event | category | flops | bytes accessed | tf_op | source)
XLA Modules:
  0.0 140.0 jit_solution(7014646729911938575)
XLA Ops:
  0.0 5.8 %collective-permute-start = (bf16[8,1024]{1,0:T(8,128)(2,1)}, bf16[8,1024]{1,0:T(8,128)(2,1)S(1)}, u32[]{:S(2)}, u32[]{:S(2)}) collective-permute-start(bf16[8,1024]{1,0:T(8,128)(2,1)} %param.6), channel_id=1, source_target_pairs={{0,8},{8,0},{1,9},{9,1},{2,10},{10,2},{3,11},{11,3},{4,12},{12,4},... | collective-permute-start | bytes 49160 | tf_op jit(solution)/shard_map/ppermute | solution.py:221
  5.8 1.1 copy.11
  7.1 0.7 maximum_bitcast_fusion
  7.9 1.3 broadcast_in_dim.8
  9.1 4.2 %all-to-all-start = ((bf16[4,288,640]{2,1,0:T(8,128)(2,1)}), bf16[4,288,640]{2,1,0:T(8,128)(2,1)S(1)}, u32[]{:S(2)}, u32[]{:S(2)}) async-start(bf16[4,288,640]{2,1,0:T(8,128)(2,1)} %broadcast_in_dim.8), calls=%async_computation | async-start | bytes 2949120 | tf_op jit(solution)/shard_map/all_to_all | solution.py:21
  13.3 3.2 %collective-permute-start.2 = (bf16[128,640]{1,0:T(8,128)(2,1)S(1)}, bf16[128,640]{1,0:T(8,128)(2,1)S(1)}, u32[]{:S(2)}, u32[]{:S(2)}) collective-permute-start(bf16[128,640]{1,0:T(8,128)(2,1)S(1)} %bitcast.22), channel_id=1, source_target_pairs={{0,16},{1,17},{2,18},{3,19},{4,20},{5,21},{6,22},{7,23},{8,24},{9,... | collective-permute-start | bytes 491528 | tf_op jit(solution)/shard_map/ppermute | solution.py:232
  16.6 9.5 %all-to-all-done.near_ref = bf16[4,288,640]{2,1,0:T(8,128)(2,1)S(1)} async-done(((bf16[4,288,640]{2,1,0:T(8,128)(2,1)}), bf16[4,288,640]{2,1,0:T(8,128)(2,1)S(1)}, u32[]{:S(2)}, u32[]{:S(2)}) %all-to-all-start) | async-done | bytes 1474592 | tf_op jit(solution)/shard_map/all_to_all | solution.py:21
  26.1 9.7 %collective-permute-start.1 = (bf16[4,288,640]{2,1,0:T(8,128)(2,1)S(1)}, bf16[4,288,640]{2,1,0:T(8,128)(2,1)S(1)}, u32[]{:S(2)}, u32[]{:S(2)}) collective-permute-start(bf16[4,288,640]{2,1,0:T(8,128)(2,1)S(1)} %all-to-all-done.near_ref), channel_id=1, source_target_pairs={{0,1},{1,0},{2,3},{3,2},{4,5},{5,4},{6,7},{7,6},{8,9},{9,8},{10,11... | collective-permute-start | bytes 4423688 | tf_op jit(solution)/shard_map/ppermute | solution.py:252
  35.9 12.0 %collective-permute-start.4 = (bf16[128,640]{1,0:T(8,128)(2,1)S(1)}, bf16[128,640]{1,0:T(8,128)(2,1)S(1)}, u32[]{:S(2)}, u32[]{:S(2)}) collective-permute-start(bf16[128,640]{1,0:T(8,128)(2,1)S(1)} %bitcast_select_fusion), channel_id=1, source_target_pairs={{0,416},{1,417},{2,418},{3,419},{4,420},{5,421},{6,422},{7,423},{8... | collective-permute-start | bytes 491528 | tf_op jit(solution)/shard_map/ppermute | solution.py:233
  47.9 2.0 %collective-permute-start.3 = (bf16[128,640]{1,0:T(8,128)(2,1)S(1)}, bf16[128,640]{1,0:T(8,128)(2,1)}, u32[]{:S(2)}, u32[]{:S(2)}) collective-permute-start(bf16[128,640]{1,0:T(8,128)(2,1)S(1)} %bitcast_select_fusion), channel_id=1, source_target_pairs={{0,96},{1,97},{2,98},{3,99},{4,100},{5,101},{6,102},{7,103},{8,104... | collective-permute-start | bytes 491528 | tf_op jit(solution)/shard_map/ppermute | solution.py:233
  49.9 1.6 %collective-permute-done.4 = bf16[128,640]{1,0:T(8,128)(2,1)S(1)} collective-permute-done((bf16[128,640]{1,0:T(8,128)(2,1)S(1)}, bf16[128,640]{1,0:T(8,128)(2,1)S(1)}, u32[]{:S(2)}, u32[]{:S(2)}) %collective-permute-start.4) | collective-permute-done | bytes 163872 | tf_op jit(solution)/shard_map/ppermute | solution.py:233
  51.4 1.3 collective-permute-done.3
  52.7 1.0 add_select_fusion.1
  53.7 0.7 collective-permute-start.5
  54.4 1.3 collective-permute-start.8
  55.7 1.3 collective-permute-start.7
  57.0 1.3 collective-permute-start.6
  58.4 0.3 collective-permute-done.8
  58.7 1.3 collective-permute-done.7
  60.0 0.7 copy-done.2
  60.6 1.1 add_select_fusion.refs_0_
  61.7 4.6 %collective-permute-start.11 = (bf16[128,640]{1,0:T(8,128)(2,1)S(1)}, bf16[128,640]{1,0:T(8,128)(2,1)S(1)}, u32[]{:S(2)}, u32[]{:S(2)}) collective-permute-start(bf16[128,640]{1,0:T(8,128)(2,1)S(1)} %add_select_fusion.refs_0_), channel_id=1, source_target_pairs={{0,24},{8,16},{16,8},{24,0},{1,25},{9,17},{17,9},{25,1},{2,26},{10... | collective-permute-start | bytes 491528 | tf_op jit(solution)/shard_map/ppermute | solution.py:249
  66.4 2.3 %collective-permute-start.10 = (bf16[128,640]{1,0:T(8,128)(2,1)S(1)}, bf16[128,640]{1,0:T(8,128)(2,1)S(1)}, u32[]{:S(2)}, u32[]{:S(2)}) collective-permute-start(bf16[128,640]{1,0:T(8,128)(2,1)S(1)} %add_select_fusion.refs_0_), channel_id=1, source_target_pairs={{0,8},{8,0},{16,24},{24,16},{1,9},{9,1},{17,25},{25,17},{2,10},{10... | collective-permute-start | bytes 491528 | tf_op jit(solution)/shard_map/ppermute | solution.py:249
  68.6 2.1 %collective-permute-start.9 = (bf16[128,640]{1,0:T(8,128)(2,1)S(1)}, bf16[128,640]{1,0:T(8,128)(2,1)}, u32[]{:S(2)}, u32[]{:S(2)}) collective-permute-start(bf16[128,640]{1,0:T(8,128)(2,1)S(1)} %add_select_fusion.refs_0_), channel_id=1, source_target_pairs={{0,16},{8,24},{16,0},{24,8},{1,17},{9,25},{17,1},{25,9},{2,18},{10... | collective-permute-start | bytes 491528 | tf_op jit(solution)/shard_map/ppermute | solution.py:249
  70.9 3.1 %collective-permute-done.10.refs_2_ = bf16[128,640]{1,0:T(8,128)(2,1)S(1)} collective-permute-done((bf16[128,640]{1,0:T(8,128)(2,1)S(1)}, bf16[128,640]{1,0:T(8,128)(2,1)S(1)}, u32[]{:S(2)}, u32[]{:S(2)}) %collective-permute-start.10) | collective-permute-done | bytes 163872 | tf_op jit(solution)/shard_map/ppermute | solution.py:249
  73.9 1.9 %collective-permute-done.9.refs_1_ = bf16[128,640]{1,0:T(8,128)(2,1)} collective-permute-done((bf16[128,640]{1,0:T(8,128)(2,1)S(1)}, bf16[128,640]{1,0:T(8,128)(2,1)}, u32[]{:S(2)}, u32[]{:S(2)}) %collective-permute-start.9) | collective-permute-done | bytes 163872 | tf_op jit(solution)/shard_map/ppermute | solution.py:249
  75.8 4.0 %shard_map.46 = bf16[32,4,1024]{2,1,0:T(4,128)(2,1)S(1)} custom-call(s32[3]{0:T(128)S(1)} %pad_add_fusion.place_ref, bf16[4,288,640]{2,1,0:T(8,128)(2,1)S(1)} %all-to-all-done.near_ref, bf16[4,288,640]{2,1,0:T(8,128)(2,1)S(1)} %collective-permute-done.1.far_ref, bf16[128,640]{1,0:T(8,128)(2,1)S(1)} %add_select_fusion.refs_0_, ...), custom_call_target="tpu_custom_call" | custom-call | flops 1509949440 | bytes 2949120 | tf_op jit(solution)/shard_map/pallas_call | solution.py:93
  79.8 39.2 %all_to_all.15.parts_ref = bf16[32,4,1024]{2,1,0:T(4,128)(2,1)S(1)} all-to-all(bf16[32,4,1024]{2,1,0:T(4,128)(2,1)S(1)} %shard_map.46), channel_id=1, replica_groups=mesh['z'=16,'yl'=2,'yh'=2,'x'=4,'core'=2] {'z','yl'}, dimensions={0} | all-to-all | bytes 524288 | tf_op jit(solution)/shard_map/all_to_all | solution.py:21
  119.0 0.8 shard_map.47
  119.8 9.8 %all-to-all-start.2 = ((f32[16,4,1024]{2,1,0:T(4,128)}), f32[16,4,1024]{2,1,0:T(4,128)S(1)}, u32[]{:S(2)}, u32[]{:S(2)}) async-start(f32[16,4,1024]{2,1,0:T(4,128)} %shard_map.47), calls=%async_computation.2 | async-start | bytes 524288 | tf_op jit(solution)/shard_map/all_to_all | solution.py:21
  129.9 8.4 %all-to-all-done.2.every_ref = f32[16,4,1024]{2,1,0:T(4,128)S(1)} async-done(((f32[16,4,1024]{2,1,0:T(4,128)}), f32[16,4,1024]{2,1,0:T(4,128)S(1)}, u32[]{:S(2)}, u32[]{:S(2)}) %all-to-all-start.2) | async-done | bytes 262176 | tf_op jit(solution)/shard_map/all_to_all | solution.py:21
  138.3 1.6 %shard_map.48 = f32[4,4,256]{2,1,0:T(4,128)} custom-call(s32[4,2]{1,0:T(4,128)S(1)} %copy.9.pairs_ref, s32[4]{0:T(128)S(1)} %dynamic-slice_subtract_fusion.swap_ref, f32[16,4,1024]{2,1,0:T(4,128)S(1)} %all-to-all-done.2.every_ref), custom_call_target="tpu_custom_call" | custom-call | flops 6553600 | bytes 262144 | tf_op jit(solution)/shard_map/pallas_call | solution.py:199
  (21 shorter events, 0.7 us)
Async XLA Ops:
  0.0 129.6 %copy-start = (s32[64,2]{0,1:T(2,128)S(1)}, s32[64,2]{0,1:T(2,128)}, u32[]{:S(2)}) copy-start(s32[64,2]{0,1:T(2,128)} %param.7) | copy-start | bytes 1540
  0.0 7.1 %collective-permute-start = (bf16[8,1024]{1,0:T(8,128)(2,1)}, bf16[8,1024]{1,0:T(8,128)(2,1)S(1)}, u32[]{:S(2)}, u32[]{:S(2)}) collective-permute-start(bf16[8,1024]{1,0:T(8,128)(2,1)} %param.6), channel_id=1, source_target_pairs={{0,8},{8,0},{1,9},{9,1},{2,10},{10,2},{3,11},{11,3},{4,12},{12,4},... | collective-permute-start | bytes 49160 | tf_op jit(solution)/shard_map/ppermute | solution.py:221
  9.1 4.2 %copy-start.1 = (bf16[8,32,640]{2,1,0:T(8,128)(2,1)S(1)}, bf16[8,32,640]{2,1,0:T(8,128)(2,1)}, u32[]{:S(2)}) copy-start(bf16[8,32,640]{2,1,0:T(8,128)(2,1)} %param.5) | copy-start | bytes 983044
  9.1 17.0 %all-to-all-start = ((bf16[4,288,640]{2,1,0:T(8,128)(2,1)}), bf16[4,288,640]{2,1,0:T(8,128)(2,1)S(1)}, u32[]{:S(2)}, u32[]{:S(2)}) async-start(bf16[4,288,640]{2,1,0:T(8,128)(2,1)} %broadcast_in_dim.8), calls=%async_computation | async-start | bytes 2949120 | tf_op jit(solution)/shard_map/all_to_all | solution.py:21
  13.3 22.5 %collective-permute-start.2 = (bf16[128,640]{1,0:T(8,128)(2,1)S(1)}, bf16[128,640]{1,0:T(8,128)(2,1)S(1)}, u32[]{:S(2)}, u32[]{:S(2)}) collective-permute-start(bf16[128,640]{1,0:T(8,128)(2,1)S(1)} %bitcast.22), channel_id=1, source_target_pairs={{0,16},{1,17},{2,18},{3,19},{4,20},{5,21},{6,22},{7,23},{8,24},{9,... | collective-permute-start | bytes 491528 | tf_op jit(solution)/shard_map/ppermute | solution.py:232
  26.1 49.7 %collective-permute-start.1 = (bf16[4,288,640]{2,1,0:T(8,128)(2,1)S(1)}, bf16[4,288,640]{2,1,0:T(8,128)(2,1)S(1)}, u32[]{:S(2)}, u32[]{:S(2)}) collective-permute-start(bf16[4,288,640]{2,1,0:T(8,128)(2,1)S(1)} %all-to-all-done.near_ref), channel_id=1, source_target_pairs={{0,1},{1,0},{2,3},{3,2},{4,5},{5,4},{6,7},{7,6},{8,9},{9,8},{10,11... | collective-permute-start | bytes 4423688 | tf_op jit(solution)/shard_map/ppermute | solution.py:252
  35.9 15.5 %collective-permute-start.4 = (bf16[128,640]{1,0:T(8,128)(2,1)S(1)}, bf16[128,640]{1,0:T(8,128)(2,1)S(1)}, u32[]{:S(2)}, u32[]{:S(2)}) collective-permute-start(bf16[128,640]{1,0:T(8,128)(2,1)S(1)} %bitcast_select_fusion), channel_id=1, source_target_pairs={{0,416},{1,417},{2,418},{3,419},{4,420},{5,421},{6,422},{7,423},{8... | collective-permute-start | bytes 491528 | tf_op jit(solution)/shard_map/ppermute | solution.py:233
  47.9 4.8 %collective-permute-start.3 = (bf16[128,640]{1,0:T(8,128)(2,1)S(1)}, bf16[128,640]{1,0:T(8,128)(2,1)}, u32[]{:S(2)}, u32[]{:S(2)}) collective-permute-start(bf16[128,640]{1,0:T(8,128)(2,1)S(1)} %bitcast_select_fusion), channel_id=1, source_target_pairs={{0,96},{1,97},{2,98},{3,99},{4,100},{5,101},{6,102},{7,103},{8,104... | collective-permute-start | bytes 491528 | tf_op jit(solution)/shard_map/ppermute | solution.py:233
  53.7 0.7 collective-permute-start.5
  54.4 4.2 %collective-permute-start.8 = (bf16[128,640]{1,0:T(8,128)(2,1)S(1)}, bf16[128,640]{1,0:T(8,128)(2,1)S(1)}, u32[]{:S(2)}, u32[]{:S(2)}) collective-permute-start(bf16[128,640]{1,0:T(8,128)(2,1)S(1)} %broadcast_select_fusion), channel_id=1, source_target_pairs={{96,64},{192,160},{320,288},{416,384},{0,480},{97,65},{193,161},{3... | collective-permute-start | bytes 491528 | tf_op jit(solution)/shard_map/ppermute | solution.py:245
  55.7 4.2 %collective-permute-start.7 = (bf16[128,640]{1,0:T(8,128)(2,1)S(1)}, bf16[128,640]{1,0:T(8,128)(2,1)S(1)}, u32[]{:S(2)}, u32[]{:S(2)}) collective-permute-start(bf16[128,640]{1,0:T(8,128)(2,1)S(1)} %broadcast_select_fusion), channel_id=1, source_target_pairs={{0,32},{96,128},{192,224},{320,352},{416,448},{1,33},{97,129},{193... | collective-permute-start | bytes 491528 | tf_op jit(solution)/shard_map/ppermute | solution.py:245
  57.0 3.6 %collective-permute-start.6 = (bf16[128,640]{1,0:T(8,128)(2,1)S(1)}, bf16[128,640]{1,0:T(8,128)(2,1)}, u32[]{:S(2)}, u32[]{:S(2)}) collective-permute-start(bf16[128,640]{1,0:T(8,128)(2,1)S(1)} %broadcast_select_fusion), channel_id=1, source_target_pairs={{192,256},{193,257},{194,258},{195,259},{196,260},{197,261},{198,2... | collective-permute-start | bytes 491528 | tf_op jit(solution)/shard_map/ppermute | solution.py:244
  60.0 0.7 copy-start.2
  61.7 9.2 %collective-permute-start.11 = (bf16[128,640]{1,0:T(8,128)(2,1)S(1)}, bf16[128,640]{1,0:T(8,128)(2,1)S(1)}, u32[]{:S(2)}, u32[]{:S(2)}) collective-permute-start(bf16[128,640]{1,0:T(8,128)(2,1)S(1)} %add_select_fusion.refs_0_), channel_id=1, source_target_pairs={{0,24},{8,16},{16,8},{24,0},{1,25},{9,17},{17,9},{25,1},{2,26},{10... | collective-permute-start | bytes 491528 | tf_op jit(solution)/shard_map/ppermute | solution.py:249
  66.4 7.6 %collective-permute-start.10 = (bf16[128,640]{1,0:T(8,128)(2,1)S(1)}, bf16[128,640]{1,0:T(8,128)(2,1)S(1)}, u32[]{:S(2)}, u32[]{:S(2)}) collective-permute-start(bf16[128,640]{1,0:T(8,128)(2,1)S(1)} %add_select_fusion.refs_0_), channel_id=1, source_target_pairs={{0,8},{8,0},{16,24},{24,16},{1,9},{9,1},{17,25},{25,17},{2,10},{10... | collective-permute-start | bytes 491528 | tf_op jit(solution)/shard_map/ppermute | solution.py:249
  68.6 7.2 %collective-permute-start.9 = (bf16[128,640]{1,0:T(8,128)(2,1)S(1)}, bf16[128,640]{1,0:T(8,128)(2,1)}, u32[]{:S(2)}, u32[]{:S(2)}) collective-permute-start(bf16[128,640]{1,0:T(8,128)(2,1)S(1)} %add_select_fusion.refs_0_), channel_id=1, source_target_pairs={{0,16},{8,24},{16,0},{24,8},{1,17},{9,25},{17,1},{25,9},{2,18},{10... | collective-permute-start | bytes 491528 | tf_op jit(solution)/shard_map/ppermute | solution.py:249
  79.8 50.0 %copy-start.3 = (s32[128]{0:T(128)S(1)}, s32[128]{0:T(128)}, u32[]{:S(2)}) copy-start(s32[128]{0:T(128)} %param.8) | copy-start | bytes 1540
  119.8 18.5 %all-to-all-start.2 = ((f32[16,4,1024]{2,1,0:T(4,128)}), f32[16,4,1024]{2,1,0:T(4,128)S(1)}, u32[]{:S(2)}, u32[]{:S(2)}) async-start(f32[16,4,1024]{2,1,0:T(4,128)} %shard_map.47), calls=%async_computation.2 | async-start | bytes 524288 | tf_op jit(solution)/shard_map/all_to_all | solution.py:21

commit v6 on v5

--- a/solution.py
+++ b/solution.py
@@ -26,22 +26,18 @@
     return exchange(jnp.broadcast_to(array[None], (count, *array.shape)), axes)
 
 
-def ladder_kernel(place_ref, near_ref, far_ref, *refs):
-    *quarter_refs, out_ref, stack_ref, right_ref = refs
-    core, yh, own = place_ref[0], place_ref[1], place_ref[2]
-    size = quarter_refs[0].shape[0]
-    for q, ref in enumerate(quarter_refs):
-        right_ref[pl.ds(pl.multiple_of((own ^ q) * size, size), size), :] = ref[...]
+def ladder_kernel(place_ref, near_ref, far_ref, amps_ref, right_ref, out_ref, stack_ref):
     b_count, depth, _ = stack_ref.shape
     ring, pair_rows = near_ref.shape[0], b_count
-    c_pairs = near_ref.shape[1] // pair_rows - 2
+    c_pairs = near_ref.shape[1] // pair_rows
     a_dev = pair_rows // 2
+    order = [lax.rem(place_ref[0] + ring - x, ring) for x in range(ring)]
     d_count = right_ref.shape[0] // b_count
     right = right_ref[...]
     for n in range(0, c_pairs, 2):
         left = jnp.concatenate(
             [
-                ref[x, m * pair_rows : (m + 1) * pair_rows, :]
+                ref[order[x], m * pair_rows : (m + 1) * pair_rows, :]
                 for m in (n, n + 1)
                 for x in range(ring)
                 for ref in (near_ref, far_ref)
@@ -55,57 +51,41 @@
         for h in range(2):
             rows = (n + h) * d_count
             stack_ref[:, rows : rows + d_count, :] = part[:, :, h * LANES : (h + 1) * LANES]
-    amps = jnp.concatenate(
-        [
-            ref[x, m * pair_rows : (m + 1) * pair_rows, :depth]
-            for m in (c_pairs, c_pairs + 1)
-            for ref in (near_ref, far_ref)
-            for x in range(ring)
-        ],
-        axis=0,
-    )
-    blocks = 4 * ring
-    odd = lax.rem(lax.broadcasted_iota(jnp.int32, (1, 1, LANES), 2) // a_dev, 2) == 1
+    i_count = amps_ref.shape[0]
+    amps = jnp.concatenate([amps_ref[:, :depth], amps_ref[:, depth:]], axis=0)
+    odd = lax.rem(lax.broadcasted_iota(jnp.int32, (1, LANES), 1) // a_dev, 2) == 1
+    rows = out_ref.shape[1]
     for q in range(b_count // 2):
         sums = []
         for b, step in ((2 * q, LANES - a_dev), (2 * q + 1, a_dev)):
             full = jnp.dot(amps, stack_ref[b], preferred_element_type=jnp.float32)
-            full = full.reshape(blocks, 2, a_dev, LANES)
-            mixed = jnp.where(odd, full[:, 1], full[:, 0]).reshape(blocks * a_dev, LANES)
+            mixed = jnp.where(odd, full[i_count:], full[:i_count])
             sums.append(mixed + pltpu.roll(mixed, step, 1))
-        found = jnp.where(odd[0], sums[1], sums[0]).astype(out_ref.dtype)
-        for block in range(blocks):
-            other_yh, other_core, x = block // (2 * ring), block // ring % 2, block % ring
-            place = (lax.rem(yh + other_yh, 2) * ring + x) * 2 + lax.rem(core + other_core, 2)
-            for h in range(2):
-                rows = found[block * a_dev + h * (a_dev // 2) : block * a_dev + (h + 1) * (a_dev // 2)]
-                out_ref[2 * place + h, :, q * LANES : (q + 1) * LANES] = rows
+        found = jnp.where(odd, sums[1], sums[0]).astype(out_ref.dtype)
+        for k in range(out_ref.shape[0]):
+            out_ref[k, :, q * LANES : (q + 1) * LANES] = found[k * rows : (k + 1) * rows]
 
 
 def in_vmem(count):
     return [pl.BlockSpec(memory_space=pltpu.VMEM)] * count
 
 
-def ladder_partials(place, near, far, quarters, b_count, i_count, con_count):
-    right = (len(quarters) * quarters[0].shape[0], quarters[0].shape[1])
-    depth = (near.shape[1] // b_count - 2) * (right[0] // b_count)
-    pairs = 2 * near.size * right[0]
+def ladder_partials(place, near, far, amps, right, b_count, con_count):
+    i_count = amps.shape[0]
+    pairs = 2 * near.size * right.shape[0]
     return pl.pallas_call(
         ladder_kernel,
         out_shape=jax.ShapeDtypeStruct(
             (con_count, i_count // con_count, b_count * LANES // 2), jnp.bfloat16
         ),
-        in_specs=[pl.BlockSpec(memory_space=pltpu.SMEM)] + in_vmem(2 + len(quarters)),
+        in_specs=[pl.BlockSpec(memory_space=pltpu.SMEM)] + in_vmem(4),
         out_specs=pl.BlockSpec(memory_space=pltpu.VMEM),
-        scratch_shapes=[
-            pltpu.VMEM((b_count, depth, LANES), jnp.bfloat16),
-            pltpu.VMEM(right, jnp.bfloat16),
-        ],
+        scratch_shapes=[pltpu.VMEM((b_count, amps.shape[1] // 2, LANES), jnp.bfloat16)],
         compiler_params=pltpu.CompilerParams(vmem_limit_bytes=12 * 1024 * 1024),
         cost_estimate=pl.CostEstimate(
             flops=2 * pairs, bytes_accessed=4 * near.size, transcendentals=0
         ),
-    )(place, near, far, *quarters)
+    )(place, near, far, amps, right)
 
 
 def total_kernel(parts_ref, out_ref):
@@ -213,20 +193,18 @@
     con_count = lax.axis_size(CONTRACT)
     ring = lax.axis_size("x")
     a_dev, c_dev, p_size = chol.shape
-    i_dev = amplitudes.shape[0]
-    i_count = i_dev * out_count
+    i_count = amplitudes.shape[0] * out_count
     half = c_dev // 2
-    pair_rows = 2 * a_dev
-
-    other_amps = lax.ppermute(amplitudes, "yh", PAIR)
+
     rows = jnp.transpose(chol.reshape(a_dev, 2, half, p_size), (2, 1, 0, 3))
-    extra = jnp.stack([amplitudes, other_amps], axis=0).reshape(2, i_dev, 2, -1)
-    extra = jnp.transpose(extra, (0, 2, 1, 3)).reshape(2, pair_rows, -1)
-    extra = jnp.pad(extra, ((0, 0), (0, 0), (0, p_size - extra.shape[2])))
-    packed = jnp.concatenate([rows.reshape(half, pair_rows, p_size), extra], axis=0)
-    near = sent_to_all(packed.reshape(-1, p_size), "x")
-
-    z, yl, yh = lax.axis_index("z"), lax.axis_index("yl"), lax.axis_index("yh")
+    rows = rows.reshape(-1, p_size)
+    near = [rows] + [
+        lax.ppermute(rows, "x", [(x, (x + shift) % ring) for x in range(ring)])
+        for shift in range(1, ring)
+    ]
+    amps = sent_to_all(amplitudes, OUT).reshape(i_count, -1)
+
+    z, yl = lax.axis_index("z"), lax.axis_index("yl")
     depth_z = lax.axis_size("z")
     window = chol.reshape(2, -1, p_size)
     piece = jnp.where(yl == 0, window[0], lax.ppermute(window[1], CONTRACT, [(0, 1)]))
@@ -245,13 +223,13 @@
     got = sum((lax.ppermute(piece, "z", reach[step]) for step in steps[1:]), got)
     sender = functools.reduce(jnp.logical_or, [z == at for at in SENDERS])
     piece = jnp.where(sender, piece, got)
-    quarters = [piece] + [
-        lax.ppermute(piece, ("yl", "yh"), [(at, at ^ q) for at in range(4)]) for q in (2, 1, 3)
-    ]
-
+    right = sent_to_all(piece, ("yh", "yl")).reshape(-1, p_size)
+
+    near = jnp.stack(near, axis=0)
     far = lax.ppermute(near, "core", PAIR)
-    place = jnp.stack([lax.axis_index("core"), yh, 2 * yh + yl])
-    partial = ladder_partials(place, near, far, quarters, 2 * a_dev, i_count, con_count)
+
+    place = lax.axis_index("x").reshape(1)
+    partial = ladder_partials(place, near, far, amps, right, 2 * a_dev, con_count)
     every = exchange(totals(exchange(partial, CONTRACT), out_count), OUT)
 
     slot_count, occ_dev = tile_pairs.shape[0] // out_count, i_count // con_count

time: 141 us -> 132 us (0.936)
  blocking collectives: 39.2 us -> 34 us
  starting transfers between devices: 60.4 us -> 55.7 us
  waiting for transfers between devices: 27.7 us -> 30.5 us
  other arithmetic: 2.99 us -> 1.33 us
    all_to_all x2 -> x3, waiting for transfers between devices: 18 us -> 26.4 us  [exchange(): return lax.all_to_all(array, axes, 0, 0, tiled=True)]
    ppermute x2, starting transfers between devices: 2.6 us -> 9.89 us  [on_device(): lax.ppermute(piece, 'z', reach[step])]
    ppermute x1, starting transfers between devices: 9.73 us -> 2.46 us  [on_device(): far = lax.ppermute(near, 'core', PAIR)]
    ppermute x4 -> x3, starting transfers between devices: 14.8 us -> 9.33 us  [on_device(): lax.ppermute(rows, 'x', [(x, (x + shift) % ring) for x in range(ring)])]
    all_to_all x1, blocking collectives: 39.2 us -> 34 us  [exchange(): return lax.all_to_all(array, axes, 0, 0, tiled=True)]
    ppermute x2, starting transfers between devices: 14 us -> 10.8 us  [on_device(): got = sum((lax.ppermute(piece, 'z', [hop]) for hop in LONG))]
    all_to_all x2 -> x3, starting transfers between devices: 14 us -> 17.2 us  [exchange(): return lax.all_to_all(array, axes, 0, 0, tiled=True)]
    ppermute x2, waiting for transfers between devices: 2.86 us -> 0.01 us  [on_device(): got = sum((lax.ppermute(piece, 'z', [hop]) for hop in LONG))]
  transfers between devices with their start and end apart: 14 -> 14, of which waited for: 9 -> 4; matrix products, arithmetic and copies ran while one was open for 3% -> 3% of each run, Pallas kernels for 0% -> 0%
where the time goes in v6:
time: 132 us; the launch traced here: 131 us
  starting transfers between devices  55.7 us (42%)
  blocking collectives  34 us (26%)
  waiting for transfers between devices  30.5 us (23%)
  Pallas kernels  5.41 us (4%)
  local copies, waits for them, and re-layouts  3.92 us (3%)
  other arithmetic  1.33 us (1%)
    all_to_all x1, blocking collectives, exchange(): return lax.all_to_all(array, axes, 0, 0, tiled=True)  34 us
    all_to_all x3, waiting for transfers between devices, exchange(): return lax.all_to_all(array, axes, 0, 0, tiled=True)  26.4 us
    all_to_all x3, starting transfers between devices, exchange(): return lax.all_to_all(array, axes, 0, 0, tiled=True)  17.2 us
    ppermute x2, starting transfers between devices, on_device(): got = sum((lax.ppermute(piece, 'z', [hop]) for hop in LONG))  10.8 us
    ppermute x2, starting transfers between devices, on_device(): lax.ppermute(piece, 'z', reach[step])  9.89 us
    ppermute x3, starting transfers between devices, on_device(): lax.ppermute(rows, 'x', [(x, (x + shift) % ring) for x in range(ring)])  9.33 us
    ppermute x3, waiting for transfers between devices, on_device(): lax.ppermute(rows, 'x', [(x, (x + shift) % ring) for x in range(ring)])  4.15 us
    ppermute x1, starting transfers between devices, on_device(): lax.ppermute(window[1], CONTRACT, [(0, 1)])  4.03 us
  transfers between devices with their start and end apart: 14, of which 4 were waited for; matrix products, arithmetic and copies ran while one was open for 3% of the time, Pallas kernels for 0%

profile of v6, /device:TPU:1, one launch (start us, length us, event | category | flops | bytes accessed | tf_op | source)
XLA Modules:
  0.0 131.1 jit_solution(3594825519219068046)
XLA Ops:
  0.0 1.0 fusion
  1.0 4.0 %collective-permute-start.4 = (bf16[128,640]{1,0:T(8,128)(2,1)S(1)}, bf16[128,640]{1,0:T(8,128)(2,1)S(1)}, u32[]{:S(2)}, u32[]{:S(2)}) collective-permute-start(bf16[128,640]{1,0:T(8,128)(2,1)S(1)} %bitcast.25), channel_id=1, source_target_pairs={{0,16},{1,17},{2,18},{3,19},{4,20},{5,21},{6,22},{7,23},{8,24},{9,... | collective-permute-start | bytes 491528 | tf_op jit(solution)/shard_map/ppermute | solution.py:210
  5.1 1.1 copy.6
  6.2 4.4 %collective-permute-start.2 = (bf16[256,640]{1,0:T(8,128)(2,1)S(1)}, bf16[256,640]{1,0:T(8,128)(2,1)S(1)}, u32[]{:S(2)}, u32[]{:S(2)}) collective-permute-start(bf16[256,640]{1,0:T(8,128)(2,1)S(1)} %bitcast.17), channel_id=1, source_target_pairs={{0,6},{2,0},{4,2},{6,4},{1,7},{3,1},{5,3},{7,5},{8,14},{10,8},{12,... | collective-permute-start | bytes 983048 | tf_op jit(solution)/shard_map/ppermute | solution.py:202
  10.6 2.4 %collective-permute-start.1 = (bf16[256,640]{1,0:T(8,128)(2,1)S(1)}, bf16[256,640]{1,0:T(8,128)(2,1)S(1)}, u32[]{:S(2)}, u32[]{:S(2)}) collective-permute-start(bf16[256,640]{1,0:T(8,128)(2,1)S(1)} %bitcast.18), channel_id=1, source_target_pairs={{0,4},{2,6},{4,0},{6,2},{1,5},{3,7},{5,1},{7,3},{8,12},{10,14},{12... | collective-permute-start | bytes 983048 | tf_op jit(solution)/shard_map/ppermute | solution.py:202
  13.0 2.5 %collective-permute-start = (bf16[256,640]{1,0:T(8,128)(2,1)S(1)}, bf16[256,640]{1,0:T(8,128)(2,1)S(1)}, u32[]{:S(2)}, u32[]{:S(2)}) collective-permute-start(bf16[256,640]{1,0:T(8,128)(2,1)S(1)} %bitcast.19), channel_id=1, source_target_pairs={{0,2},{2,4},{4,6},{6,0},{1,3},{3,5},{5,7},{7,1},{8,10},{10,12},{12... | collective-permute-start | bytes 983048 | tf_op jit(solution)/shard_map/ppermute | solution.py:202
  15.6 9.5 %collective-permute-start.6 = (bf16[128,640]{1,0:T(8,128)(2,1)S(1)}, bf16[128,640]{1,0:T(8,128)(2,1)S(1)}, u32[]{:S(2)}, u32[]{:S(2)}) collective-permute-start(bf16[128,640]{1,0:T(8,128)(2,1)S(1)} %bitcast_select_fusion), channel_id=1, source_target_pairs={{0,416},{1,417},{2,418},{3,419},{4,420},{5,421},{6,422},{7,423},{8... | collective-permute-start | bytes 491528 | tf_op jit(solution)/shard_map/ppermute | solution.py:211
  25.1 1.3 collective-permute-start.5
  26.4 4.1 %collective-permute-done = bf16[256,640]{1,0:T(8,128)(2,1)S(1)} collective-permute-done((bf16[256,640]{1,0:T(8,128)(2,1)S(1)}, bf16[256,640]{1,0:T(8,128)(2,1)S(1)}, u32[]{:S(2)}, u32[]{:S(2)}) %collective-permute-start) | collective-permute-done | bytes 327712 | tf_op jit(solution)/shard_map/ppermute | solution.py:202
  30.5 0.2 pad_maximum_fusion.near_ref
  30.7 2.5 %collective-permute-start.3 = (bf16[4,256,640]{2,1,0:T(8,128)(2,1)S(1)}, bf16[4,256,640]{2,1,0:T(8,128)(2,1)S(1)}, u32[]{:S(2)}, u32[]{:S(2)}) collective-permute-start(bf16[4,256,640]{2,1,0:T(8,128)(2,1)S(1)} %pad_maximum_fusion.near_ref), channel_id=1, source_target_pairs={{0,1},{1,0},{2,3},{3,2},{4,5},{5,4},{6,7},{7,6},{8,9},{9,8},{10,11... | collective-permute-start | bytes 3932168 | tf_op jit(solution)/shard_map/ppermute | solution.py:229
  33.3 0.7 collective-permute-start.7
  34.0 8.6 %collective-permute-start.10 = (bf16[128,640]{1,0:T(8,128)(2,1)S(1)}, bf16[128,640]{1,0:T(8,128)(2,1)S(1)}, u32[]{:S(2)}, u32[]{:S(2)}) collective-permute-start(bf16[128,640]{1,0:T(8,128)(2,1)S(1)} %broadcast_select_fusion), channel_id=1, source_target_pairs={{96,64},{192,160},{320,288},{416,384},{0,480},{97,65},{193,161},{3... | collective-permute-start | bytes 491528 | tf_op jit(solution)/shard_map/ppermute | solution.py:223
  42.6 1.3 collective-permute-start.9
  43.9 1.3 %collective-permute-start.8 = (bf16[128,640]{1,0:T(8,128)(2,1)S(1)}, bf16[128,640]{1,0:T(8,128)(2,1)}, u32[]{:S(2)}, u32[]{:S(2)}) collective-permute-start(bf16[128,640]{1,0:T(8,128)(2,1)S(1)} %broadcast_select_fusion), channel_id=1, source_target_pairs={{192,256},{193,257},{194,258},{195,259},{196,260},{197,261},{198,2... | collective-permute-start | bytes 491528 | tf_op jit(solution)/shard_map/ppermute | solution.py:222
  45.3 0.7 broadcast_in_dim.4
  46.0 5.0 %all-to-all-start = ((bf16[16,8,1024]{2,1,0:T(8,128)(2,1)}), bf16[16,8,1024]{2,1,0:T(8,128)(2,1)S(1)}, u32[]{:S(2)}, u32[]{:S(2)}) async-start(bf16[16,8,1024]{2,1,0:T(8,128)(2,1)} %broadcast_in_dim.4), calls=%async_computation | async-start | bytes 524288 | tf_op jit(solution)/shard_map/all_to_all | solution.py:21
  51.0 1.0 add_select_fusion
  52.0 7.7 %all-to-all-done = bf16[16,8,1024]{2,1,0:T(8,128)(2,1)S(1)} async-done(((bf16[16,8,1024]{2,1,0:T(8,128)(2,1)}), bf16[16,8,1024]{2,1,0:T(8,128)(2,1)S(1)}, u32[]{:S(2)}, u32[]{:S(2)}) %all-to-all-start) | async-done | bytes 262176 | tf_op jit(solution)/shard_map/all_to_all | solution.py:21
  59.7 0.9 broadcast_in_dim.5
  60.6 3.5 %all-to-all-start.1 = ((bf16[4,128,640]{2,1,0:T(8,128)(2,1)}), bf16[4,128,640]{2,1,0:T(8,128)(2,1)S(1)}, u32[]{:S(2)}, u32[]{:S(2)}) async-start(bf16[4,128,640]{2,1,0:T(8,128)(2,1)} %broadcast_in_dim.5), calls=%async_computation.1 | async-start | bytes 1310720 | tf_op jit(solution)/shard_map/all_to_all | solution.py:21
  64.1 10.2 %all-to-all-done.1 = bf16[4,128,640]{2,1,0:T(8,128)(2,1)S(1)} async-done(((bf16[4,128,640]{2,1,0:T(8,128)(2,1)}), bf16[4,128,640]{2,1,0:T(8,128)(2,1)S(1)}, u32[]{:S(2)}, u32[]{:S(2)}) %all-to-all-start.1) | async-done | bytes 655392 | tf_op jit(solution)/shard_map/all_to_all | solution.py:21
  74.3 3.0 %shard_map.46 = bf16[32,4,1024]{2,1,0:T(4,128)(2,1)S(1)} custom-call(s32[1]{0:T(128)} %bitcast.place_ref, bf16[4,256,640]{2,1,0:T(8,128)(2,1)S(1)} %pad_maximum_fusion.near_ref, bf16[4,256,640]{2,1,0:T(8,128)(2,1)S(1)} %collective-permute-done.3.far_ref, bf16[128,1024]{1,0:T(8,128)(2,1)S(1)} %bitcast.16, bf16[512,640]{1,0:T(8,128)(2,1)S(1)} %bitcast.15), custom_call_target="tpu_custom_call" | custom-call | flops 1342177280 | bytes 2621440 | tf_op jit(solution)/shard_map/pallas_call | solution.py:76
  77.3 0.0 copy-start.2
  77.3 34.0 %all_to_all.20.parts_ref = bf16[32,4,1024]{2,1,0:T(4,128)(2,1)S(1)} all-to-all(bf16[32,4,1024]{2,1,0:T(4,128)(2,1)S(1)} %shard_map.46), channel_id=1, replica_groups=mesh['z'=16,'yl'=2,'yh'=2,'x'=4,'core'=2] {'z','yl'}, dimensions={0} | all-to-all | bytes 524288 | tf_op jit(solution)/shard_map/all_to_all | solution.py:21
  111.3 0.8 shard_map.47
  112.0 8.7 %all-to-all-start.3 = ((f32[16,4,1024]{2,1,0:T(4,128)}), f32[16,4,1024]{2,1,0:T(4,128)S(1)}, u32[]{:S(2)}, u32[]{:S(2)}) async-start(f32[16,4,1024]{2,1,0:T(4,128)} %shard_map.47), calls=%async_computation.3 | async-start | bytes 524288 | tf_op jit(solution)/shard_map/all_to_all | solution.py:21
  120.8 0.1 constant_dynamic-slice_fusion
  120.8 0.1 copy.7.pairs_ref
  120.9 0.1 dynamic-slice_subtract_fusion.swap_ref
  121.0 8.4 %all-to-all-done.3.every_ref = f32[16,4,1024]{2,1,0:T(4,128)S(1)} async-done(((f32[16,4,1024]{2,1,0:T(4,128)}), f32[16,4,1024]{2,1,0:T(4,128)S(1)}, u32[]{:S(2)}, u32[]{:S(2)}) %all-to-all-start.3) | async-done | bytes 262176 | tf_op jit(solution)/shard_map/all_to_all | solution.py:21
  129.5 1.6 %shard_map.48 = f32[4,4,256]{2,1,0:T(4,128)} custom-call(s32[4,2]{1,0:T(4,128)S(1)} %copy.7.pairs_ref, s32[4]{0:T(128)S(1)} %dynamic-slice_subtract_fusion.swap_ref, f32[16,4,1024]{2,1,0:T(4,128)S(1)} %all-to-all-done.3.every_ref), custom_call_target="tpu_custom_call" | custom-call | flops 6553600 | bytes 262144 | tf_op jit(solution)/shard_map/pallas_call | solution.py:179
  (18 shorter events, 0.1 us)
Async XLA Ops:
  0.0 120.8 %copy-start = (s32[64,2]{0,1:T(2,128)S(1)}, s32[64,2]{0,1:T(2,128)}, u32[]{:S(2)}) copy-start(s32[64,2]{0,1:T(2,128)} %param.7) | copy-start | bytes 1540
  1.0 14.5 %collective-permute-start.4 = (bf16[128,640]{1,0:T(8,128)(2,1)S(1)}, bf16[128,640]{1,0:T(8,128)(2,1)S(1)}, u32[]{:S(2)}, u32[]{:S(2)}) collective-permute-start(bf16[128,640]{1,0:T(8,128)(2,1)S(1)} %bitcast.25), channel_id=1, source_target_pairs={{0,16},{1,17},{2,18},{3,19},{4,20},{5,21},{6,22},{7,23},{8,24},{9,... | collective-permute-start | bytes 491528 | tf_op jit(solution)/shard_map/ppermute | solution.py:210
  6.2 20.2 %collective-permute-start.2 = (bf16[256,640]{1,0:T(8,128)(2,1)S(1)}, bf16[256,640]{1,0:T(8,128)(2,1)S(1)}, u32[]{:S(2)}, u32[]{:S(2)}) collective-permute-start(bf16[256,640]{1,0:T(8,128)(2,1)S(1)} %bitcast.17), channel_id=1, source_target_pairs={{0,6},{2,0},{4,2},{6,4},{1,7},{3,1},{5,3},{7,5},{8,14},{10,8},{12,... | collective-permute-start | bytes 983048 | tf_op jit(solution)/shard_map/ppermute | solution.py:202
  10.6 15.8 %collective-permute-start.1 = (bf16[256,640]{1,0:T(8,128)(2,1)S(1)}, bf16[256,640]{1,0:T(8,128)(2,1)S(1)}, u32[]{:S(2)}, u32[]{:S(2)}) collective-permute-start(bf16[256,640]{1,0:T(8,128)(2,1)S(1)} %bitcast.18), channel_id=1, source_target_pairs={{0,4},{2,6},{4,0},{6,2},{1,5},{3,7},{5,1},{7,3},{8,12},{10,14},{12... | collective-permute-start | bytes 983048 | tf_op jit(solution)/shard_map/ppermute | solution.py:202
  13.0 17.6 %collective-permute-start = (bf16[256,640]{1,0:T(8,128)(2,1)S(1)}, bf16[256,640]{1,0:T(8,128)(2,1)S(1)}, u32[]{:S(2)}, u32[]{:S(2)}) collective-permute-start(bf16[256,640]{1,0:T(8,128)(2,1)S(1)} %bitcast.19), channel_id=1, source_target_pairs={{0,2},{2,4},{4,6},{6,0},{1,3},{3,5},{5,7},{7,1},{8,10},{10,12},{12... | collective-permute-start | bytes 983048 | tf_op jit(solution)/shard_map/ppermute | solution.py:202
  15.6 17.6 %collective-permute-start.6 = (bf16[128,640]{1,0:T(8,128)(2,1)S(1)}, bf16[128,640]{1,0:T(8,128)(2,1)S(1)}, u32[]{:S(2)}, u32[]{:S(2)}) collective-permute-start(bf16[128,640]{1,0:T(8,128)(2,1)S(1)} %bitcast_select_fusion), channel_id=1, source_target_pairs={{0,416},{1,417},{2,418},{3,419},{4,420},{5,421},{6,422},{7,423},{8... | collective-permute-start | bytes 491528 | tf_op jit(solution)/shard_map/ppermute | solution.py:211
  25.1 8.2 %collective-permute-start.5 = (bf16[128,640]{1,0:T(8,128)(2,1)S(1)}, bf16[128,640]{1,0:T(8,128)(2,1)S(1)}, u32[]{:S(2)}, u32[]{:S(2)}) collective-permute-start(bf16[128,640]{1,0:T(8,128)(2,1)S(1)} %bitcast_select_fusion), channel_id=1, source_target_pairs={{0,96},{1,97},{2,98},{3,99},{4,100},{5,101},{6,102},{7,103},{8,104... | collective-permute-start | bytes 491528 | tf_op jit(solution)/shard_map/ppermute | solution.py:211
  30.5 14.7 %copy-start.1 = (bf16[8,1024]{1,0:T(8,128)(2,1)S(1)}, bf16[8,1024]{1,0:T(8,128)(2,1)}, u32[]{:S(2)}) copy-start(bf16[8,1024]{1,0:T(8,128)(2,1)} %param.6) | copy-start | bytes 49156
  30.7 43.5 %collective-permute-start.3 = (bf16[4,256,640]{2,1,0:T(8,128)(2,1)S(1)}, bf16[4,256,640]{2,1,0:T(8,128)(2,1)S(1)}, u32[]{:S(2)}, u32[]{:S(2)}) collective-permute-start(bf16[4,256,640]{2,1,0:T(8,128)(2,1)S(1)} %pad_maximum_fusion.near_ref), channel_id=1, source_target_pairs={{0,1},{1,0},{2,3},{3,2},{4,5},{5,4},{6,7},{7,6},{8,9},{9,8},{10,11... | collective-permute-start | bytes 3932168 | tf_op jit(solution)/shard_map/ppermute | solution.py:229
  33.3 0.7 collective-permute-start.7
  34.0 17.0 %collective-permute-start.10 = (bf16[128,640]{1,0:T(8,128)(2,1)S(1)}, bf16[128,640]{1,0:T(8,128)(2,1)S(1)}, u32[]{:S(2)}, u32[]{:S(2)}) collective-permute-start(bf16[128,640]{1,0:T(8,128)(2,1)S(1)} %broadcast_select_fusion), channel_id=1, source_target_pairs={{96,64},{192,160},{320,288},{416,384},{0,480},{97,65},{193,161},{3... | collective-permute-start | bytes 491528 | tf_op jit(solution)/shard_map/ppermute | solution.py:223
  42.6 8.4 %collective-permute-start.9 = (bf16[128,640]{1,0:T(8,128)(2,1)S(1)}, bf16[128,640]{1,0:T(8,128)(2,1)S(1)}, u32[]{:S(2)}, u32[]{:S(2)}) collective-permute-start(bf16[128,640]{1,0:T(8,128)(2,1)S(1)} %broadcast_select_fusion), channel_id=1, source_target_pairs={{0,32},{96,128},{192,224},{320,352},{416,448},{1,33},{97,129},{193... | collective-permute-start | bytes 491528 | tf_op jit(solution)/shard_map/ppermute | solution.py:223
  43.9 7.1 %collective-permute-start.8 = (bf16[128,640]{1,0:T(8,128)(2,1)S(1)}, bf16[128,640]{1,0:T(8,128)(2,1)}, u32[]{:S(2)}, u32[]{:S(2)}) collective-permute-start(bf16[128,640]{1,0:T(8,128)(2,1)S(1)} %broadcast_select_fusion), channel_id=1, source_target_pairs={{192,256},{193,257},{194,258},{195,259},{196,260},{197,261},{198,2... | collective-permute-start | bytes 491528 | tf_op jit(solution)/shard_map/ppermute | solution.py:222
  46.0 13.7 %all-to-all-start = ((bf16[16,8,1024]{2,1,0:T(8,128)(2,1)}), bf16[16,8,1024]{2,1,0:T(8,128)(2,1)S(1)}, u32[]{:S(2)}, u32[]{:S(2)}) async-start(bf16[16,8,1024]{2,1,0:T(8,128)(2,1)} %broadcast_in_dim.4), calls=%async_computation | async-start | bytes 524288 | tf_op jit(solution)/shard_map/all_to_all | solution.py:21
  60.6 13.7 %all-to-all-start.1 = ((bf16[4,128,640]{2,1,0:T(8,128)(2,1)}), bf16[4,128,640]{2,1,0:T(8,128)(2,1)S(1)}, u32[]{:S(2)}, u32[]{:S(2)}) async-start(bf16[4,128,640]{2,1,0:T(8,128)(2,1)} %broadcast_in_dim.5), calls=%async_computation.1 | async-start | bytes 1310720 | tf_op jit(solution)/shard_map/all_to_all | solution.py:21
  77.3 43.6 %copy-start.2 = (s32[128]{0:T(128)S(1)}, s32[128]{0:T(128)}, u32[]{:S(2)}) copy-start(s32[128]{0:T(128)} %param.8) | copy-start | bytes 1540
  112.0 17.4 %all-to-all-start.3 = ((f32[16,4,1024]{2,1,0:T(4,128)}), f32[16,4,1024]{2,1,0:T(4,128)S(1)}, u32[]{:S(2)}, u32[]{:S(2)}) async-start(f32[16,4,1024]{2,1,0:T(4,128)} %shard_map.47), calls=%async_computation.3 | async-start | bytes 524288 | tf_op jit(solution)/shard_map/all_to_all | solution.py:21

commit v7 on v5

--- a/solution.py
+++ b/solution.py
@@ -21,13 +21,8 @@
     return lax.all_to_all(array, axes, 0, 0, tiled=True)
 
 
-def sent_to_all(array, axes):
-    count = lax.axis_size(axes)
-    return exchange(jnp.broadcast_to(array[None], (count, *array.shape)), axes)
-
-
 def ladder_kernel(place_ref, near_ref, far_ref, *refs):
-    *quarter_refs, out_ref, stack_ref, right_ref = refs
+    *quarter_refs, out_ref, stack_ref, right_ref, amps_ref = refs
     core, yh, own = place_ref[0], place_ref[1], place_ref[2]
     size = quarter_refs[0].shape[0]
     for q, ref in enumerate(quarter_refs):
@@ -55,31 +50,27 @@
         for h in range(2):
             rows = (n + h) * d_count
             stack_ref[:, rows : rows + d_count, :] = part[:, :, h * LANES : (h + 1) * LANES]
-    amps = jnp.concatenate(
-        [
-            ref[x, m * pair_rows : (m + 1) * pair_rows, :depth]
-            for m in (c_pairs, c_pairs + 1)
-            for ref in (near_ref, far_ref)
-            for x in range(ring)
-        ],
-        axis=0,
-    )
-    blocks = 4 * ring
-    odd = lax.rem(lax.broadcasted_iota(jnp.int32, (1, 1, LANES), 2) // a_dev, 2) == 1
+    for m in range(2):
+        for rc, ref in enumerate((near_ref, far_ref)):
+            for x in range(ring):
+                place = (lax.rem(yh + m, 2) * ring + x) * 2 + lax.rem(core + rc, 2)
+                first = (c_pairs + m) * pair_rows
+                block = ref[x, first : first + pair_rows, :depth].astype(jnp.float32)
+                for g in range(2):
+                    amps_ref[g, place] = block[g * a_dev : (g + 1) * a_dev]
+    i_count = amps_ref.shape[1] * a_dev
+    amps = amps_ref[...].reshape(2 * i_count, depth).astype(jnp.bfloat16)
+    odd = lax.rem(lax.broadcasted_iota(jnp.int32, (1, LANES), 1) // a_dev, 2) == 1
+    rows = out_ref.shape[1]
     for q in range(b_count // 2):
         sums = []
         for b, step in ((2 * q, LANES - a_dev), (2 * q + 1, a_dev)):
             full = jnp.dot(amps, stack_ref[b], preferred_element_type=jnp.float32)
-            full = full.reshape(blocks, 2, a_dev, LANES)
-            mixed = jnp.where(odd, full[:, 1], full[:, 0]).reshape(blocks * a_dev, LANES)
+            mixed = jnp.where(odd, full[i_count:], full[:i_count])
             sums.append(mixed + pltpu.roll(mixed, step, 1))
-        found = jnp.where(odd[0], sums[1], sums[0]).astype(out_ref.dtype)
-        for block in range(blocks):
-            other_yh, other_core, x = block // (2 * ring), block // ring % 2, block % ring
-            place = (lax.rem(yh + other_yh, 2) * ring + x) * 2 + lax.rem(core + other_core, 2)
-            for h in range(2):
-                rows = found[block * a_dev + h * (a_dev // 2) : block * a_dev + (h + 1) * (a_dev // 2)]
-                out_ref[2 * place + h, :, q * LANES : (q + 1) * LANES] = rows
+        found = jnp.where(odd, sums[1], sums[0]).astype(out_ref.dtype)
+        for k in range(out_ref.shape[0]):
+            out_ref[k, :, q * LANES : (q + 1) * LANES] = found[k * rows : (k + 1) * rows]
 
 
 def in_vmem(count):
@@ -100,18 +91,46 @@
         scratch_shapes=[
             pltpu.VMEM((b_count, depth, LANES), jnp.bfloat16),
             pltpu.VMEM(right, jnp.bfloat16),
+            pltpu.VMEM((2, 4 * near.shape[0], b_count // 2, depth), jnp.float32),
         ],
         compiler_params=pltpu.CompilerParams(vmem_limit_bytes=12 * 1024 * 1024),
         cost_estimate=pl.CostEstimate(
             flops=2 * pairs, bytes_accessed=4 * near.size, transcendentals=0
         ),
     )(place, near, far, *quarters)
+
+
+def pack_kernel(rows_ref, amps_ref, other_ref, out_ref):
+    count, cells = rows_ref.shape[0], amps_ref.shape[1] // 2
+    for n in range(out_ref.shape[0]):
+        out_ref[n, :count, :] = rows_ref[...]
+    out_ref[:, count:, cells:] = jnp.zeros_like(out_ref[:, count:, cells:])
+    for m, ref in enumerate((amps_ref, other_ref)):
+        block = jnp.concatenate([ref[:, :cells], ref[:, cells:]], axis=0)
+        for n in range(out_ref.shape[0]):
+            first = count + m * block.shape[0]
+            out_ref[n, first : first + block.shape[0], :cells] = block
+
+
+def packed_copies(rows, amps, other, copies):
+    count = rows.shape[0] + 4 * amps.shape[0]
+    return pl.pallas_call(
+        pack_kernel,
+        out_shape=jax.ShapeDtypeStruct((copies, count, rows.shape[1]), rows.dtype),
+        in_specs=in_vmem(3),
+        out_specs=pl.BlockSpec(memory_space=pltpu.VMEM),
+        compiler_params=pltpu.CompilerParams(vmem_limit_bytes=6 * 1024 * 1024),
+        cost_estimate=pl.CostEstimate(
+            flops=rows.size, bytes_accessed=16 * rows.size, transcendentals=0
+        ),
+    )(rows, amps, other)
 
 
 def total_kernel(parts_ref, out_ref):
     total = parts_ref[0].astype(jnp.float32)
     for k in range(1, parts_ref.shape[0]):
         total = total + parts_ref[k].astype(jnp.float32)
+    total = total.astype(out_ref.dtype)
     for o in range(out_ref.shape[0]):
         out_ref[o] = total
 
@@ -119,7 +138,7 @@
 def totals(parts, copies):
     return pl.pallas_call(
         total_kernel,
-        out_shape=jax.ShapeDtypeStruct((copies, *parts.shape[1:]), jnp.float32),
+        out_shape=jax.ShapeDtypeStruct((copies, *parts.shape[1:]), parts.dtype),
         in_specs=in_vmem(1),
         out_specs=pl.BlockSpec(memory_space=pltpu.VMEM),
         compiler_params=pltpu.CompilerParams(vmem_limit_bytes=4 * 1024 * 1024),
@@ -141,6 +160,7 @@
         found = jnp.zeros((occ, LANES), jnp.float32)
         for m in range(chunks):
             block = every_ref[holder, :, pl.ds(pl.multiple_of(first + m * LANES, LANES), LANES)]
+            block = block.astype(jnp.float32)
             shift = lax.rem((m + ring - lax.rem(a_tile, ring)) * group, LANES)
             found = jnp.where(lane_group == m, pltpu.roll(block, shift, 1), found)
         return found
@@ -155,40 +175,26 @@
                 for s in range(slots)
             ],
             axis=0,
-        )
-
-    def thirds(rows):
-        high = rows.astype(jnp.bfloat16)
-        rest = rows - high.astype(jnp.float32)
-        middle = rest.astype(jnp.bfloat16)
-        low = (rest - middle.astype(jnp.float32)).astype(jnp.bfloat16)
-        return high, middle, low
-
-    def placed(parts, spot):
+        ).astype(jnp.bfloat16)
+
+    def placed(rows, spot):
         column = lax.broadcasted_iota(jnp.int32, (width, width), 1)
         chosen = (column == spot).astype(jnp.float32).astype(jnp.bfloat16)
-        found = jnp.dot(
-            jnp.concatenate(parts, axis=0), chosen, preferred_element_type=jnp.float32
-        )
-        high, middle, low = (found[n * slots * occ : (n + 1) * slots * occ] for n in range(3))
-        return high + middle + low
+        return jnp.dot(rows, chosen, preferred_element_type=jnp.float32)
 
     lane = lax.broadcasted_iota(jnp.int32, (width, width), 0)
     core_b = lane // LANES
     core_a = lax.rem(lane // (group // 2) + core_b, 2)
     a = core_a * (TS // 2) + lax.rem(lane, TS // 2)
     b = core_b * (TS // 2) + lax.rem(lane, LANES) // group * 2 + lax.rem(lane // (TS // 2), 2)
-    straight = placed(thirds(tiles(0)), a * TS + b)
+    straight = placed(tiles(0), a * TS + b)
     row = lax.broadcasted_iota(jnp.int32, (slots * occ, slots * occ), 0)
     column = lax.broadcasted_iota(jnp.int32, (slots * occ, slots * occ), 1)
     source = row // occ * occ
     for i in range(occ):
         source = source + jnp.where(lax.rem(row, occ) == i, swap_ref[i], 0)
     chosen = (column == source).astype(jnp.float32).astype(jnp.bfloat16)
-    swapped = [
-        jnp.dot(chosen, part, preferred_element_type=jnp.float32).astype(jnp.bfloat16)
-        for part in thirds(tiles(1))
-    ]
+    swapped = jnp.dot(chosen, tiles(1), preferred_element_type=jnp.float32).astype(jnp.bfloat16)
     total = straight + placed(swapped, b * TS + a)
     for s in range(slots):
         out_ref[s] = total[s * occ : (s + 1) * occ]
@@ -213,18 +219,13 @@
     con_count = lax.axis_size(CONTRACT)
     ring = lax.axis_size("x")
     a_dev, c_dev, p_size = chol.shape
-    i_dev = amplitudes.shape[0]
-    i_count = i_dev * out_count
+    i_count = amplitudes.shape[0] * out_count
     half = c_dev // 2
-    pair_rows = 2 * a_dev
 
     other_amps = lax.ppermute(amplitudes, "yh", PAIR)
     rows = jnp.transpose(chol.reshape(a_dev, 2, half, p_size), (2, 1, 0, 3))
-    extra = jnp.stack([amplitudes, other_amps], axis=0).reshape(2, i_dev, 2, -1)
-    extra = jnp.transpose(extra, (0, 2, 1, 3)).reshape(2, pair_rows, -1)
-    extra = jnp.pad(extra, ((0, 0), (0, 0), (0, p_size - extra.shape[2])))
-    packed = jnp.concatenate([rows.reshape(half, pair_rows, p_size), extra], axis=0)
-    near = sent_to_all(packed.reshape(-1, p_size), "x")
+    packed = packed_copies(rows.reshape(-1, p_size), amplitudes, other_amps, ring)
+    near = exchange(packed, "x")
 
     z, yl, yh = lax.axis_index("z"), lax.axis_index("yl"), lax.axis_index("yh")
     depth_z = lax.axis_size("z")

time: 141 us -> 140 us (level)
  blocking collectives: 39.2 us -> 0 us
  starting transfers between devices: 60.4 us -> 81.6 us
  waiting for transfers between devices: 27.7 us -> 44.7 us
  Pallas kernels: 6.35 us -> 8.16 us
    all_to_all x1 -> x0, blocking collectives: 39.2 us -> none  [exchange(): return lax.all_to_all(array, axes, 0, 0, tiled=True)]
    all_to_all x2 -> x3, starting transfers between devices: 14 us -> 35.2 us  [exchange(): return lax.all_to_all(array, axes, 0, 0, tiled=True)]
    all_to_all x2 -> x3, waiting for transfers between devices: 18 us -> 35 us  [exchange(): return lax.all_to_all(array, axes, 0, 0, tiled=True)]
  transfers between devices with their start and end apart: 14 -> 15, of which waited for: 9 -> 10; matrix products, arithmetic and copies ran while one was open for 3% -> 3% of each run, Pallas kernels for 0% -> 0%
where the time goes in v7:
time: 140 us
  starting transfers between devices  81.6 us (58%)
  waiting for transfers between devices  44.7 us (32%)
  Pallas kernels  8.16 us (6%)
  local copies, waits for them, and re-layouts  2.66 us (2%)
  other arithmetic  2.23 us (2%)
    all_to_all x3, starting transfers between devices, exchange(): return lax.all_to_all(array, axes, 0, 0, tiled=True)  35.2 us
    all_to_all x3, waiting for transfers between devices, exchange(): return lax.all_to_all(array, axes, 0, 0, tiled=True)  35 us
    ppermute x2, starting transfers between devices, on_device(): got = sum((lax.ppermute(piece, 'z', [hop]) for hop in LONG))  14 us
    ppermute x1, starting transfers between devices, on_device(): far = lax.ppermute(near, 'core', PAIR)  9.73 us
    ppermute x3, starting transfers between devices, on_device(): lax.ppermute(piece, ('yl', 'yh'), [(at, at ^ q) for at in range(4)])  9.05 us
    ppermute x1, starting transfers between devices, on_device(): other_amps = lax.ppermute(amplitudes, 'yh', PAIR)  5.76 us
    ppermute x3, waiting for transfers between devices, on_device(): lax.ppermute(piece, ('yl', 'yh'), [(at, at ^ q) for at in range(4)])  4.96 us
    pallas_call x1, Pallas kernels, ladder_partials(): pl.pallas_call(ladder_kernel, out_shape=jax.ShapeDtypeStruct((con_count,...  4.63 us
  transfers between devices with their start and end apart: 15, of which 10 were waited for; matrix products, arithmetic and copies ran while one was open for 3% of the time, Pallas kernels for 0%

profile of v7, /device:TPU:1, one launch (start us, length us, event | category | flops | bytes accessed | tf_op | source)
XLA Modules:
  0.0 139.5 jit_solution(4245948389773380082)
XLA Ops:
  0.0 5.8 %collective-permute-start = (bf16[8,1024]{1,0:T(8,128)(2,1)}, bf16[8,1024]{1,0:T(8,128)(2,1)S(1)}, u32[]{:S(2)}, u32[]{:S(2)}) collective-permute-start(bf16[8,1024]{1,0:T(8,128)(2,1)} %amps_ref.1), channel_id=1, source_target_pairs={{0,8},{8,0},{1,9},{9,1},{2,10},{10,2},{3,11},{11,3},{4,12},{12,4},... | collective-permute-start | bytes 49160 | tf_op jit(solution)/shard_map/ppermute | solution.py:225
  5.8 1.1 copy.6
  7.1 0.7 copy-done.1
  7.8 1.3 shard_map.46
  9.1 4.2 %all-to-all-start = ((bf16[4,288,640]{2,1,0:T(8,128)(2,1)}), bf16[4,288,640]{2,1,0:T(8,128)(2,1)S(1)}, u32[]{:S(2)}, u32[]{:S(2)}) async-start(bf16[4,288,640]{2,1,0:T(8,128)(2,1)} %shard_map.46), calls=%async_computation | async-start | bytes 2949120 | tf_op jit(solution)/shard_map/all_to_all | solution.py:21
  13.3 3.2 %collective-permute-start.2 = (bf16[128,640]{1,0:T(8,128)(2,1)S(1)}, bf16[128,640]{1,0:T(8,128)(2,1)S(1)}, u32[]{:S(2)}, u32[]{:S(2)}) collective-permute-start(bf16[128,640]{1,0:T(8,128)(2,1)S(1)} %bitcast.12), channel_id=1, source_target_pairs={{0,16},{1,17},{2,18},{3,19},{4,20},{5,21},{6,22},{7,23},{8,24},{9,... | collective-permute-start | bytes 491528 | tf_op jit(solution)/shard_map/ppermute | solution.py:233
  16.5 9.5 %all-to-all-done.near_ref = bf16[4,288,640]{2,1,0:T(8,128)(2,1)S(1)} async-done(((bf16[4,288,640]{2,1,0:T(8,128)(2,1)}), bf16[4,288,640]{2,1,0:T(8,128)(2,1)S(1)}, u32[]{:S(2)}, u32[]{:S(2)}) %all-to-all-start) | async-done | bytes 1474592 | tf_op jit(solution)/shard_map/all_to_all | solution.py:21
  26.0 9.7 %collective-permute-start.1 = (bf16[4,288,640]{2,1,0:T(8,128)(2,1)S(1)}, bf16[4,288,640]{2,1,0:T(8,128)(2,1)S(1)}, u32[]{:S(2)}, u32[]{:S(2)}) collective-permute-start(bf16[4,288,640]{2,1,0:T(8,128)(2,1)S(1)} %all-to-all-done.near_ref), channel_id=1, source_target_pairs={{0,1},{1,0},{2,3},{3,2},{4,5},{5,4},{6,7},{7,6},{8,9},{9,8},{10,11... | collective-permute-start | bytes 4423688 | tf_op jit(solution)/shard_map/ppermute | solution.py:253
  35.8 12.0 %collective-permute-start.4 = (bf16[128,640]{1,0:T(8,128)(2,1)S(1)}, bf16[128,640]{1,0:T(8,128)(2,1)S(1)}, u32[]{:S(2)}, u32[]{:S(2)}) collective-permute-start(bf16[128,640]{1,0:T(8,128)(2,1)S(1)} %bitcast_select_fusion), channel_id=1, source_target_pairs={{0,416},{1,417},{2,418},{3,419},{4,420},{5,421},{6,422},{7,423},{8... | collective-permute-start | bytes 491528 | tf_op jit(solution)/shard_map/ppermute | solution.py:234
  47.9 1.9 %collective-permute-start.3 = (bf16[128,640]{1,0:T(8,128)(2,1)S(1)}, bf16[128,640]{1,0:T(8,128)(2,1)}, u32[]{:S(2)}, u32[]{:S(2)}) collective-permute-start(bf16[128,640]{1,0:T(8,128)(2,1)S(1)} %bitcast_select_fusion), channel_id=1, source_target_pairs={{0,96},{1,97},{2,98},{3,99},{4,100},{5,101},{6,102},{7,103},{8,104... | collective-permute-start | bytes 491528 | tf_op jit(solution)/shard_map/ppermute | solution.py:234
  49.8 1.6 %collective-permute-done.4 = bf16[128,640]{1,0:T(8,128)(2,1)S(1)} collective-permute-done((bf16[128,640]{1,0:T(8,128)(2,1)S(1)}, bf16[128,640]{1,0:T(8,128)(2,1)S(1)}, u32[]{:S(2)}, u32[]{:S(2)}) %collective-permute-start.4) | collective-permute-done | bytes 163872 | tf_op jit(solution)/shard_map/ppermute | solution.py:234
  51.4 1.3 collective-permute-done.3
  52.7 1.0 add_select_fusion.1
  53.6 0.7 collective-permute-start.5
  54.4 1.3 collective-permute-start.8
  55.7 1.3 collective-permute-start.7
  57.0 1.3 collective-permute-start.6
  58.6 1.3 collective-permute-done.7
  59.9 0.7 copy-done.3
  60.6 1.1 add_select_fusion.refs_0_
  61.6 4.6 %collective-permute-start.11 = (bf16[128,640]{1,0:T(8,128)(2,1)S(1)}, bf16[128,640]{1,0:T(8,128)(2,1)S(1)}, u32[]{:S(2)}, u32[]{:S(2)}) collective-permute-start(bf16[128,640]{1,0:T(8,128)(2,1)S(1)} %add_select_fusion.refs_0_), channel_id=1, source_target_pairs={{0,24},{8,16},{16,8},{24,0},{1,25},{9,17},{17,9},{25,1},{2,26},{10... | collective-permute-start | bytes 491528 | tf_op jit(solution)/shard_map/ppermute | solution.py:250
  66.3 2.3 %collective-permute-start.10 = (bf16[128,640]{1,0:T(8,128)(2,1)S(1)}, bf16[128,640]{1,0:T(8,128)(2,1)S(1)}, u32[]{:S(2)}, u32[]{:S(2)}) collective-permute-start(bf16[128,640]{1,0:T(8,128)(2,1)S(1)} %add_select_fusion.refs_0_), channel_id=1, source_target_pairs={{0,8},{8,0},{16,24},{24,16},{1,9},{9,1},{17,25},{25,17},{2,10},{10... | collective-permute-start | bytes 491528 | tf_op jit(solution)/shard_map/ppermute | solution.py:250
  68.6 2.1 %collective-permute-start.9 = (bf16[128,640]{1,0:T(8,128)(2,1)S(1)}, bf16[128,640]{1,0:T(8,128)(2,1)}, u32[]{:S(2)}, u32[]{:S(2)}) collective-permute-start(bf16[128,640]{1,0:T(8,128)(2,1)S(1)} %add_select_fusion.refs_0_), channel_id=1, source_target_pairs={{0,16},{8,24},{16,0},{24,8},{1,17},{9,25},{17,1},{25,9},{2,18},{10... | collective-permute-start | bytes 491528 | tf_op jit(solution)/shard_map/ppermute | solution.py:250
  70.8 3.1 %collective-permute-done.10.refs_2_ = bf16[128,640]{1,0:T(8,128)(2,1)S(1)} collective-permute-done((bf16[128,640]{1,0:T(8,128)(2,1)S(1)}, bf16[128,640]{1,0:T(8,128)(2,1)S(1)}, u32[]{:S(2)}, u32[]{:S(2)}) %collective-permute-start.10) | collective-permute-done | bytes 163872 | tf_op jit(solution)/shard_map/ppermute | solution.py:250
  73.9 1.9 %collective-permute-done.9.refs_1_ = bf16[128,640]{1,0:T(8,128)(2,1)} collective-permute-done((bf16[128,640]{1,0:T(8,128)(2,1)S(1)}, bf16[128,640]{1,0:T(8,128)(2,1)}, u32[]{:S(2)}, u32[]{:S(2)}) %collective-permute-start.9) | collective-permute-done | bytes 163872 | tf_op jit(solution)/shard_map/ppermute | solution.py:250
  75.8 4.6 %shard_map.47 = bf16[32,4,1024]{2,1,0:T(4,128)(2,1)} custom-call(s32[3]{0:T(128)S(1)} %pad_add_fusion.place_ref, bf16[4,288,640]{2,1,0:T(8,128)(2,1)S(1)} %all-to-all-done.near_ref, bf16[4,288,640]{2,1,0:T(8,128)(2,1)S(1)} %collective-permute-done.1.far_ref, bf16[128,640]{1,0:T(8,128)(2,1)S(1)} %add_select_fusion.refs_0_, ...), custom_call_target="tpu_custom_call" | custom-call | flops 1509949440 | bytes 2949120 | tf_op jit(solution)/shard_map/pallas_call | solution.py:84
  80.4 21.2 %all-to-all-start.1 = ((bf16[32,4,1024]{2,1,0:T(4,128)(2,1)}), bf16[32,4,1024]{2,1,0:T(4,128)(2,1)S(1)}, u32[]{:S(2)}, u32[]{:S(2)}) async-start(bf16[32,4,1024]{2,1,0:T(4,128)(2,1)} %shard_map.47), calls=%async_computation.1 | async-start | bytes 524288 | tf_op jit(solution)/shard_map/all_to_all | solution.py:21
  101.6 18.2 %all-to-all-done.1.parts_ref = bf16[32,4,1024]{2,1,0:T(4,128)(2,1)S(1)} async-done(((bf16[32,4,1024]{2,1,0:T(4,128)(2,1)}), bf16[32,4,1024]{2,1,0:T(4,128)(2,1)S(1)}, u32[]{:S(2)}, u32[]{:S(2)}) %all-to-all-start.1) | async-done | bytes 262176 | tf_op jit(solution)/shard_map/all_to_all | solution.py:21
  119.9 0.7 shard_map.48
  120.6 9.8 %all-to-all-start.2 = ((bf16[16,4,1024]{2,1,0:T(4,128)(2,1)}), bf16[16,4,1024]{2,1,0:T(4,128)(2,1)S(1)}, u32[]{:S(2)}, u32[]{:S(2)}) async-start(bf16[16,4,1024]{2,1,0:T(4,128)(2,1)} %shard_map.48), calls=%async_computation.2 | async-start | bytes 262144 | tf_op jit(solution)/shard_map/all_to_all | solution.py:21
  130.7 7.3 %all-to-all-done.2.every_ref = bf16[16,4,1024]{2,1,0:T(4,128)(2,1)S(1)} async-done(((bf16[16,4,1024]{2,1,0:T(4,128)(2,1)}), bf16[16,4,1024]{2,1,0:T(4,128)(2,1)S(1)}, u32[]{:S(2)}, u32[]{:S(2)}) %all-to-all-start.2) | async-done | bytes 131104 | tf_op jit(solution)/shard_map/all_to_all | solution.py:21
  138.0 1.6 %shard_map.49 = f32[4,4,256]{2,1,0:T(4,128)} custom-call(s32[4,2]{1,0:T(4,128)S(1)} %copy.7.pairs_ref, s32[4]{0:T(128)S(1)} %dynamic-slice_subtract_fusion.swap_ref, bf16[16,4,1024]{2,1,0:T(4,128)(2,1)S(1)} %all-to-all-done.2.every_ref), custom_call_target="tpu_custom_call" | custom-call | flops 6553600 | bytes 262144 | tf_op jit(solution)/shard_map/pallas_call | solution.py:205
  (22 shorter events, 1.0 us)
Async XLA Ops:
  0.0 130.4 %copy-start = (s32[64,2]{0,1:T(2,128)S(1)}, s32[64,2]{0,1:T(2,128)}, u32[]{:S(2)}) copy-start(s32[64,2]{0,1:T(2,128)} %param.7) | copy-start | bytes 1540
  0.0 7.1 %collective-permute-start = (bf16[8,1024]{1,0:T(8,128)(2,1)}, bf16[8,1024]{1,0:T(8,128)(2,1)S(1)}, u32[]{:S(2)}, u32[]{:S(2)}) collective-permute-start(bf16[8,1024]{1,0:T(8,128)(2,1)} %amps_ref.1), channel_id=1, source_target_pairs={{0,8},{8,0},{1,9},{9,1},{2,10},{10,2},{3,11},{11,3},{4,12},{12,4},... | collective-permute-start | bytes 49160 | tf_op jit(solution)/shard_map/ppermute | solution.py:225
  7.1 0.7 copy-start.1
  9.1 4.2 %copy-start.2 = (bf16[8,32,640]{2,1,0:T(8,128)(2,1)S(1)}, bf16[8,32,640]{2,1,0:T(8,128)(2,1)}, u32[]{:S(2)}) copy-start(bf16[8,32,640]{2,1,0:T(8,128)(2,1)} %param.5) | copy-start | bytes 983044
  9.1 17.0 %all-to-all-start = ((bf16[4,288,640]{2,1,0:T(8,128)(2,1)}), bf16[4,288,640]{2,1,0:T(8,128)(2,1)S(1)}, u32[]{:S(2)}, u32[]{:S(2)}) async-start(bf16[4,288,640]{2,1,0:T(8,128)(2,1)} %shard_map.46), calls=%async_computation | async-start | bytes 2949120 | tf_op jit(solution)/shard_map/all_to_all | solution.py:21
  13.3 22.5 %collective-permute-start.2 = (bf16[128,640]{1,0:T(8,128)(2,1)S(1)}, bf16[128,640]{1,0:T(8,128)(2,1)S(1)}, u32[]{:S(2)}, u32[]{:S(2)}) collective-permute-start(bf16[128,640]{1,0:T(8,128)(2,1)S(1)} %bitcast.12), channel_id=1, source_target_pairs={{0,16},{1,17},{2,18},{3,19},{4,20},{5,21},{6,22},{7,23},{8,24},{9,... | collective-permute-start | bytes 491528 | tf_op jit(solution)/shard_map/ppermute | solution.py:233
  26.0 49.7 %collective-permute-start.1 = (bf16[4,288,640]{2,1,0:T(8,128)(2,1)S(1)}, bf16[4,288,640]{2,1,0:T(8,128)(2,1)S(1)}, u32[]{:S(2)}, u32[]{:S(2)}) collective-permute-start(bf16[4,288,640]{2,1,0:T(8,128)(2,1)S(1)} %all-to-all-done.near_ref), channel_id=1, source_target_pairs={{0,1},{1,0},{2,3},{3,2},{4,5},{5,4},{6,7},{7,6},{8,9},{9,8},{10,11... | collective-permute-start | bytes 4423688 | tf_op jit(solution)/shard_map/ppermute | solution.py:253
  35.8 15.5 %collective-permute-start.4 = (bf16[128,640]{1,0:T(8,128)(2,1)S(1)}, bf16[128,640]{1,0:T(8,128)(2,1)S(1)}, u32[]{:S(2)}, u32[]{:S(2)}) collective-permute-start(bf16[128,640]{1,0:T(8,128)(2,1)S(1)} %bitcast_select_fusion), channel_id=1, source_target_pairs={{0,416},{1,417},{2,418},{3,419},{4,420},{5,421},{6,422},{7,423},{8... | collective-permute-start | bytes 491528 | tf_op jit(solution)/shard_map/ppermute | solution.py:234
  47.9 4.8 %collective-permute-start.3 = (bf16[128,640]{1,0:T(8,128)(2,1)S(1)}, bf16[128,640]{1,0:T(8,128)(2,1)}, u32[]{:S(2)}, u32[]{:S(2)}) collective-permute-start(bf16[128,640]{1,0:T(8,128)(2,1)S(1)} %bitcast_select_fusion), channel_id=1, source_target_pairs={{0,96},{1,97},{2,98},{3,99},{4,100},{5,101},{6,102},{7,103},{8,104... | collective-permute-start | bytes 491528 | tf_op jit(solution)/shard_map/ppermute | solution.py:234
  53.6 0.7 collective-permute-start.5
  54.4 4.2 %collective-permute-start.8 = (bf16[128,640]{1,0:T(8,128)(2,1)S(1)}, bf16[128,640]{1,0:T(8,128)(2,1)S(1)}, u32[]{:S(2)}, u32[]{:S(2)}) collective-permute-start(bf16[128,640]{1,0:T(8,128)(2,1)S(1)} %broadcast_select_fusion), channel_id=1, source_target_pairs={{96,64},{192,160},{320,288},{416,384},{0,480},{97,65},{193,161},{3... | collective-permute-start | bytes 491528 | tf_op jit(solution)/shard_map/ppermute | solution.py:246
  55.7 4.2 %collective-permute-start.7 = (bf16[128,640]{1,0:T(8,128)(2,1)S(1)}, bf16[128,640]{1,0:T(8,128)(2,1)S(1)}, u32[]{:S(2)}, u32[]{:S(2)}) collective-permute-start(bf16[128,640]{1,0:T(8,128)(2,1)S(1)} %broadcast_select_fusion), channel_id=1, source_target_pairs={{0,32},{96,128},{192,224},{320,352},{416,448},{1,33},{97,129},{193... | collective-permute-start | bytes 491528 | tf_op jit(solution)/shard_map/ppermute | solution.py:246
  57.0 3.6 %collective-permute-start.6 = (bf16[128,640]{1,0:T(8,128)(2,1)S(1)}, bf16[128,640]{1,0:T(8,128)(2,1)}, u32[]{:S(2)}, u32[]{:S(2)}) collective-permute-start(bf16[128,640]{1,0:T(8,128)(2,1)S(1)} %broadcast_select_fusion), channel_id=1, source_target_pairs={{192,256},{193,257},{194,258},{195,259},{196,260},{197,261},{198,2... | collective-permute-start | bytes 491528 | tf_op jit(solution)/shard_map/ppermute | solution.py:245
  59.9 0.7 copy-start.3
  61.6 9.2 %collective-permute-start.11 = (bf16[128,640]{1,0:T(8,128)(2,1)S(1)}, bf16[128,640]{1,0:T(8,128)(2,1)S(1)}, u32[]{:S(2)}, u32[]{:S(2)}) collective-permute-start(bf16[128,640]{1,0:T(8,128)(2,1)S(1)} %add_select_fusion.refs_0_), channel_id=1, source_target_pairs={{0,24},{8,16},{16,8},{24,0},{1,25},{9,17},{17,9},{25,1},{2,26},{10... | collective-permute-start | bytes 491528 | tf_op jit(solution)/shard_map/ppermute | solution.py:250
  66.3 7.6 %collective-permute-start.10 = (bf16[128,640]{1,0:T(8,128)(2,1)S(1)}, bf16[128,640]{1,0:T(8,128)(2,1)S(1)}, u32[]{:S(2)}, u32[]{:S(2)}) collective-permute-start(bf16[128,640]{1,0:T(8,128)(2,1)S(1)} %add_select_fusion.refs_0_), channel_id=1, source_target_pairs={{0,8},{8,0},{16,24},{24,16},{1,9},{9,1},{17,25},{25,17},{2,10},{10... | collective-permute-start | bytes 491528 | tf_op jit(solution)/shard_map/ppermute | solution.py:250
  68.6 7.2 %collective-permute-start.9 = (bf16[128,640]{1,0:T(8,128)(2,1)S(1)}, bf16[128,640]{1,0:T(8,128)(2,1)}, u32[]{:S(2)}, u32[]{:S(2)}) collective-permute-start(bf16[128,640]{1,0:T(8,128)(2,1)S(1)} %add_select_fusion.refs_0_), channel_id=1, source_target_pairs={{0,16},{8,24},{16,0},{24,8},{1,17},{9,25},{17,1},{25,9},{2,18},{10... | collective-permute-start | bytes 491528 | tf_op jit(solution)/shard_map/ppermute | solution.py:250
  70.8 59.8 %copy-start.4 = (s32[128]{0:T(128)S(1)}, s32[128]{0:T(128)}, u32[]{:S(2)}) copy-start(s32[128]{0:T(128)} %param.8) | copy-start | bytes 1540
  80.4 39.4 %all-to-all-start.1 = ((bf16[32,4,1024]{2,1,0:T(4,128)(2,1)}), bf16[32,4,1024]{2,1,0:T(4,128)(2,1)S(1)}, u32[]{:S(2)}, u32[]{:S(2)}) async-start(bf16[32,4,1024]{2,1,0:T(4,128)(2,1)} %shard_map.47), calls=%async_computation.1 | async-start | bytes 524288 | tf_op jit(solution)/shard_map/all_to_all | solution.py:21
  120.6 17.4 %all-to-all-start.2 = ((bf16[16,4,1024]{2,1,0:T(4,128)(2,1)}), bf16[16,4,1024]{2,1,0:T(4,128)(2,1)S(1)}, u32[]{:S(2)}, u32[]{:S(2)}) async-start(bf16[16,4,1024]{2,1,0:T(4,128)(2,1)} %shard_map.48), calls=%async_computation.2 | async-start | bytes 262144 | tf_op jit(solution)/shard_map/all_to_all | solution.py:21

commit v8 on v7

--- a/solution.py
+++ b/solution.py
@@ -13,8 +13,8 @@
 CONTRACT = ("z", "yl")
 OUT = ("yh", "x", "core")
 PAIR = [(0, 1), (1, 0)]
-LONG, MIDDLE = [(0, 3), (0, 13)], [(3, 6), (13, 10)]
-SENDERS = (0, 3, 6, 10, 13)
+LONG, MIDDLE = [(0, 3), (0, 12)], [(3, 6), (12, 9), (0, 14)]
+SENDERS, HOLDERS = (0, 3, 6, 9, 12), (0, 3, 6, 9, 12, 14)
 
 
 def exchange(array, axes):
@@ -22,7 +22,7 @@
 
 
 def ladder_kernel(place_ref, near_ref, far_ref, *refs):
-    *quarter_refs, out_ref, stack_ref, right_ref, amps_ref = refs
+    *quarter_refs, out_ref, stack_ref, right_ref = refs
     core, yh, own = place_ref[0], place_ref[1], place_ref[2]
     size = quarter_refs[0].shape[0]
     for q, ref in enumerate(quarter_refs):
@@ -50,16 +50,27 @@
         for h in range(2):
             rows = (n + h) * d_count
             stack_ref[:, rows : rows + d_count, :] = part[:, :, h * LANES : (h + 1) * LANES]
-    for m in range(2):
-        for rc, ref in enumerate((near_ref, far_ref)):
-            for x in range(ring):
-                place = (lax.rem(yh + m, 2) * ring + x) * 2 + lax.rem(core + rc, 2)
-                first = (c_pairs + m) * pair_rows
-                block = ref[x, first : first + pair_rows, :depth].astype(jnp.float32)
-                for g in range(2):
-                    amps_ref[g, place] = block[g * a_dev : (g + 1) * a_dev]
-    i_count = amps_ref.shape[1] * a_dev
-    amps = amps_ref[...].reshape(2 * i_count, depth).astype(jnp.bfloat16)
+    held = jnp.concatenate(
+        [
+            ref[x, m * pair_rows : (m + 1) * pair_rows, :depth]
+            for m in (c_pairs, c_pairs + 1)
+            for ref in (near_ref, far_ref)
+            for x in range(ring)
+        ],
+        axis=0,
+    )
+    count = held.shape[0]
+    i_count = count // 2
+    row = lax.broadcasted_iota(jnp.int32, (count, 1), 0)
+    block = lax.rem(row, i_count) // a_dev
+    from_yh = lax.rem(block // (2 * ring) + yh, 2)
+    from_core = lax.rem(block + core, 2)
+    from_x = lax.rem(block // 2, ring)
+    source = ((from_yh * 2 + from_core) * ring + from_x) * 2 + row // i_count
+    source = source * a_dev + lax.rem(row, a_dev)
+    column = lax.broadcasted_iota(jnp.int32, (count, count), 1)
+    chosen = (column == source).astype(jnp.float32).astype(jnp.bfloat16)
+    amps = jnp.dot(chosen, held, preferred_element_type=jnp.float32).astype(jnp.bfloat16)
     odd = lax.rem(lax.broadcasted_iota(jnp.int32, (1, LANES), 1) // a_dev, 2) == 1
     rows = out_ref.shape[1]
     for q in range(b_count // 2):
@@ -91,7 +102,6 @@
         scratch_shapes=[
             pltpu.VMEM((b_count, depth, LANES), jnp.bfloat16),
             pltpu.VMEM(right, jnp.bfloat16),
-            pltpu.VMEM((2, 4 * near.shape[0], b_count // 2, depth), jnp.float32),
         ],
         compiler_params=pltpu.CompilerParams(vmem_limit_bytes=12 * 1024 * 1024),
         cost_estimate=pl.CostEstimate(
@@ -237,15 +247,15 @@
     piece = jnp.where(functools.reduce(jnp.logical_or, [z == to for _, to in MIDDLE]), got, piece)
     reach = {}
     for to in range(depth_z):
-        if to not in SENDERS:
+        if to not in HOLDERS:
             steps = [((to - at + depth_z // 2) % depth_z - depth_z // 2, at) for at in SENDERS]
             step, at = min(steps, key=lambda pair: abs(pair[0]))
             reach.setdefault(step, []).append((at, to))
     steps = sorted(reach, key=abs, reverse=True)
     got = lax.ppermute(piece, "z", reach[steps[0]])
     got = sum((lax.ppermute(piece, "z", reach[step]) for step in steps[1:]), got)
-    sender = functools.reduce(jnp.logical_or, [z == at for at in SENDERS])
-    piece = jnp.where(sender, piece, got)
+    holder = functools.reduce(jnp.logical_or, [z == at for at in HOLDERS])
+    piece = jnp.where(holder, piece, got)
     quarters = [piece] + [
         lax.ppermute(piece, ("yl", "yh"), [(at, at ^ q) for at in range(4)]) for q in (2, 1, 3)
     ]

time: 140 us -> 135 us (0.964)
  starting transfers between devices: 81.6 us -> 73.5 us
  waiting for transfers between devices: 44.7 us -> 48.3 us
    all_to_all x3, starting transfers between devices: 35.2 us -> 26.7 us  [exchange(): return lax.all_to_all(array, axes, 0, 0, tiled=True)]
    ppermute x1, waiting for transfers between devices: 0.01 us -> 2.92 us  [on_device(): got = lax.ppermute(piece, 'z', MIDDLE)]
  transfers between devices with their start and end apart: 15 -> 14, of which waited for: 10 -> 11; matrix products, arithmetic and copies ran while one was open for 3% -> 3% of each run, Pallas kernels for 0% -> 0%
where the time goes in v8:
time: 135 us; the launch traced here: 134 us
  starting transfers between devices  73.5 us (54%)
  waiting for transfers between devices  48.3 us (36%)
  Pallas kernels  8.32 us (6%)
  other arithmetic  2.13 us (2%)
  local copies, waits for them, and re-layouts  2.01 us (1%)
    all_to_all x3, waiting for transfers between devices, exchange(): return lax.all_to_all(array, axes, 0, 0, tiled=True)  35 us
    all_to_all x3, starting transfers between devices, exchange(): return lax.all_to_all(array, axes, 0, 0, tiled=True)  26.7 us
    ppermute x2, starting transfers between devices, on_device(): got = sum((lax.ppermute(piece, 'z', [hop]) for hop in LONG))  14.4 us
    ppermute x1, starting transfers between devices, on_device(): far = lax.ppermute(near, 'core', PAIR)  9.73 us
    ppermute x3, starting transfers between devices, on_device(): lax.ppermute(piece, ('yl', 'yh'), [(at, at ^ q) for at in range(4)])  9.05 us
    ppermute x1, starting transfers between devices, on_device(): other_amps = lax.ppermute(amplitudes, 'yh', PAIR)  5.76 us
    ppermute x3, waiting for transfers between devices, on_device(): lax.ppermute(piece, ('yl', 'yh'), [(at, at ^ q) for at in range(4)])  5.67 us
    pallas_call x1, Pallas kernels, ladder_partials(): pl.pallas_call(ladder_kernel, out_shape=jax.ShapeDtypeStruct((con_count,...  4.81 us
  transfers between devices with their start and end apart: 14, of which 11 were waited for; matrix products, arithmetic and copies ran while one was open for 3% of the time, Pallas kernels for 0%

profile of v8, /device:TPU:1, one launch (start us, length us, event | category | flops | bytes accessed | tf_op | source)
XLA Modules:
  0.0 134.4 jit_solution(17402686180773726199)
XLA Ops:
  0.0 5.8 %collective-permute-start = (bf16[8,1024]{1,0:T(8,128)(2,1)}, bf16[8,1024]{1,0:T(8,128)(2,1)S(1)}, u32[]{:S(2)}, u32[]{:S(2)}) collective-permute-start(bf16[8,1024]{1,0:T(8,128)(2,1)} %amps_ref.1), channel_id=1, source_target_pairs={{0,8},{8,0},{1,9},{9,1},{2,10},{10,2},{3,11},{11,3},{4,12},{12,4},... | collective-permute-start | bytes 49160 | tf_op jit(solution)/shard_map/ppermute | solution.py:235
  5.8 1.1 copy.6
  7.1 0.7 copy-done.1
  7.8 1.2 shard_map.46
  9.1 4.2 %all-to-all-start = ((bf16[4,288,640]{2,1,0:T(8,128)(2,1)}), bf16[4,288,640]{2,1,0:T(8,128)(2,1)S(1)}, u32[]{:S(2)}, u32[]{:S(2)}) async-start(bf16[4,288,640]{2,1,0:T(8,128)(2,1)} %shard_map.46), calls=%async_computation | async-start | bytes 2949120 | tf_op jit(solution)/shard_map/all_to_all | solution.py:21
  13.3 3.2 %collective-permute-start.2 = (bf16[128,640]{1,0:T(8,128)(2,1)S(1)}, bf16[128,640]{1,0:T(8,128)(2,1)S(1)}, u32[]{:S(2)}, u32[]{:S(2)}) collective-permute-start(bf16[128,640]{1,0:T(8,128)(2,1)S(1)} %bitcast.12), channel_id=1, source_target_pairs={{0,16},{1,17},{2,18},{3,19},{4,20},{5,21},{6,22},{7,23},{8,24},{9,... | collective-permute-start | bytes 491528 | tf_op jit(solution)/shard_map/ppermute | solution.py:243
  16.5 9.5 %all-to-all-done.near_ref = bf16[4,288,640]{2,1,0:T(8,128)(2,1)S(1)} async-done(((bf16[4,288,640]{2,1,0:T(8,128)(2,1)}), bf16[4,288,640]{2,1,0:T(8,128)(2,1)S(1)}, u32[]{:S(2)}, u32[]{:S(2)}) %all-to-all-start) | async-done | bytes 1474592 | tf_op jit(solution)/shard_map/all_to_all | solution.py:21
  26.0 9.7 %collective-permute-start.1 = (bf16[4,288,640]{2,1,0:T(8,128)(2,1)S(1)}, bf16[4,288,640]{2,1,0:T(8,128)(2,1)S(1)}, u32[]{:S(2)}, u32[]{:S(2)}) collective-permute-start(bf16[4,288,640]{2,1,0:T(8,128)(2,1)S(1)} %all-to-all-done.near_ref), channel_id=1, source_target_pairs={{0,1},{1,0},{2,3},{3,2},{4,5},{5,4},{6,7},{7,6},{8,9},{9,8},{10,11... | collective-permute-start | bytes 4423688 | tf_op jit(solution)/shard_map/ppermute | solution.py:263
  35.8 12.5 %collective-permute-start.4 = (bf16[128,640]{1,0:T(8,128)(2,1)S(1)}, bf16[128,640]{1,0:T(8,128)(2,1)S(1)}, u32[]{:S(2)}, u32[]{:S(2)}) collective-permute-start(bf16[128,640]{1,0:T(8,128)(2,1)S(1)} %bitcast_select_fusion), channel_id=1, source_target_pairs={{0,384},{1,385},{2,386},{3,387},{4,388},{5,389},{6,390},{7,391},{8... | collective-permute-start | bytes 491528 | tf_op jit(solution)/shard_map/ppermute | solution.py:244
  48.3 2.0 %collective-permute-start.3 = (bf16[128,640]{1,0:T(8,128)(2,1)S(1)}, bf16[128,640]{1,0:T(8,128)(2,1)}, u32[]{:S(2)}, u32[]{:S(2)}) collective-permute-start(bf16[128,640]{1,0:T(8,128)(2,1)S(1)} %bitcast_select_fusion), channel_id=1, source_target_pairs={{0,96},{1,97},{2,98},{3,99},{4,100},{5,101},{6,102},{7,103},{8,104... | collective-permute-start | bytes 491528 | tf_op jit(solution)/shard_map/ppermute | solution.py:244
  50.3 1.6 %collective-permute-done.4 = bf16[128,640]{1,0:T(8,128)(2,1)S(1)} collective-permute-done((bf16[128,640]{1,0:T(8,128)(2,1)S(1)}, bf16[128,640]{1,0:T(8,128)(2,1)S(1)}, u32[]{:S(2)}, u32[]{:S(2)}) %collective-permute-start.4) | collective-permute-done | bytes 163872 | tf_op jit(solution)/shard_map/ppermute | solution.py:244
  51.8 1.3 collective-permute-done.3
  53.1 1.0 add_select_fusion.1
  54.1 1.3 collective-permute-start.5
  55.4 2.9 %collective-permute-done.5 = bf16[128,640]{1,0:T(8,128)(2,1)S(1)} collective-permute-done((bf16[128,640]{1,0:T(8,128)(2,1)S(1)}, bf16[128,640]{1,0:T(8,128)(2,1)S(1)}, u32[]{:S(2)}, u32[]{:S(2)}) %collective-permute-start.5) | collective-permute-done | bytes 163872 | tf_op jit(solution)/shard_map/ppermute | solution.py:246
  58.4 1.3 collective-permute-start.7
  59.7 2.0 %collective-permute-start.6 = (bf16[128,640]{1,0:T(8,128)(2,1)S(1)}, bf16[128,640]{1,0:T(8,128)(2,1)}, u32[]{:S(2)}, u32[]{:S(2)}) collective-permute-start(bf16[128,640]{1,0:T(8,128)(2,1)S(1)} %broadcast_select_fusion), channel_id=1, source_target_pairs={{0,32},{96,128},{192,224},{288,320},{384,416},{1,33},{97,129},{193... | collective-permute-start | bytes 491528 | tf_op jit(solution)/shard_map/ppermute | solution.py:255
  61.6 0.3 collective-permute-done.7
  61.9 1.3 collective-permute-done.6
  63.2 1.0 add_select_fusion.refs_0_
  64.2 4.6 %collective-permute-start.10 = (bf16[128,640]{1,0:T(8,128)(2,1)S(1)}, bf16[128,640]{1,0:T(8,128)(2,1)S(1)}, u32[]{:S(2)}, u32[]{:S(2)}) collective-permute-start(bf16[128,640]{1,0:T(8,128)(2,1)S(1)} %add_select_fusion.refs_0_), channel_id=1, source_target_pairs={{0,24},{8,16},{16,8},{24,0},{1,25},{9,17},{17,9},{25,1},{2,26},{10... | collective-permute-start | bytes 491528 | tf_op jit(solution)/shard_map/ppermute | solution.py:260
  68.8 2.3 %collective-permute-start.9 = (bf16[128,640]{1,0:T(8,128)(2,1)S(1)}, bf16[128,640]{1,0:T(8,128)(2,1)S(1)}, u32[]{:S(2)}, u32[]{:S(2)}) collective-permute-start(bf16[128,640]{1,0:T(8,128)(2,1)S(1)} %add_select_fusion.refs_0_), channel_id=1, source_target_pairs={{0,8},{8,0},{16,24},{24,16},{1,9},{9,1},{17,25},{25,17},{2,10},{10... | collective-permute-start | bytes 491528 | tf_op jit(solution)/shard_map/ppermute | solution.py:260
  71.1 2.1 %collective-permute-start.8 = (bf16[128,640]{1,0:T(8,128)(2,1)S(1)}, bf16[128,640]{1,0:T(8,128)(2,1)}, u32[]{:S(2)}, u32[]{:S(2)}) collective-permute-start(bf16[128,640]{1,0:T(8,128)(2,1)S(1)} %add_select_fusion.refs_0_), channel_id=1, source_target_pairs={{0,16},{8,24},{16,0},{24,8},{1,17},{9,25},{17,1},{25,9},{2,18},{10... | collective-permute-start | bytes 491528 | tf_op jit(solution)/shard_map/ppermute | solution.py:260
  73.3 3.1 %collective-permute-done.9.refs_2_ = bf16[128,640]{1,0:T(8,128)(2,1)S(1)} collective-permute-done((bf16[128,640]{1,0:T(8,128)(2,1)S(1)}, bf16[128,640]{1,0:T(8,128)(2,1)S(1)}, u32[]{:S(2)}, u32[]{:S(2)}) %collective-permute-start.9) | collective-permute-done | bytes 163872 | tf_op jit(solution)/shard_map/ppermute | solution.py:260
  76.4 2.6 %collective-permute-done.8.refs_1_ = bf16[128,640]{1,0:T(8,128)(2,1)} collective-permute-done((bf16[128,640]{1,0:T(8,128)(2,1)S(1)}, bf16[128,640]{1,0:T(8,128)(2,1)}, u32[]{:S(2)}, u32[]{:S(2)}) %collective-permute-start.8) | collective-permute-done | bytes 163872 | tf_op jit(solution)/shard_map/ppermute | solution.py:260
  79.0 4.8 %shard_map.47 = bf16[32,4,1024]{2,1,0:T(4,128)(2,1)} custom-call(s32[3]{0:T(128)S(1)} %pad_add_fusion.place_ref, bf16[4,288,640]{2,1,0:T(8,128)(2,1)S(1)} %all-to-all-done.near_ref, bf16[4,288,640]{2,1,0:T(8,128)(2,1)S(1)} %collective-permute-done.1.far_ref, bf16[128,640]{1,0:T(8,128)(2,1)S(1)} %add_select_fusion.refs_0_, ...), custom_call_target="tpu_custom_call" | custom-call | flops 1509949440 | bytes 2949120 | tf_op jit(solution)/shard_map/pallas_call | solution.py:95
  83.8 12.7 %all-to-all-start.1 = ((bf16[32,4,1024]{2,1,0:T(4,128)(2,1)}), bf16[32,4,1024]{2,1,0:T(4,128)(2,1)S(1)}, u32[]{:S(2)}, u32[]{:S(2)}) async-start(bf16[32,4,1024]{2,1,0:T(4,128)(2,1)} %shard_map.47), calls=%async_computation.1 | async-start | bytes 524288 | tf_op jit(solution)/shard_map/all_to_all | solution.py:21
  96.5 18.2 %all-to-all-done.1.parts_ref = bf16[32,4,1024]{2,1,0:T(4,128)(2,1)S(1)} async-done(((bf16[32,4,1024]{2,1,0:T(4,128)(2,1)}), bf16[32,4,1024]{2,1,0:T(4,128)(2,1)S(1)}, u32[]{:S(2)}, u32[]{:S(2)}) %all-to-all-start.1) | async-done | bytes 262176 | tf_op jit(solution)/shard_map/all_to_all | solution.py:21
  114.7 0.7 shard_map.48
  115.4 9.8 %all-to-all-start.2 = ((bf16[16,4,1024]{2,1,0:T(4,128)(2,1)}), bf16[16,4,1024]{2,1,0:T(4,128)(2,1)S(1)}, u32[]{:S(2)}, u32[]{:S(2)}) async-start(bf16[16,4,1024]{2,1,0:T(4,128)(2,1)} %shard_map.48), calls=%async_computation.2 | async-start | bytes 262144 | tf_op jit(solution)/shard_map/all_to_all | solution.py:21
  125.5 7.3 %all-to-all-done.2.every_ref = bf16[16,4,1024]{2,1,0:T(4,128)(2,1)S(1)} async-done(((bf16[16,4,1024]{2,1,0:T(4,128)(2,1)}), bf16[16,4,1024]{2,1,0:T(4,128)(2,1)S(1)}, u32[]{:S(2)}, u32[]{:S(2)}) %all-to-all-start.2) | async-done | bytes 131104 | tf_op jit(solution)/shard_map/all_to_all | solution.py:21
  132.8 1.6 %shard_map.49 = f32[4,4,256]{2,1,0:T(4,128)} custom-call(s32[4,2]{1,0:T(4,128)S(1)} %copy.7.pairs_ref, s32[4]{0:T(128)S(1)} %dynamic-slice_subtract_fusion.swap_ref, bf16[16,4,1024]{2,1,0:T(4,128)(2,1)S(1)} %all-to-all-done.2.every_ref), custom_call_target="tpu_custom_call" | custom-call | flops 6553600 | bytes 262144 | tf_op jit(solution)/shard_map/pallas_call | solution.py:215
  (18 shorter events, 0.7 us)
Async XLA Ops:
  0.0 125.3 %copy-start = (s32[64,2]{0,1:T(2,128)S(1)}, s32[64,2]{0,1:T(2,128)}, u32[]{:S(2)}) copy-start(s32[64,2]{0,1:T(2,128)} %param.7) | copy-start | bytes 1540
  0.0 7.1 %collective-permute-start = (bf16[8,1024]{1,0:T(8,128)(2,1)}, bf16[8,1024]{1,0:T(8,128)(2,1)S(1)}, u32[]{:S(2)}, u32[]{:S(2)}) collective-permute-start(bf16[8,1024]{1,0:T(8,128)(2,1)} %amps_ref.1), channel_id=1, source_target_pairs={{0,8},{8,0},{1,9},{9,1},{2,10},{10,2},{3,11},{11,3},{4,12},{12,4},... | collective-permute-start | bytes 49160 | tf_op jit(solution)/shard_map/ppermute | solution.py:235
  7.1 0.7 copy-start.1
  9.1 4.2 %copy-start.2 = (bf16[8,32,640]{2,1,0:T(8,128)(2,1)S(1)}, bf16[8,32,640]{2,1,0:T(8,128)(2,1)}, u32[]{:S(2)}) copy-start(bf16[8,32,640]{2,1,0:T(8,128)(2,1)} %param.5) | copy-start | bytes 983044
  9.1 17.0 %all-to-all-start = ((bf16[4,288,640]{2,1,0:T(8,128)(2,1)}), bf16[4,288,640]{2,1,0:T(8,128)(2,1)S(1)}, u32[]{:S(2)}, u32[]{:S(2)}) async-start(bf16[4,288,640]{2,1,0:T(8,128)(2,1)} %shard_map.46), calls=%async_computation | async-start | bytes 2949120 | tf_op jit(solution)/shard_map/all_to_all | solution.py:21
  13.3 22.5 %collective-permute-start.2 = (bf16[128,640]{1,0:T(8,128)(2,1)S(1)}, bf16[128,640]{1,0:T(8,128)(2,1)S(1)}, u32[]{:S(2)}, u32[]{:S(2)}) collective-permute-start(bf16[128,640]{1,0:T(8,128)(2,1)S(1)} %bitcast.12), channel_id=1, source_target_pairs={{0,16},{1,17},{2,18},{3,19},{4,20},{5,21},{6,22},{7,23},{8,24},{9,... | collective-permute-start | bytes 491528 | tf_op jit(solution)/shard_map/ppermute | solution.py:243
  26.0 53.0 %collective-permute-start.1 = (bf16[4,288,640]{2,1,0:T(8,128)(2,1)S(1)}, bf16[4,288,640]{2,1,0:T(8,128)(2,1)S(1)}, u32[]{:S(2)}, u32[]{:S(2)}) collective-permute-start(bf16[4,288,640]{2,1,0:T(8,128)(2,1)S(1)} %all-to-all-done.near_ref), channel_id=1, source_target_pairs={{0,1},{1,0},{2,3},{3,2},{4,5},{5,4},{6,7},{7,6},{8,9},{9,8},{10,11... | collective-permute-start | bytes 4423688 | tf_op jit(solution)/shard_map/ppermute | solution.py:263
  35.8 16.0 %collective-permute-start.4 = (bf16[128,640]{1,0:T(8,128)(2,1)S(1)}, bf16[128,640]{1,0:T(8,128)(2,1)S(1)}, u32[]{:S(2)}, u32[]{:S(2)}) collective-permute-start(bf16[128,640]{1,0:T(8,128)(2,1)S(1)} %bitcast_select_fusion), channel_id=1, source_target_pairs={{0,384},{1,385},{2,386},{3,387},{4,388},{5,389},{6,390},{7,391},{8... | collective-permute-start | bytes 491528 | tf_op jit(solution)/shard_map/ppermute | solution.py:244
  48.3 4.8 %collective-permute-start.3 = (bf16[128,640]{1,0:T(8,128)(2,1)S(1)}, bf16[128,640]{1,0:T(8,128)(2,1)}, u32[]{:S(2)}, u32[]{:S(2)}) collective-permute-start(bf16[128,640]{1,0:T(8,128)(2,1)S(1)} %bitcast_select_fusion), channel_id=1, source_target_pairs={{0,96},{1,97},{2,98},{3,99},{4,100},{5,101},{6,102},{7,103},{8,104... | collective-permute-start | bytes 491528 | tf_op jit(solution)/shard_map/ppermute | solution.py:244
  54.1 4.2 %collective-permute-start.5 = (bf16[128,640]{1,0:T(8,128)(2,1)S(1)}, bf16[128,640]{1,0:T(8,128)(2,1)S(1)}, u32[]{:S(2)}, u32[]{:S(2)}) collective-permute-start(bf16[128,640]{1,0:T(8,128)(2,1)S(1)} %add_select_fusion.1), channel_id=1, source_target_pairs={{96,192},{384,288},{0,448},{97,193},{385,289},{1,449},{98,194},{38... | collective-permute-start | bytes 491528 | tf_op jit(solution)/shard_map/ppermute | solution.py:246
  58.4 3.5 %collective-permute-start.7 = (bf16[128,640]{1,0:T(8,128)(2,1)S(1)}, bf16[128,640]{1,0:T(8,128)(2,1)S(1)}, u32[]{:S(2)}, u32[]{:S(2)}) collective-permute-start(bf16[128,640]{1,0:T(8,128)(2,1)S(1)} %broadcast_select_fusion), channel_id=1, source_target_pairs={{96,64},{192,160},{288,256},{384,352},{0,480},{97,65},{193,161},{2... | collective-permute-start | bytes 491528 | tf_op jit(solution)/shard_map/ppermute | solution.py:256
  59.7 3.5 %collective-permute-start.6 = (bf16[128,640]{1,0:T(8,128)(2,1)S(1)}, bf16[128,640]{1,0:T(8,128)(2,1)}, u32[]{:S(2)}, u32[]{:S(2)}) collective-permute-start(bf16[128,640]{1,0:T(8,128)(2,1)S(1)} %broadcast_select_fusion), channel_id=1, source_target_pairs={{0,32},{96,128},{192,224},{288,320},{384,416},{1,33},{97,129},{193... | collective-permute-start | bytes 491528 | tf_op jit(solution)/shard_map/ppermute | solution.py:255
  64.2 9.2 %collective-permute-start.10 = (bf16[128,640]{1,0:T(8,128)(2,1)S(1)}, bf16[128,640]{1,0:T(8,128)(2,1)S(1)}, u32[]{:S(2)}, u32[]{:S(2)}) collective-permute-start(bf16[128,640]{1,0:T(8,128)(2,1)S(1)} %add_select_fusion.refs_0_), channel_id=1, source_target_pairs={{0,24},{8,16},{16,8},{24,0},{1,25},{9,17},{17,9},{25,1},{2,26},{10... | collective-permute-start | bytes 491528 | tf_op jit(solution)/shard_map/ppermute | solution.py:260
  68.8 7.6 %collective-permute-start.9 = (bf16[128,640]{1,0:T(8,128)(2,1)S(1)}, bf16[128,640]{1,0:T(8,128)(2,1)S(1)}, u32[]{:S(2)}, u32[]{:S(2)}) collective-permute-start(bf16[128,640]{1,0:T(8,128)(2,1)S(1)} %add_select_fusion.refs_0_), channel_id=1, source_target_pairs={{0,8},{8,0},{16,24},{24,16},{1,9},{9,1},{17,25},{25,17},{2,10},{10... | collective-permute-start | bytes 491528 | tf_op jit(solution)/shard_map/ppermute | solution.py:260
  71.1 7.9 %collective-permute-start.8 = (bf16[128,640]{1,0:T(8,128)(2,1)S(1)}, bf16[128,640]{1,0:T(8,128)(2,1)}, u32[]{:S(2)}, u32[]{:S(2)}) collective-permute-start(bf16[128,640]{1,0:T(8,128)(2,1)S(1)} %add_select_fusion.refs_0_), channel_id=1, source_target_pairs={{0,16},{8,24},{16,0},{24,8},{1,17},{9,25},{17,1},{25,9},{2,18},{10... | collective-permute-start | bytes 491528 | tf_op jit(solution)/shard_map/ppermute | solution.py:260
  73.3 52.1 %copy-start.3 = (s32[128]{0:T(128)S(1)}, s32[128]{0:T(128)}, u32[]{:S(2)}) copy-start(s32[128]{0:T(128)} %param.8) | copy-start | bytes 1540
  83.8 30.9 %all-to-all-start.1 = ((bf16[32,4,1024]{2,1,0:T(4,128)(2,1)}), bf16[32,4,1024]{2,1,0:T(4,128)(2,1)S(1)}, u32[]{:S(2)}, u32[]{:S(2)}) async-start(bf16[32,4,1024]{2,1,0:T(4,128)(2,1)} %shard_map.47), calls=%async_computation.1 | async-start | bytes 524288 | tf_op jit(solution)/shard_map/all_to_all | solution.py:21
  115.4 17.4 %all-to-all-start.2 = ((bf16[16,4,1024]{2,1,0:T(4,128)(2,1)}), bf16[16,4,1024]{2,1,0:T(4,128)(2,1)S(1)}, u32[]{:S(2)}, u32[]{:S(2)}) async-start(bf16[16,4,1024]{2,1,0:T(4,128)(2,1)} %shard_map.48), calls=%async_computation.2 | async-start | bytes 262144 | tf_op jit(solution)/shard_map/all_to_all | solution.py:21

commit v9 on v6

--- a/solution.py
+++ b/solution.py
@@ -13,8 +13,8 @@
 CONTRACT = ("z", "yl")
 OUT = ("yh", "x", "core")
 PAIR = [(0, 1), (1, 0)]
-LONG, MIDDLE = [(0, 3), (0, 13)], [(3, 6), (13, 10)]
-SENDERS = (0, 3, 6, 10, 13)
+LONG, MIDDLE = [(0, 3), (0, 12)], [(3, 6), (12, 9), (0, 14)]
+SENDERS, HOLDERS = (0, 3, 6, 9, 12), (0, 3, 6, 9, 12, 14)
 
 
 def exchange(array, axes):
@@ -92,6 +92,7 @@
     total = parts_ref[0].astype(jnp.float32)
     for k in range(1, parts_ref.shape[0]):
         total = total + parts_ref[k].astype(jnp.float32)
+    total = total.astype(out_ref.dtype)
     for o in range(out_ref.shape[0]):
         out_ref[o] = total
 
@@ -99,7 +100,7 @@
 def totals(parts, copies):
     return pl.pallas_call(
         total_kernel,
-        out_shape=jax.ShapeDtypeStruct((copies, *parts.shape[1:]), jnp.float32),
+        out_shape=jax.ShapeDtypeStruct((copies, *parts.shape[1:]), parts.dtype),
         in_specs=in_vmem(1),
         out_specs=pl.BlockSpec(memory_space=pltpu.VMEM),
         compiler_params=pltpu.CompilerParams(vmem_limit_bytes=4 * 1024 * 1024),
@@ -121,6 +122,7 @@
         found = jnp.zeros((occ, LANES), jnp.float32)
         for m in range(chunks):
             block = every_ref[holder, :, pl.ds(pl.multiple_of(first + m * LANES, LANES), LANES)]
+            block = block.astype(jnp.float32)
             shift = lax.rem((m + ring - lax.rem(a_tile, ring)) * group, LANES)
             found = jnp.where(lane_group == m, pltpu.roll(block, shift, 1), found)
         return found
@@ -135,40 +137,26 @@
                 for s in range(slots)
             ],
             axis=0,
-        )
-
-    def thirds(rows):
-        high = rows.astype(jnp.bfloat16)
-        rest = rows - high.astype(jnp.float32)
-        middle = rest.astype(jnp.bfloat16)
-        low = (rest - middle.astype(jnp.float32)).astype(jnp.bfloat16)
-        return high, middle, low
-
-    def placed(parts, spot):
+        ).astype(jnp.bfloat16)
+
+    def placed(rows, spot):
         column = lax.broadcasted_iota(jnp.int32, (width, width), 1)
         chosen = (column == spot).astype(jnp.float32).astype(jnp.bfloat16)
-        found = jnp.dot(
-            jnp.concatenate(parts, axis=0), chosen, preferred_element_type=jnp.float32
-        )
-        high, middle, low = (found[n * slots * occ : (n + 1) * slots * occ] for n in range(3))
-        return high + middle + low
+        return jnp.dot(rows, chosen, preferred_element_type=jnp.float32)
 
     lane = lax.broadcasted_iota(jnp.int32, (width, width), 0)
     core_b = lane // LANES
     core_a = lax.rem(lane // (group // 2) + core_b, 2)
     a = core_a * (TS // 2) + lax.rem(lane, TS // 2)
     b = core_b * (TS // 2) + lax.rem(lane, LANES) // group * 2 + lax.rem(lane // (TS // 2), 2)
-    straight = placed(thirds(tiles(0)), a * TS + b)
+    straight = placed(tiles(0), a * TS + b)
     row = lax.broadcasted_iota(jnp.int32, (slots * occ, slots * occ), 0)
     column = lax.broadcasted_iota(jnp.int32, (slots * occ, slots * occ), 1)
     source = row // occ * occ
     for i in range(occ):
         source = source + jnp.where(lax.rem(row, occ) == i, swap_ref[i], 0)
     chosen = (column == source).astype(jnp.float32).astype(jnp.bfloat16)
-    swapped = [
-        jnp.dot(chosen, part, preferred_element_type=jnp.float32).astype(jnp.bfloat16)
-        for part in thirds(tiles(1))
-    ]
+    swapped = jnp.dot(chosen, tiles(1), preferred_element_type=jnp.float32).astype(jnp.bfloat16)
     total = straight + placed(swapped, b * TS + a)
     for s in range(slots):
         out_ref[s] = total[s * occ : (s + 1) * occ]
@@ -214,15 +202,15 @@
     piece = jnp.where(functools.reduce(jnp.logical_or, [z == to for _, to in MIDDLE]), got, piece)
     reach = {}
     for to in range(depth_z):
-        if to not in SENDERS:
+        if to not in HOLDERS:
             steps = [((to - at + depth_z // 2) % depth_z - depth_z // 2, at) for at in SENDERS]
             step, at = min(steps, key=lambda pair: abs(pair[0]))
             reach.setdefault(step, []).append((at, to))
     steps = sorted(reach, key=abs, reverse=True)
     got = lax.ppermute(piece, "z", reach[steps[0]])
     got = sum((lax.ppermute(piece, "z", reach[step]) for step in steps[1:]), got)
-    sender = functools.reduce(jnp.logical_or, [z == at for at in SENDERS])
-    piece = jnp.where(sender, piece, got)
+    holder = functools.reduce(jnp.logical_or, [z == at for at in HOLDERS])
+    piece = jnp.where(holder, piece, got)
     right = sent_to_all(piece, ("yh", "yl")).reshape(-1, p_size)
 
     near = jnp.stack(near, axis=0)

time: 132 us -> 131 us (level)
  blocking collectives: 34 us -> 0 us
  waiting for transfers between devices: 30.5 us -> 52.5 us
  starting transfers between devices: 55.7 us -> 66.8 us
    all_to_all x1 -> x0, blocking collectives: 34 us -> none  [exchange(): return lax.all_to_all(array, axes, 0, 0, tiled=True)]
    all_to_all x3 -> x4, waiting for transfers between devices: 26.4 us -> 45.3 us  [exchange(): return lax.all_to_all(array, axes, 0, 0, tiled=True)]
    all_to_all x3 -> x4, starting transfers between devices: 17.2 us -> 28.1 us  [exchange(): return lax.all_to_all(array, axes, 0, 0, tiled=True)]
    ppermute x2 -> x1, starting transfers between devices: 9.89 us -> 1.3 us  [on_device(): lax.ppermute(piece, 'z', reach[step])]
    ppermute x1, starting transfers between devices: 0.67 us -> 9.03 us  [on_device(): got = lax.ppermute(piece, 'z', MIDDLE)]
    ppermute x1, waiting for transfers between devices: 0.01 us -> 3.5 us  [on_device(): got = lax.ppermute(piece, 'z', MIDDLE)]
  transfers between devices with their start and end apart: 14 -> 14, of which waited for: 4 -> 6; matrix products, arithmetic and copies ran while one was open for 3% -> 3% of each run, Pallas kernels for 0% -> 0%
where the time goes in v9:
time: 131 us; the launch traced here: 130 us
  starting transfers between devices  66.8 us (51%)
  waiting for transfers between devices  52.5 us (40%)
  Pallas kernels  5.98 us (5%)
  local copies, waits for them, and re-layouts  3.93 us (3%)
    all_to_all x4, waiting for transfers between devices, exchange(): return lax.all_to_all(array, axes, 0, 0, tiled=True)  45.3 us
    all_to_all x4, starting transfers between devices, exchange(): return lax.all_to_all(array, axes, 0, 0, tiled=True)  28.1 us
    ppermute x2, starting transfers between devices, on_device(): got = sum((lax.ppermute(piece, 'z', [hop]) for hop in LONG))  11.2 us
    ppermute x3, starting transfers between devices, on_device(): lax.ppermute(rows, 'x', [(x, (x + shift) % ring) for x in range(ring)])  9.33 us
    ppermute x1, starting transfers between devices, on_device(): got = lax.ppermute(piece, 'z', MIDDLE)  9.03 us
    ppermute x1, starting transfers between devices, on_device(): lax.ppermute(window[1], CONTRACT, [(0, 1)])  4.03 us
    pallas_call x1, Pallas kernels, ladder_partials(): pl.pallas_call(ladder_kernel, out_shape=jax.ShapeDtypeStruct((con_count,...  3.71 us
    ppermute x3, waiting for transfers between devices, on_device(): lax.ppermute(rows, 'x', [(x, (x + shift) % ring) for x in range(ring)])  3.71 us
  transfers between devices with their start and end apart: 14, of which 6 were waited for; matrix products, arithmetic and copies ran while one was open for 3% of the time, Pallas kernels for 0%

profile of v9, /device:TPU:1, one launch (start us, length us, event | category | flops | bytes accessed | tf_op | source)
XLA Modules:
  0.0 129.8 jit_solution(6850267828071139807)
XLA Ops:
  0.0 1.0 fusion
  1.0 4.0 %collective-permute-start.4 = (bf16[128,640]{1,0:T(8,128)(2,1)S(1)}, bf16[128,640]{1,0:T(8,128)(2,1)S(1)}, u32[]{:S(2)}, u32[]{:S(2)}) collective-permute-start(bf16[128,640]{1,0:T(8,128)(2,1)S(1)} %bitcast.25), channel_id=1, source_target_pairs={{0,16},{1,17},{2,18},{3,19},{4,20},{5,21},{6,22},{7,23},{8,24},{9,... | collective-permute-start | bytes 491528 | tf_op jit(solution)/shard_map/ppermute | solution.py:198
  5.1 1.1 copy.6
  6.2 4.4 %collective-permute-start.2 = (bf16[256,640]{1,0:T(8,128)(2,1)S(1)}, bf16[256,640]{1,0:T(8,128)(2,1)S(1)}, u32[]{:S(2)}, u32[]{:S(2)}) collective-permute-start(bf16[256,640]{1,0:T(8,128)(2,1)S(1)} %bitcast.17), channel_id=1, source_target_pairs={{0,6},{2,0},{4,2},{6,4},{1,7},{3,1},{5,3},{7,5},{8,14},{10,8},{12,... | collective-permute-start | bytes 983048 | tf_op jit(solution)/shard_map/ppermute | solution.py:190
  10.6 2.4 %collective-permute-start.1 = (bf16[256,640]{1,0:T(8,128)(2,1)S(1)}, bf16[256,640]{1,0:T(8,128)(2,1)S(1)}, u32[]{:S(2)}, u32[]{:S(2)}) collective-permute-start(bf16[256,640]{1,0:T(8,128)(2,1)S(1)} %bitcast.18), channel_id=1, source_target_pairs={{0,4},{2,6},{4,0},{6,2},{1,5},{3,7},{5,1},{7,3},{8,12},{10,14},{12... | collective-permute-start | bytes 983048 | tf_op jit(solution)/shard_map/ppermute | solution.py:190
  13.0 2.5 %collective-permute-start = (bf16[256,640]{1,0:T(8,128)(2,1)S(1)}, bf16[256,640]{1,0:T(8,128)(2,1)S(1)}, u32[]{:S(2)}, u32[]{:S(2)}) collective-permute-start(bf16[256,640]{1,0:T(8,128)(2,1)S(1)} %bitcast.19), channel_id=1, source_target_pairs={{0,2},{2,4},{4,6},{6,0},{1,3},{3,5},{5,7},{7,1},{8,10},{10,12},{12... | collective-permute-start | bytes 983048 | tf_op jit(solution)/shard_map/ppermute | solution.py:190
  15.6 9.9 %collective-permute-start.6 = (bf16[128,640]{1,0:T(8,128)(2,1)S(1)}, bf16[128,640]{1,0:T(8,128)(2,1)S(1)}, u32[]{:S(2)}, u32[]{:S(2)}) collective-permute-start(bf16[128,640]{1,0:T(8,128)(2,1)S(1)} %bitcast_select_fusion), channel_id=1, source_target_pairs={{0,384},{1,385},{2,386},{3,387},{4,388},{5,389},{6,390},{7,391},{8... | collective-permute-start | bytes 491528 | tf_op jit(solution)/shard_map/ppermute | solution.py:199
  25.5 1.3 %collective-permute-start.5 = (bf16[128,640]{1,0:T(8,128)(2,1)S(1)}, bf16[128,640]{1,0:T(8,128)(2,1)S(1)}, u32[]{:S(2)}, u32[]{:S(2)}) collective-permute-start(bf16[128,640]{1,0:T(8,128)(2,1)S(1)} %bitcast_select_fusion), channel_id=1, source_target_pairs={{0,96},{1,97},{2,98},{3,99},{4,100},{5,101},{6,102},{7,103},{8,104... | collective-permute-start | bytes 491528 | tf_op jit(solution)/shard_map/ppermute | solution.py:199
  26.8 0.0 collective-permute-done.2
  26.8 3.7 %collective-permute-done = bf16[256,640]{1,0:T(8,128)(2,1)S(1)} collective-permute-done((bf16[256,640]{1,0:T(8,128)(2,1)S(1)}, bf16[256,640]{1,0:T(8,128)(2,1)S(1)}, u32[]{:S(2)}, u32[]{:S(2)}) %collective-permute-start) | collective-permute-done | bytes 327712 | tf_op jit(solution)/shard_map/ppermute | solution.py:190
  30.5 0.2 pad_maximum_fusion.near_ref
  30.7 2.5 %collective-permute-start.3 = (bf16[4,256,640]{2,1,0:T(8,128)(2,1)S(1)}, bf16[4,256,640]{2,1,0:T(8,128)(2,1)S(1)}, u32[]{:S(2)}, u32[]{:S(2)}) collective-permute-start(bf16[4,256,640]{2,1,0:T(8,128)(2,1)S(1)} %pad_maximum_fusion.near_ref), channel_id=1, source_target_pairs={{0,1},{1,0},{2,3},{3,2},{4,5},{5,4},{6,7},{7,6},{8,9},{9,8},{10,11... | collective-permute-start | bytes 3932168 | tf_op jit(solution)/shard_map/ppermute | solution.py:217
  33.3 9.0 %collective-permute-start.7 = (bf16[128,640]{1,0:T(8,128)(2,1)S(1)}, bf16[128,640]{1,0:T(8,128)(2,1)S(1)}, u32[]{:S(2)}, u32[]{:S(2)}) collective-permute-start(bf16[128,640]{1,0:T(8,128)(2,1)S(1)} %add_select_fusion.1), channel_id=1, source_target_pairs={{96,192},{384,288},{0,448},{97,193},{385,289},{1,449},{98,194},{38... | collective-permute-start | bytes 491528 | tf_op jit(solution)/shard_map/ppermute | solution.py:201
  42.3 3.5 %collective-permute-done.7 = bf16[128,640]{1,0:T(8,128)(2,1)S(1)} collective-permute-done((bf16[128,640]{1,0:T(8,128)(2,1)S(1)}, bf16[128,640]{1,0:T(8,128)(2,1)S(1)}, u32[]{:S(2)}, u32[]{:S(2)}) %collective-permute-start.7) | collective-permute-done | bytes 163872 | tf_op jit(solution)/shard_map/ppermute | solution.py:201
  45.9 1.3 %collective-permute-start.9 = (bf16[128,640]{1,0:T(8,128)(2,1)S(1)}, bf16[128,640]{1,0:T(8,128)(2,1)S(1)}, u32[]{:S(2)}, u32[]{:S(2)}) collective-permute-start(bf16[128,640]{1,0:T(8,128)(2,1)S(1)} %broadcast_select_fusion), channel_id=1, source_target_pairs={{96,64},{192,160},{288,256},{384,352},{0,480},{97,65},{193,161},{2... | collective-permute-start | bytes 491528 | tf_op jit(solution)/shard_map/ppermute | solution.py:211
  47.2 1.3 %collective-permute-start.8 = (bf16[128,640]{1,0:T(8,128)(2,1)S(1)}, bf16[128,640]{1,0:T(8,128)(2,1)S(1)}, u32[]{:S(2)}, u32[]{:S(2)}) collective-permute-start(bf16[128,640]{1,0:T(8,128)(2,1)S(1)} %broadcast_select_fusion), channel_id=1, source_target_pairs={{0,32},{96,128},{192,224},{288,320},{384,416},{1,33},{97,129},{193... | collective-permute-start | bytes 491528 | tf_op jit(solution)/shard_map/ppermute | solution.py:210
  48.5 0.7 broadcast_in_dim.4
  49.2 5.6 %all-to-all-start = ((bf16[16,8,1024]{2,1,0:T(8,128)(2,1)}), bf16[16,8,1024]{2,1,0:T(8,128)(2,1)S(1)}, u32[]{:S(2)}, u32[]{:S(2)}) async-start(bf16[16,8,1024]{2,1,0:T(8,128)(2,1)} %broadcast_in_dim.4), calls=%async_computation | async-start | bytes 524288 | tf_op jit(solution)/shard_map/all_to_all | solution.py:21
  54.9 8.6 %all-to-all-done = bf16[16,8,1024]{2,1,0:T(8,128)(2,1)S(1)} async-done(((bf16[16,8,1024]{2,1,0:T(8,128)(2,1)}), bf16[16,8,1024]{2,1,0:T(8,128)(2,1)S(1)}, u32[]{:S(2)}, u32[]{:S(2)}) %all-to-all-start) | async-done | bytes 262176 | tf_op jit(solution)/shard_map/all_to_all | solution.py:21
  63.5 0.9 broadcast_in_dim.5
  64.4 3.5 %all-to-all-start.1 = ((bf16[4,128,640]{2,1,0:T(8,128)(2,1)}), bf16[4,128,640]{2,1,0:T(8,128)(2,1)S(1)}, u32[]{:S(2)}, u32[]{:S(2)}) async-start(bf16[4,128,640]{2,1,0:T(8,128)(2,1)} %broadcast_in_dim.5), calls=%async_computation.1 | async-start | bytes 1310720 | tf_op jit(solution)/shard_map/all_to_all | solution.py:21
  67.9 10.2 %all-to-all-done.1 = bf16[4,128,640]{2,1,0:T(8,128)(2,1)S(1)} async-done(((bf16[4,128,640]{2,1,0:T(8,128)(2,1)}), bf16[4,128,640]{2,1,0:T(8,128)(2,1)S(1)}, u32[]{:S(2)}, u32[]{:S(2)}) %all-to-all-start.1) | async-done | bytes 655392 | tf_op jit(solution)/shard_map/all_to_all | solution.py:21
  78.1 3.7 %shard_map.46 = bf16[32,4,1024]{2,1,0:T(4,128)(2,1)} custom-call(s32[1]{0:T(128)} %bitcast.place_ref, bf16[4,256,640]{2,1,0:T(8,128)(2,1)S(1)} %pad_maximum_fusion.near_ref, bf16[4,256,640]{2,1,0:T(8,128)(2,1)S(1)} %collective-permute-done.3.far_ref, bf16[128,1024]{1,0:T(8,128)(2,1)S(1)} %bitcast.16, bf16[512,640]{1,0:T(8,128)(2,1)S(1)} %bitcast.15), custom_call_target="tpu_custom_call" | custom-call | flops 1342177280 | bytes 2621440 | tf_op jit(solution)/shard_map/pallas_call | solution.py:76
  81.8 10.3 %all-to-all-start.2 = ((bf16[32,4,1024]{2,1,0:T(4,128)(2,1)}), bf16[32,4,1024]{2,1,0:T(4,128)(2,1)S(1)}, u32[]{:S(2)}, u32[]{:S(2)}) async-start(bf16[32,4,1024]{2,1,0:T(4,128)(2,1)} %shard_map.46), calls=%async_computation.2 | async-start | bytes 524288 | tf_op jit(solution)/shard_map/all_to_all | solution.py:21
  92.1 19.1 %all-to-all-done.2.parts_ref = bf16[32,4,1024]{2,1,0:T(4,128)(2,1)S(1)} async-done(((bf16[32,4,1024]{2,1,0:T(4,128)(2,1)}), bf16[32,4,1024]{2,1,0:T(4,128)(2,1)S(1)}, u32[]{:S(2)}, u32[]{:S(2)}) %all-to-all-start.2) | async-done | bytes 262176 | tf_op jit(solution)/shard_map/all_to_all | solution.py:21
  111.3 0.7 shard_map.47
  112.0 8.7 %all-to-all-start.3 = ((bf16[16,4,1024]{2,1,0:T(4,128)(2,1)}), bf16[16,4,1024]{2,1,0:T(4,128)(2,1)S(1)}, u32[]{:S(2)}, u32[]{:S(2)}) async-start(bf16[16,4,1024]{2,1,0:T(4,128)(2,1)} %shard_map.47), calls=%async_computation.3 | async-start | bytes 262144 | tf_op jit(solution)/shard_map/all_to_all | solution.py:21
  120.7 0.1 constant_dynamic-slice_fusion
  120.8 0.1 copy.7.pairs_ref
  120.9 0.1 dynamic-slice_subtract_fusion.swap_ref
  121.0 7.3 %all-to-all-done.3.every_ref = bf16[16,4,1024]{2,1,0:T(4,128)(2,1)S(1)} async-done(((bf16[16,4,1024]{2,1,0:T(4,128)(2,1)}), bf16[16,4,1024]{2,1,0:T(4,128)(2,1)S(1)}, u32[]{:S(2)}, u32[]{:S(2)}) %all-to-all-start.3) | async-done | bytes 131104 | tf_op jit(solution)/shard_map/all_to_all | solution.py:21
  128.3 1.6 %shard_map.48 = f32[4,4,256]{2,1,0:T(4,128)} custom-call(s32[4,2]{1,0:T(4,128)S(1)} %copy.7.pairs_ref, s32[4]{0:T(128)S(1)} %dynamic-slice_subtract_fusion.swap_ref, bf16[16,4,1024]{2,1,0:T(4,128)(2,1)S(1)} %all-to-all-done.3.every_ref), custom_call_target="tpu_custom_call" | custom-call | flops 6553600 | bytes 262144 | tf_op jit(solution)/shard_map/pallas_call | solution.py:167
  (17 shorter events, 0.2 us)
Async XLA Ops:
  0.0 120.7 %copy-start = (s32[64,2]{0,1:T(2,128)S(1)}, s32[64,2]{0,1:T(2,128)}, u32[]{:S(2)}) copy-start(s32[64,2]{0,1:T(2,128)} %param.7) | copy-start | bytes 1540
  1.0 14.5 %collective-permute-start.4 = (bf16[128,640]{1,0:T(8,128)(2,1)S(1)}, bf16[128,640]{1,0:T(8,128)(2,1)S(1)}, u32[]{:S(2)}, u32[]{:S(2)}) collective-permute-start(bf16[128,640]{1,0:T(8,128)(2,1)S(1)} %bitcast.25), channel_id=1, source_target_pairs={{0,16},{1,17},{2,18},{3,19},{4,20},{5,21},{6,22},{7,23},{8,24},{9,... | collective-permute-start | bytes 491528 | tf_op jit(solution)/shard_map/ppermute | solution.py:198
  6.2 20.7 %collective-permute-start.2 = (bf16[256,640]{1,0:T(8,128)(2,1)S(1)}, bf16[256,640]{1,0:T(8,128)(2,1)S(1)}, u32[]{:S(2)}, u32[]{:S(2)}) collective-permute-start(bf16[256,640]{1,0:T(8,128)(2,1)S(1)} %bitcast.17), channel_id=1, source_target_pairs={{0,6},{2,0},{4,2},{6,4},{1,7},{3,1},{5,3},{7,5},{8,14},{10,8},{12,... | collective-permute-start | bytes 983048 | tf_op jit(solution)/shard_map/ppermute | solution.py:190
  10.6 16.3 %collective-permute-start.1 = (bf16[256,640]{1,0:T(8,128)(2,1)S(1)}, bf16[256,640]{1,0:T(8,128)(2,1)S(1)}, u32[]{:S(2)}, u32[]{:S(2)}) collective-permute-start(bf16[256,640]{1,0:T(8,128)(2,1)S(1)} %bitcast.18), channel_id=1, source_target_pairs={{0,4},{2,6},{4,0},{6,2},{1,5},{3,7},{5,1},{7,3},{8,12},{10,14},{12... | collective-permute-start | bytes 983048 | tf_op jit(solution)/shard_map/ppermute | solution.py:190
  13.0 17.6 %collective-permute-start = (bf16[256,640]{1,0:T(8,128)(2,1)S(1)}, bf16[256,640]{1,0:T(8,128)(2,1)S(1)}, u32[]{:S(2)}, u32[]{:S(2)}) collective-permute-start(bf16[256,640]{1,0:T(8,128)(2,1)S(1)} %bitcast.19), channel_id=1, source_target_pairs={{0,2},{2,4},{4,6},{6,0},{1,3},{3,5},{5,7},{7,1},{8,10},{10,12},{12... | collective-permute-start | bytes 983048 | tf_op jit(solution)/shard_map/ppermute | solution.py:190
  15.6 17.6 %collective-permute-start.6 = (bf16[128,640]{1,0:T(8,128)(2,1)S(1)}, bf16[128,640]{1,0:T(8,128)(2,1)S(1)}, u32[]{:S(2)}, u32[]{:S(2)}) collective-permute-start(bf16[128,640]{1,0:T(8,128)(2,1)S(1)} %bitcast_select_fusion), channel_id=1, source_target_pairs={{0,384},{1,385},{2,386},{3,387},{4,388},{5,389},{6,390},{7,391},{8... | collective-permute-start | bytes 491528 | tf_op jit(solution)/shard_map/ppermute | solution.py:199
  25.5 7.7 %collective-permute-start.5 = (bf16[128,640]{1,0:T(8,128)(2,1)S(1)}, bf16[128,640]{1,0:T(8,128)(2,1)S(1)}, u32[]{:S(2)}, u32[]{:S(2)}) collective-permute-start(bf16[128,640]{1,0:T(8,128)(2,1)S(1)} %bitcast_select_fusion), channel_id=1, source_target_pairs={{0,96},{1,97},{2,98},{3,99},{4,100},{5,101},{6,102},{7,103},{8,104... | collective-permute-start | bytes 491528 | tf_op jit(solution)/shard_map/ppermute | solution.py:199
  30.5 17.9 %copy-start.1 = (bf16[8,1024]{1,0:T(8,128)(2,1)S(1)}, bf16[8,1024]{1,0:T(8,128)(2,1)}, u32[]{:S(2)}) copy-start(bf16[8,1024]{1,0:T(8,128)(2,1)} %param.6) | copy-start | bytes 49156
  30.7 47.4 %collective-permute-start.3 = (bf16[4,256,640]{2,1,0:T(8,128)(2,1)S(1)}, bf16[4,256,640]{2,1,0:T(8,128)(2,1)S(1)}, u32[]{:S(2)}, u32[]{:S(2)}) collective-permute-start(bf16[4,256,640]{2,1,0:T(8,128)(2,1)S(1)} %pad_maximum_fusion.near_ref), channel_id=1, source_target_pairs={{0,1},{1,0},{2,3},{3,2},{4,5},{5,4},{6,7},{7,6},{8,9},{9,8},{10,11... | collective-permute-start | bytes 3932168 | tf_op jit(solution)/shard_map/ppermute | solution.py:217
  33.3 12.6 %collective-permute-start.7 = (bf16[128,640]{1,0:T(8,128)(2,1)S(1)}, bf16[128,640]{1,0:T(8,128)(2,1)S(1)}, u32[]{:S(2)}, u32[]{:S(2)}) collective-permute-start(bf16[128,640]{1,0:T(8,128)(2,1)S(1)} %add_select_fusion.1), channel_id=1, source_target_pairs={{96,192},{384,288},{0,448},{97,193},{385,289},{1,449},{98,194},{38... | collective-permute-start | bytes 491528 | tf_op jit(solution)/shard_map/ppermute | solution.py:201
  45.9 8.9 %collective-permute-start.9 = (bf16[128,640]{1,0:T(8,128)(2,1)S(1)}, bf16[128,640]{1,0:T(8,128)(2,1)S(1)}, u32[]{:S(2)}, u32[]{:S(2)}) collective-permute-start(bf16[128,640]{1,0:T(8,128)(2,1)S(1)} %broadcast_select_fusion), channel_id=1, source_target_pairs={{96,64},{192,160},{288,256},{384,352},{0,480},{97,65},{193,161},{2... | collective-permute-start | bytes 491528 | tf_op jit(solution)/shard_map/ppermute | solution.py:211
  47.2 7.6 %collective-permute-start.8 = (bf16[128,640]{1,0:T(8,128)(2,1)S(1)}, bf16[128,640]{1,0:T(8,128)(2,1)S(1)}, u32[]{:S(2)}, u32[]{:S(2)}) collective-permute-start(bf16[128,640]{1,0:T(8,128)(2,1)S(1)} %broadcast_select_fusion), channel_id=1, source_target_pairs={{0,32},{96,128},{192,224},{288,320},{384,416},{1,33},{97,129},{193... | collective-permute-start | bytes 491528 | tf_op jit(solution)/shard_map/ppermute | solution.py:210
  49.2 14.3 %all-to-all-start = ((bf16[16,8,1024]{2,1,0:T(8,128)(2,1)}), bf16[16,8,1024]{2,1,0:T(8,128)(2,1)S(1)}, u32[]{:S(2)}, u32[]{:S(2)}) async-start(bf16[16,8,1024]{2,1,0:T(8,128)(2,1)} %broadcast_in_dim.4), calls=%async_computation | async-start | bytes 524288 | tf_op jit(solution)/shard_map/all_to_all | solution.py:21
  64.4 13.7 %all-to-all-start.1 = ((bf16[4,128,640]{2,1,0:T(8,128)(2,1)}), bf16[4,128,640]{2,1,0:T(8,128)(2,1)S(1)}, u32[]{:S(2)}, u32[]{:S(2)}) async-start(bf16[4,128,640]{2,1,0:T(8,128)(2,1)} %broadcast_in_dim.5), calls=%async_computation.1 | async-start | bytes 1310720 | tf_op jit(solution)/shard_map/all_to_all | solution.py:21
  78.1 42.8 %copy-start.2 = (s32[128]{0:T(128)S(1)}, s32[128]{0:T(128)}, u32[]{:S(2)}) copy-start(s32[128]{0:T(128)} %param.8) | copy-start | bytes 1540
  81.8 29.4 %all-to-all-start.2 = ((bf16[32,4,1024]{2,1,0:T(4,128)(2,1)}), bf16[32,4,1024]{2,1,0:T(4,128)(2,1)S(1)}, u32[]{:S(2)}, u32[]{:S(2)}) async-start(bf16[32,4,1024]{2,1,0:T(4,128)(2,1)} %shard_map.46), calls=%async_computation.2 | async-start | bytes 524288 | tf_op jit(solution)/shard_map/all_to_all | solution.py:21
  112.0 16.3 %all-to-all-start.3 = ((bf16[16,4,1024]{2,1,0:T(4,128)(2,1)}), bf16[16,4,1024]{2,1,0:T(4,128)(2,1)S(1)}, u32[]{:S(2)}, u32[]{:S(2)}) async-start(bf16[16,4,1024]{2,1,0:T(4,128)(2,1)} %shard_map.47), calls=%async_computation.3 | async-start | bytes 262144 | tf_op jit(solution)/shard_map/all_to_all | solution.py:21

commit v10 on v7

--- a/solution.py
+++ b/solution.py
@@ -22,16 +22,27 @@
 
 
 def ladder_kernel(place_ref, near_ref, far_ref, *refs):
-    *quarter_refs, out_ref, stack_ref, right_ref, amps_ref = refs
+    *quarter_refs, last_ref, out_ref, stack_ref, right_ref, amps_ref, landing_ref, landed = refs
     core, yh, own = place_ref[0], place_ref[1], place_ref[2]
-    size = quarter_refs[0].shape[0]
-    for q, ref in enumerate(quarter_refs):
-        right_ref[pl.ds(pl.multiple_of((own ^ q) * size, size), size), :] = ref[...]
+    landing = pltpu.make_async_copy(last_ref, landing_ref, landed)
+    landing.start()
     b_count, depth, _ = stack_ref.shape
     ring, pair_rows = near_ref.shape[0], b_count
     c_pairs = near_ref.shape[1] // pair_rows - 2
     a_dev = pair_rows // 2
     d_count = right_ref.shape[0] // b_count
+    for m in range(2):
+        for rc, ref in enumerate((near_ref, far_ref)):
+            for x in range(ring):
+                place = (lax.rem(yh + m, 2) * ring + x) * 2 + lax.rem(core + rc, 2)
+                first = (c_pairs + m) * pair_rows
+                block = ref[x, first : first + pair_rows, :depth].astype(jnp.float32)
+                for g in range(2):
+                    amps_ref[g, place] = block[g * a_dev : (g + 1) * a_dev]
+    landing.wait()
+    size = landing_ref.shape[0]
+    for q, ref in enumerate((*quarter_refs, landing_ref)):
+        right_ref[pl.ds(pl.multiple_of((own ^ q) * size, size), size), :] = ref[...]
     right = right_ref[...]
     for n in range(0, c_pairs, 2):
         left = jnp.concatenate(
@@ -50,14 +61,6 @@
         for h in range(2):
             rows = (n + h) * d_count
             stack_ref[:, rows : rows + d_count, :] = part[:, :, h * LANES : (h + 1) * LANES]
-    for m in range(2):
-        for rc, ref in enumerate((near_ref, far_ref)):
-            for x in range(ring):
-                place = (lax.rem(yh + m, 2) * ring + x) * 2 + lax.rem(core + rc, 2)
-                first = (c_pairs + m) * pair_rows
-                block = ref[x, first : first + pair_rows, :depth].astype(jnp.float32)
-                for g in range(2):
-                    amps_ref[g, place] = block[g * a_dev : (g + 1) * a_dev]
     i_count = amps_ref.shape[1] * a_dev
     amps = amps_ref[...].reshape(2 * i_count, depth).astype(jnp.bfloat16)
     odd = lax.rem(lax.broadcasted_iota(jnp.int32, (1, LANES), 1) // a_dev, 2) == 1
@@ -86,12 +89,15 @@
         out_shape=jax.ShapeDtypeStruct(
             (con_count, i_count // con_count, b_count * LANES // 2), jnp.bfloat16
         ),
-        in_specs=[pl.BlockSpec(memory_space=pltpu.SMEM)] + in_vmem(2 + len(quarters)),
+        in_specs=[pl.BlockSpec(memory_space=pltpu.SMEM)] + in_vmem(1 + len(quarters))
+        + [pl.BlockSpec(memory_space=pl.ANY)],
         out_specs=pl.BlockSpec(memory_space=pltpu.VMEM),
         scratch_shapes=[
             pltpu.VMEM((b_count, depth, LANES), jnp.bfloat16),
             pltpu.VMEM(right, jnp.bfloat16),
             pltpu.VMEM((2, 4 * near.shape[0], b_count // 2, depth), jnp.float32),
+            pltpu.VMEM(quarters[-1].shape, jnp.bfloat16),
+            pltpu.SemaphoreType.DMA,
         ],
         compiler_params=pltpu.CompilerParams(vmem_limit_bytes=12 * 1024 * 1024),
         cost_estimate=pl.CostEstimate(
@@ -251,15 +257,16 @@
     ]
 
     far = lax.ppermute(near, "core", PAIR)
-    place = jnp.stack([lax.axis_index("core"), yh, 2 * yh + yl])
-    partial = ladder_partials(place, near, far, quarters, 2 * a_dev, i_count, con_count)
-    every = exchange(totals(exchange(partial, CONTRACT), out_count), OUT)
-
     slot_count, occ_dev = tile_pairs.shape[0] // out_count, i_count // con_count
     first = lax.axis_index(OUT) * slot_count
     pairs = lax.dynamic_slice_in_dim(tile_pairs, first, slot_count, 0)
     first = lax.axis_index(CONTRACT) * occ_dev
     swap = lax.dynamic_slice_in_dim(pair_swap, first, occ_dev, 0) - first
+    far, pairs, swap = lax.optimization_barrier((far, pairs, swap))
+    place = jnp.stack([lax.axis_index("core"), yh, 2 * yh + yl])
+    partial = ladder_partials(place, near, far, quarters, 2 * a_dev, i_count, con_count)
+    every = exchange(totals(exchange(partial, CONTRACT), out_count), OUT)
+
     return residual_tiles(pairs, swap, every, ring)
 
 

time: 140 us -> 136 us (0.971)
  blocking collectives: 0 us -> 50.5 us
  starting transfers between devices: 81.6 us -> 52.7 us
  waiting for transfers between devices: 44.7 us -> 20 us
    all_to_all x0 -> x2, blocking collectives: none -> 50.5 us  [exchange(): return lax.all_to_all(array, axes, 0, 0, tiled=True)]
    all_to_all x3 -> x1, starting transfers between devices: 35.2 us -> 4.19 us  [exchange(): return lax.all_to_all(array, axes, 0, 0, tiled=True)]
    all_to_all x3 -> x1, waiting for transfers between devices: 35 us -> 8.88 us  [exchange(): return lax.all_to_all(array, axes, 0, 0, tiled=True)]
    ppermute x3, starting transfers between devices: 9.05 us -> 10.6 us  [on_device(): lax.ppermute(piece, ('yl', 'yh'), [(at, at ^ q) for at in range(4)])]
  transfers between devices with their start and end apart: 15 -> 13, of which waited for: 10 -> 6; matrix products, arithmetic and copies ran while one was open for 3% -> 3% of each run, Pallas kernels for 0% -> 0%
where the time goes in v10:
time: 136 us; the launch traced here: 135 us
  starting transfers between devices  52.7 us (39%)
  blocking collectives  50.5 us (37%)
  waiting for transfers between devices  20 us (15%)
  Pallas kernels  7.36 us (5%)
  other arithmetic  2.22 us (2%)
  local copies, waits for them, and re-layouts  2 us (1%)
    all_to_all x2, blocking collectives, exchange(): return lax.all_to_all(array, axes, 0, 0, tiled=True)  50.5 us
    ppermute x2, starting transfers between devices, on_device(): got = sum((lax.ppermute(piece, 'z', [hop]) for hop in LONG))  13.4 us
    ppermute x3, starting transfers between devices, on_device(): lax.ppermute(piece, ('yl', 'yh'), [(at, at ^ q) for at in range(4)])  10.6 us
    ppermute x1, starting transfers between devices, on_device(): far = lax.ppermute(near, 'core', PAIR)  9.73 us
    all_to_all x1, waiting for transfers between devices, exchange(): return lax.all_to_all(array, axes, 0, 0, tiled=True)  8.88 us
    ppermute x3, waiting for transfers between devices, on_device(): lax.ppermute(piece, ('yl', 'yh'), [(at, at ^ q) for at in range(4)])  5.85 us
    ppermute x1, starting transfers between devices, on_device(): other_amps = lax.ppermute(amplitudes, 'yh', PAIR)  5.76 us
    pallas_call x1, Pallas kernels, ladder_partials(): pl.pallas_call(ladder_kernel, out_shape=jax.ShapeDtypeStruct((con_count,...  4.49 us
  transfers between devices with their start and end apart: 13, of which 6 were waited for; matrix products, arithmetic and copies ran while one was open for 3% of the time, Pallas kernels for 0%

profile of v10, /device:TPU:1, one launch (start us, length us, event | category | flops | bytes accessed | tf_op | source)
XLA Modules:
  0.0 135.0 jit_solution(2649569522904182387)
XLA Ops:
  0.0 5.8 %collective-permute-start = (bf16[8,1024]{1,0:T(8,128)(2,1)}, bf16[8,1024]{1,0:T(8,128)(2,1)S(1)}, u32[]{:S(2)}, u32[]{:S(2)}) collective-permute-start(bf16[8,1024]{1,0:T(8,128)(2,1)} %amps_ref.1), channel_id=1, source_target_pairs={{0,8},{8,0},{1,9},{9,1},{2,10},{10,2},{3,11},{11,3},{4,12},{12,4},... | collective-permute-start | bytes 49160 | tf_op jit(solution)/shard_map/ppermute | solution.py:231
  5.8 1.1 copy.5
  6.9 0.2 collective-permute-done.other_ref
  7.1 0.7 copy-done.1
  7.8 1.3 shard_map.46
  9.1 4.2 %all-to-all-start = ((bf16[4,288,640]{2,1,0:T(8,128)(2,1)}), bf16[4,288,640]{2,1,0:T(8,128)(2,1)S(1)}, u32[]{:S(2)}, u32[]{:S(2)}) async-start(bf16[4,288,640]{2,1,0:T(8,128)(2,1)} %shard_map.46), calls=%async_computation | async-start | bytes 2949120 | tf_op jit(solution)/shard_map/all_to_all | solution.py:21
  13.3 3.9 %collective-permute-start.2 = (bf16[128,640]{1,0:T(8,128)(2,1)S(1)}, bf16[128,640]{1,0:T(8,128)(2,1)}, u32[]{:S(2)}, u32[]{:S(2)}) collective-permute-start(bf16[128,640]{1,0:T(8,128)(2,1)S(1)} %bitcast.12), channel_id=1, source_target_pairs={{0,16},{1,17},{2,18},{3,19},{4,20},{5,21},{6,22},{7,23},{8,24},{9,... | collective-permute-start | bytes 491528 | tf_op jit(solution)/shard_map/ppermute | solution.py:239
  17.2 8.9 %all-to-all-done.near_ref = bf16[4,288,640]{2,1,0:T(8,128)(2,1)S(1)} async-done(((bf16[4,288,640]{2,1,0:T(8,128)(2,1)}), bf16[4,288,640]{2,1,0:T(8,128)(2,1)S(1)}, u32[]{:S(2)}, u32[]{:S(2)}) %all-to-all-start) | async-done | bytes 1474592 | tf_op jit(solution)/shard_map/all_to_all | solution.py:21
  26.0 9.7 %collective-permute-start.1 = (bf16[4,288,640]{2,1,0:T(8,128)(2,1)S(1)}, bf16[4,288,640]{2,1,0:T(8,128)(2,1)S(1)}, u32[]{:S(2)}, u32[]{:S(2)}) collective-permute-start(bf16[4,288,640]{2,1,0:T(8,128)(2,1)S(1)} %all-to-all-done.near_ref), channel_id=1, source_target_pairs={{0,1},{1,0},{2,3},{3,2},{4,5},{5,4},{6,7},{7,6},{8,9},{9,8},{10,11... | collective-permute-start | bytes 4423688 | tf_op jit(solution)/shard_map/ppermute | solution.py:259
  35.8 6.3 %collective-permute-start.3 = (bf16[128,640]{1,0:T(8,128)(2,1)S(1)}, bf16[128,640]{1,0:T(8,128)(2,1)S(1)}, u32[]{:S(2)}, u32[]{:S(2)}) collective-permute-start(bf16[128,640]{1,0:T(8,128)(2,1)S(1)} %bitcast_select_fusion), channel_id=1, source_target_pairs={{0,96},{1,97},{2,98},{3,99},{4,100},{5,101},{6,102},{7,103},{8,104... | collective-permute-start | bytes 491528 | tf_op jit(solution)/shard_map/ppermute | solution.py:240
  42.1 7.1 %collective-permute-start.4 = (bf16[128,640]{1,0:T(8,128)(2,1)S(1)}, bf16[128,640]{1,0:T(8,128)(2,1)}, u32[]{:S(2)}, u32[]{:S(2)}) collective-permute-start(bf16[128,640]{1,0:T(8,128)(2,1)S(1)} %bitcast_select_fusion), channel_id=1, source_target_pairs={{0,416},{1,417},{2,418},{3,419},{4,420},{5,421},{6,422},{7,423},{8... | collective-permute-start | bytes 491528 | tf_op jit(solution)/shard_map/ppermute | solution.py:240
  49.2 2.9 %collective-permute-done.4 = bf16[128,640]{1,0:T(8,128)(2,1)} collective-permute-done((bf16[128,640]{1,0:T(8,128)(2,1)S(1)}, bf16[128,640]{1,0:T(8,128)(2,1)}, u32[]{:S(2)}, u32[]{:S(2)}) %collective-permute-start.4) | collective-permute-done | bytes 163872 | tf_op jit(solution)/shard_map/ppermute | solution.py:240
  52.1 1.0 add_select_fusion.1
  53.0 0.7 collective-permute-start.5
  53.8 1.3 collective-permute-start.8
  55.1 1.3 collective-permute-start.6
  56.4 2.0 %collective-permute-start.7 = (bf16[128,640]{1,0:T(8,128)(2,1)S(1)}, bf16[128,640]{1,0:T(8,128)(2,1)}, u32[]{:S(2)}, u32[]{:S(2)}) collective-permute-start(bf16[128,640]{1,0:T(8,128)(2,1)S(1)} %broadcast_select_fusion), channel_id=1, source_target_pairs={{0,32},{96,128},{192,224},{320,352},{416,448},{1,33},{97,129},{193... | collective-permute-start | bytes 491528 | tf_op jit(solution)/shard_map/ppermute | solution.py:252
  58.4 0.1 constant_dynamic-slice_fusion
  58.4 2.2 %collective-permute-done.7 = bf16[128,640]{1,0:T(8,128)(2,1)} collective-permute-done((bf16[128,640]{1,0:T(8,128)(2,1)S(1)}, bf16[128,640]{1,0:T(8,128)(2,1)}, u32[]{:S(2)}, u32[]{:S(2)}) %collective-permute-start.7) | collective-permute-done | bytes 163872 | tf_op jit(solution)/shard_map/ppermute | solution.py:252
  60.6 1.0 add_select_fusion.refs_0_
  61.7 4.1 %collective-permute-start.9 = (bf16[128,640]{1,0:T(8,128)(2,1)S(1)}, bf16[128,640]{1,0:T(8,128)(2,1)S(1)}, u32[]{:S(2)}, u32[]{:S(2)}) collective-permute-start(bf16[128,640]{1,0:T(8,128)(2,1)S(1)} %add_select_fusion.refs_0_), channel_id=1, source_target_pairs={{0,16},{8,24},{16,0},{24,8},{1,17},{9,25},{17,1},{25,9},{2,18},{10... | collective-permute-start | bytes 491528 | tf_op jit(solution)/shard_map/ppermute | solution.py:256
  65.8 4.5 %collective-permute-start.10 = (bf16[128,640]{1,0:T(8,128)(2,1)S(1)}, bf16[128,640]{1,0:T(8,128)(2,1)S(1)}, u32[]{:S(2)}, u32[]{:S(2)}) collective-permute-start(bf16[128,640]{1,0:T(8,128)(2,1)S(1)} %add_select_fusion.refs_0_), channel_id=1, source_target_pairs={{0,8},{8,0},{16,24},{24,16},{1,9},{9,1},{17,25},{25,17},{2,10},{10... | collective-permute-start | bytes 491528 | tf_op jit(solution)/shard_map/ppermute | solution.py:256
  70.3 1.9 %collective-permute-start.11 = (bf16[128,640]{1,0:T(8,128)(2,1)S(1)}, bf16[128,640]{1,0:T(8,128)(2,1)}, u32[]{:S(2)}, u32[]{:S(2)}) collective-permute-start(bf16[128,640]{1,0:T(8,128)(2,1)S(1)} %add_select_fusion.refs_0_), channel_id=1, source_target_pairs={{0,24},{8,16},{16,8},{24,0},{1,25},{9,17},{17,9},{25,1},{2,26},{10... | collective-permute-start | bytes 491528 | tf_op jit(solution)/shard_map/ppermute | solution.py:256
  72.3 0.1 dynamic-slice_subtract_fusion.swap_ref
  72.3 0.1 copy.7.pairs_ref
  72.4 0.1 pad_add_fusion.place_ref
  72.5 2.9 %collective-permute-done.10.refs_2_ = bf16[128,640]{1,0:T(8,128)(2,1)S(1)} collective-permute-done((bf16[128,640]{1,0:T(8,128)(2,1)S(1)}, bf16[128,640]{1,0:T(8,128)(2,1)S(1)}, u32[]{:S(2)}, u32[]{:S(2)}) %collective-permute-start.10) | collective-permute-done | bytes 163872 | tf_op jit(solution)/shard_map/ppermute | solution.py:256
  75.4 3.0 %collective-permute-done.11.refs_3_ = bf16[128,640]{1,0:T(8,128)(2,1)} collective-permute-done((bf16[128,640]{1,0:T(8,128)(2,1)S(1)}, bf16[128,640]{1,0:T(8,128)(2,1)}, u32[]{:S(2)}, u32[]{:S(2)}) %collective-permute-start.11) | collective-permute-done | bytes 163872 | tf_op jit(solution)/shard_map/ppermute | solution.py:256
  78.4 4.5 %shard_map.47 = bf16[32,4,1024]{2,1,0:T(4,128)(2,1)S(1)} custom-call(s32[3]{0:T(128)S(1)} %pad_add_fusion.place_ref, bf16[4,288,640]{2,1,0:T(8,128)(2,1)S(1)} %all-to-all-done.near_ref, bf16[4,288,640]{2,1,0:T(8,128)(2,1)S(1)} %collective-permute-done.1.far_ref, bf16[128,640]{1,0:T(8,128)(2,1)S(1)} %add_select_fusion.refs_0_, ...), custom_call_target="tpu_custom_call" | custom-call | flops 1509949440 | bytes 2949120 | tf_op jit(solution)/shard_map/pallas_call | solution.py:87
  82.9 35.5 %all_to_all.15.parts_ref = bf16[32,4,1024]{2,1,0:T(4,128)(2,1)S(1)} all-to-all(bf16[32,4,1024]{2,1,0:T(4,128)(2,1)S(1)} %shard_map.47), channel_id=1, replica_groups=mesh['z'=16,'yl'=2,'yh'=2,'x'=4,'core'=2] {'z','yl'}, dimensions={0} | all-to-all | bytes 524288 | tf_op jit(solution)/shard_map/all_to_all | solution.py:21
  118.4 15.1 %all_to_all.16.every_ref = bf16[16,4,1024]{2,1,0:T(4,128)(2,1)S(1)} all-to-all(bf16[16,4,1024]{2,1,0:T(4,128)(2,1)S(1)} %shard_map.48), channel_id=1, replica_groups=mesh['z'=16,'yl'=2,'yh'=2,'x'=4,'core'=2] {'yh','x','core'}, dimensions={0} | all-to-all | bytes 262144 | tf_op jit(solution)/shard_map/all_to_all | solution.py:21
  133.5 1.6 %shard_map.49 = f32[4,4,256]{2,1,0:T(4,128)} custom-call(s32[4,2]{1,0:T(4,128)S(1)} %copy.7.pairs_ref, s32[4]{0:T(128)S(1)} %dynamic-slice_subtract_fusion.swap_ref, bf16[16,4,1024]{2,1,0:T(4,128)(2,1)S(1)} %all_to_all.16.every_ref), custom_call_target="tpu_custom_call" | custom-call | flops 6553600 | bytes 262144 | tf_op jit(solution)/shard_map/pallas_call | solution.py:211
  (18 shorter events, 0.2 us)
Async XLA Ops:
  0.0 58.4 %copy-start = (s32[64,2]{0,1:T(2,128)S(1)}, s32[64,2]{0,1:T(2,128)}, u32[]{:S(2)}) copy-start(s32[64,2]{0,1:T(2,128)} %param.7) | copy-start | bytes 1540
  0.0 7.1 %collective-permute-start = (bf16[8,1024]{1,0:T(8,128)(2,1)}, bf16[8,1024]{1,0:T(8,128)(2,1)S(1)}, u32[]{:S(2)}, u32[]{:S(2)}) collective-permute-start(bf16[8,1024]{1,0:T(8,128)(2,1)} %amps_ref.1), channel_id=1, source_target_pairs={{0,8},{8,0},{1,9},{9,1},{2,10},{10,2},{3,11},{11,3},{4,12},{12,4},... | collective-permute-start | bytes 49160 | tf_op jit(solution)/shard_map/ppermute | solution.py:231
  7.1 0.7 copy-start.1
  9.1 4.2 %copy-start.2 = (bf16[8,32,640]{2,1,0:T(8,128)(2,1)S(1)}, bf16[8,32,640]{2,1,0:T(8,128)(2,1)}, u32[]{:S(2)}) copy-start(bf16[8,32,640]{2,1,0:T(8,128)(2,1)} %param.5) | copy-start | bytes 983044
  9.1 17.0 %all-to-all-start = ((bf16[4,288,640]{2,1,0:T(8,128)(2,1)}), bf16[4,288,640]{2,1,0:T(8,128)(2,1)S(1)}, u32[]{:S(2)}, u32[]{:S(2)}) async-start(bf16[4,288,640]{2,1,0:T(8,128)(2,1)} %shard_map.46), calls=%async_computation | async-start | bytes 2949120 | tf_op jit(solution)/shard_map/all_to_all | solution.py:21
  13.3 59.0 %copy-start.3 = (s32[128]{0:T(128)S(1)}, s32[128]{0:T(128)}, u32[]{:S(2)}) copy-start(s32[128]{0:T(128)} %param.8) | copy-start | bytes 1540
  13.3 22.5 %collective-permute-start.2 = (bf16[128,640]{1,0:T(8,128)(2,1)S(1)}, bf16[128,640]{1,0:T(8,128)(2,1)}, u32[]{:S(2)}, u32[]{:S(2)}) collective-permute-start(bf16[128,640]{1,0:T(8,128)(2,1)S(1)} %bitcast.12), channel_id=1, source_target_pairs={{0,16},{1,17},{2,18},{3,19},{4,20},{5,21},{6,22},{7,23},{8,24},{9,... | collective-permute-start | bytes 491528 | tf_op jit(solution)/shard_map/ppermute | solution.py:239
  26.0 46.5 %collective-permute-start.1 = (bf16[4,288,640]{2,1,0:T(8,128)(2,1)S(1)}, bf16[4,288,640]{2,1,0:T(8,128)(2,1)S(1)}, u32[]{:S(2)}, u32[]{:S(2)}) collective-permute-start(bf16[4,288,640]{2,1,0:T(8,128)(2,1)S(1)} %all-to-all-done.near_ref), channel_id=1, source_target_pairs={{0,1},{1,0},{2,3},{3,2},{4,5},{5,4},{6,7},{7,6},{8,9},{9,8},{10,11... | collective-permute-start | bytes 4423688 | tf_op jit(solution)/shard_map/ppermute | solution.py:259
  35.8 13.4 %collective-permute-start.3 = (bf16[128,640]{1,0:T(8,128)(2,1)S(1)}, bf16[128,640]{1,0:T(8,128)(2,1)S(1)}, u32[]{:S(2)}, u32[]{:S(2)}) collective-permute-start(bf16[128,640]{1,0:T(8,128)(2,1)S(1)} %bitcast_select_fusion), channel_id=1, source_target_pairs={{0,96},{1,97},{2,98},{3,99},{4,100},{5,101},{6,102},{7,103},{8,104... | collective-permute-start | bytes 491528 | tf_op jit(solution)/shard_map/ppermute | solution.py:240
  42.1 10.0 %collective-permute-start.4 = (bf16[128,640]{1,0:T(8,128)(2,1)S(1)}, bf16[128,640]{1,0:T(8,128)(2,1)}, u32[]{:S(2)}, u32[]{:S(2)}) collective-permute-start(bf16[128,640]{1,0:T(8,128)(2,1)S(1)} %bitcast_select_fusion), channel_id=1, source_target_pairs={{0,416},{1,417},{2,418},{3,419},{4,420},{5,421},{6,422},{7,423},{8... | collective-permute-start | bytes 491528 | tf_op jit(solution)/shard_map/ppermute | solution.py:240
  53.0 0.7 collective-permute-start.5
  53.8 4.7 %collective-permute-start.8 = (bf16[128,640]{1,0:T(8,128)(2,1)S(1)}, bf16[128,640]{1,0:T(8,128)(2,1)S(1)}, u32[]{:S(2)}, u32[]{:S(2)}) collective-permute-start(bf16[128,640]{1,0:T(8,128)(2,1)S(1)} %broadcast_select_fusion), channel_id=1, source_target_pairs={{96,64},{192,160},{320,288},{416,384},{0,480},{97,65},{193,161},{3... | collective-permute-start | bytes 491528 | tf_op jit(solution)/shard_map/ppermute | solution.py:252
  55.1 3.4 %collective-permute-start.6 = (bf16[128,640]{1,0:T(8,128)(2,1)S(1)}, bf16[128,640]{1,0:T(8,128)(2,1)}, u32[]{:S(2)}, u32[]{:S(2)}) collective-permute-start(bf16[128,640]{1,0:T(8,128)(2,1)S(1)} %broadcast_select_fusion), channel_id=1, source_target_pairs={{192,256},{193,257},{194,258},{195,259},{196,260},{197,261},{198,2... | collective-permute-start | bytes 491528 | tf_op jit(solution)/shard_map/ppermute | solution.py:251
  56.4 4.2 %collective-permute-start.7 = (bf16[128,640]{1,0:T(8,128)(2,1)S(1)}, bf16[128,640]{1,0:T(8,128)(2,1)}, u32[]{:S(2)}, u32[]{:S(2)}) collective-permute-start(bf16[128,640]{1,0:T(8,128)(2,1)S(1)} %broadcast_select_fusion), channel_id=1, source_target_pairs={{0,32},{96,128},{192,224},{320,352},{416,448},{1,33},{97,129},{193... | collective-permute-start | bytes 491528 | tf_op jit(solution)/shard_map/ppermute | solution.py:252
  61.7 10.8 %collective-permute-start.9 = (bf16[128,640]{1,0:T(8,128)(2,1)S(1)}, bf16[128,640]{1,0:T(8,128)(2,1)S(1)}, u32[]{:S(2)}, u32[]{:S(2)}) collective-permute-start(bf16[128,640]{1,0:T(8,128)(2,1)S(1)} %add_select_fusion.refs_0_), channel_id=1, source_target_pairs={{0,16},{8,24},{16,0},{24,8},{1,17},{9,25},{17,1},{25,9},{2,18},{10... | collective-permute-start | bytes 491528 | tf_op jit(solution)/shard_map/ppermute | solution.py:256
  65.8 9.6 %collective-permute-start.10 = (bf16[128,640]{1,0:T(8,128)(2,1)S(1)}, bf16[128,640]{1,0:T(8,128)(2,1)S(1)}, u32[]{:S(2)}, u32[]{:S(2)}) collective-permute-start(bf16[128,640]{1,0:T(8,128)(2,1)S(1)} %add_select_fusion.refs_0_), channel_id=1, source_target_pairs={{0,8},{8,0},{16,24},{24,16},{1,9},{9,1},{17,25},{25,17},{2,10},{10... | collective-permute-start | bytes 491528 | tf_op jit(solution)/shard_map/ppermute | solution.py:256
  70.3 8.0 %collective-permute-start.11 = (bf16[128,640]{1,0:T(8,128)(2,1)S(1)}, bf16[128,640]{1,0:T(8,128)(2,1)}, u32[]{:S(2)}, u32[]{:S(2)}) collective-permute-start(bf16[128,640]{1,0:T(8,128)(2,1)S(1)} %add_select_fusion.refs_0_), channel_id=1, source_target_pairs={{0,24},{8,16},{16,8},{24,0},{1,25},{9,17},{17,9},{25,1},{2,26},{10... | collective-permute-start | bytes 491528 | tf_op jit(solution)/shard_map/ppermute | solution.py:256

commit v11 on v10

--- a/solution.py
+++ b/solution.py
@@ -22,7 +22,7 @@
 
 
 def ladder_kernel(place_ref, near_ref, far_ref, *refs):
-    *quarter_refs, last_ref, out_ref, stack_ref, right_ref, amps_ref, landing_ref, landed = refs
+    *quarter_refs, last_ref, out_ref, stack_ref, right_ref, amps_ref, landing_ref, rows_ref, landed = refs
     core, yh, own = place_ref[0], place_ref[1], place_ref[2]
     landing = pltpu.make_async_copy(last_ref, landing_ref, landed)
     landing.start()
@@ -39,11 +39,12 @@
                 block = ref[x, first : first + pair_rows, :depth].astype(jnp.float32)
                 for g in range(2):
                     amps_ref[g, place] = block[g * a_dev : (g + 1) * a_dev]
+    i_count = amps_ref.shape[1] * a_dev
+    rows_ref[...] = amps_ref[...].reshape(2 * i_count, depth).astype(rows_ref.dtype)
     landing.wait()
     size = landing_ref.shape[0]
     for q, ref in enumerate((*quarter_refs, landing_ref)):
         right_ref[pl.ds(pl.multiple_of((own ^ q) * size, size), size), :] = ref[...]
-    right = right_ref[...]
     for n in range(0, c_pairs, 2):
         left = jnp.concatenate(
             [
@@ -55,20 +56,18 @@
             axis=0,
         )
         part = lax.dot_general(
-            right, left, (((1,), (1,)), ((), ())), preferred_element_type=jnp.float32
+            right_ref[...], left, (((1,), (1,)), ((), ())), preferred_element_type=jnp.float32
         ).astype(jnp.bfloat16)
         part = part.reshape(b_count, d_count, 2 * LANES)
         for h in range(2):
             rows = (n + h) * d_count
             stack_ref[:, rows : rows + d_count, :] = part[:, :, h * LANES : (h + 1) * LANES]
-    i_count = amps_ref.shape[1] * a_dev
-    amps = amps_ref[...].reshape(2 * i_count, depth).astype(jnp.bfloat16)
     odd = lax.rem(lax.broadcasted_iota(jnp.int32, (1, LANES), 1) // a_dev, 2) == 1
     rows = out_ref.shape[1]
     for q in range(b_count // 2):
         sums = []
         for b, step in ((2 * q, LANES - a_dev), (2 * q + 1, a_dev)):
-            full = jnp.dot(amps, stack_ref[b], preferred_element_type=jnp.float32)
+            full = jnp.dot(rows_ref[...], stack_ref[b], preferred_element_type=jnp.float32)
             mixed = jnp.where(odd, full[i_count:], full[:i_count])
             sums.append(mixed + pltpu.roll(mixed, step, 1))
         found = jnp.where(odd, sums[1], sums[0]).astype(out_ref.dtype)
@@ -97,6 +96,7 @@
             pltpu.VMEM(right, jnp.bfloat16),
             pltpu.VMEM((2, 4 * near.shape[0], b_count // 2, depth), jnp.float32),
             pltpu.VMEM(quarters[-1].shape, jnp.bfloat16),
+            pltpu.VMEM((2 * i_count, depth), jnp.bfloat16),
             pltpu.SemaphoreType.DMA,
         ],
         compiler_params=pltpu.CompilerParams(vmem_limit_bytes=12 * 1024 * 1024),

time: 136 us -> 136 us (level)
  no operation moved by 1% of the time
where the time goes in v11:
time: 136 us; the launch traced here: 135 us
  starting transfers between devices  52.7 us (39%)
  blocking collectives  50.6 us (37%)
  waiting for transfers between devices  20 us (15%)
  Pallas kernels  7.35 us (5%)
  other arithmetic  2.22 us (2%)
  local copies, waits for them, and re-layouts  2 us (1%)
    all_to_all x2, blocking collectives, exchange(): return lax.all_to_all(array, axes, 0, 0, tiled=True)  50.6 us
    ppermute x2, starting transfers between devices, on_device(): got = sum((lax.ppermute(piece, 'z', [hop]) for hop in LONG))  13.4 us
    ppermute x3, starting transfers between devices, on_device(): lax.ppermute(piece, ('yl', 'yh'), [(at, at ^ q) for at in range(4)])  10.6 us
    ppermute x1, starting transfers between devices, on_device(): far = lax.ppermute(near, 'core', PAIR)  9.73 us
    all_to_all x1, waiting for transfers between devices, exchange(): return lax.all_to_all(array, axes, 0, 0, tiled=True)  8.88 us
    ppermute x3, waiting for transfers between devices, on_device(): lax.ppermute(piece, ('yl', 'yh'), [(at, at ^ q) for at in range(4)])  5.85 us
    ppermute x1, starting transfers between devices, on_device(): other_amps = lax.ppermute(amplitudes, 'yh', PAIR)  5.76 us
    pallas_call x1, Pallas kernels, ladder_partials(): pl.pallas_call(ladder_kernel, out_shape=jax.ShapeDtypeStruct((con_count,...  4.48 us
  transfers between devices with their start and end apart: 13, of which 6 were waited for; matrix products, arithmetic and copies ran while one was open for 3% of the time, Pallas kernels for 0%

profile of v11, /device:TPU:1, one launch (start us, length us, event | category | flops | bytes accessed | tf_op | source)
XLA Modules:
  0.0 135.0 jit_solution(1721919634511170074)
XLA Ops:
  0.0 5.8 %collective-permute-start = (bf16[8,1024]{1,0:T(8,128)(2,1)}, bf16[8,1024]{1,0:T(8,128)(2,1)S(1)}, u32[]{:S(2)}, u32[]{:S(2)}) collective-permute-start(bf16[8,1024]{1,0:T(8,128)(2,1)} %amps_ref.1), channel_id=1, source_target_pairs={{0,8},{8,0},{1,9},{9,1},{2,10},{10,2},{3,11},{11,3},{4,12},{12,4},... | collective-permute-start | bytes 49160 | tf_op jit(solution)/shard_map/ppermute | solution.py:231
  5.8 1.1 copy.5
  6.9 0.2 collective-permute-done.other_ref
  7.1 0.7 copy-done.1
  7.8 1.3 shard_map.46
  9.1 4.2 %all-to-all-start = ((bf16[4,288,640]{2,1,0:T(8,128)(2,1)}), bf16[4,288,640]{2,1,0:T(8,128)(2,1)S(1)}, u32[]{:S(2)}, u32[]{:S(2)}) async-start(bf16[4,288,640]{2,1,0:T(8,128)(2,1)} %shard_map.46), calls=%async_computation | async-start | bytes 2949120 | tf_op jit(solution)/shard_map/all_to_all | solution.py:21
  13.3 3.9 %collective-permute-start.2 = (bf16[128,640]{1,0:T(8,128)(2,1)S(1)}, bf16[128,640]{1,0:T(8,128)(2,1)}, u32[]{:S(2)}, u32[]{:S(2)}) collective-permute-start(bf16[128,640]{1,0:T(8,128)(2,1)S(1)} %bitcast.12), channel_id=1, source_target_pairs={{0,16},{1,17},{2,18},{3,19},{4,20},{5,21},{6,22},{7,23},{8,24},{9,... | collective-permute-start | bytes 491528 | tf_op jit(solution)/shard_map/ppermute | solution.py:239
  17.2 8.9 %all-to-all-done.near_ref = bf16[4,288,640]{2,1,0:T(8,128)(2,1)S(1)} async-done(((bf16[4,288,640]{2,1,0:T(8,128)(2,1)}), bf16[4,288,640]{2,1,0:T(8,128)(2,1)S(1)}, u32[]{:S(2)}, u32[]{:S(2)}) %all-to-all-start) | async-done | bytes 1474592 | tf_op jit(solution)/shard_map/all_to_all | solution.py:21
  26.0 9.7 %collective-permute-start.1 = (bf16[4,288,640]{2,1,0:T(8,128)(2,1)S(1)}, bf16[4,288,640]{2,1,0:T(8,128)(2,1)S(1)}, u32[]{:S(2)}, u32[]{:S(2)}) collective-permute-start(bf16[4,288,640]{2,1,0:T(8,128)(2,1)S(1)} %all-to-all-done.near_ref), channel_id=1, source_target_pairs={{0,1},{1,0},{2,3},{3,2},{4,5},{5,4},{6,7},{7,6},{8,9},{9,8},{10,11... | collective-permute-start | bytes 4423688 | tf_op jit(solution)/shard_map/ppermute | solution.py:259
  35.8 6.3 %collective-permute-start.3 = (bf16[128,640]{1,0:T(8,128)(2,1)S(1)}, bf16[128,640]{1,0:T(8,128)(2,1)S(1)}, u32[]{:S(2)}, u32[]{:S(2)}) collective-permute-start(bf16[128,640]{1,0:T(8,128)(2,1)S(1)} %bitcast_select_fusion), channel_id=1, source_target_pairs={{0,96},{1,97},{2,98},{3,99},{4,100},{5,101},{6,102},{7,103},{8,104... | collective-permute-start | bytes 491528 | tf_op jit(solution)/shard_map/ppermute | solution.py:240
  42.1 7.1 %collective-permute-start.4 = (bf16[128,640]{1,0:T(8,128)(2,1)S(1)}, bf16[128,640]{1,0:T(8,128)(2,1)}, u32[]{:S(2)}, u32[]{:S(2)}) collective-permute-start(bf16[128,640]{1,0:T(8,128)(2,1)S(1)} %bitcast_select_fusion), channel_id=1, source_target_pairs={{0,416},{1,417},{2,418},{3,419},{4,420},{5,421},{6,422},{7,423},{8... | collective-permute-start | bytes 491528 | tf_op jit(solution)/shard_map/ppermute | solution.py:240
  49.2 2.9 %collective-permute-done.4 = bf16[128,640]{1,0:T(8,128)(2,1)} collective-permute-done((bf16[128,640]{1,0:T(8,128)(2,1)S(1)}, bf16[128,640]{1,0:T(8,128)(2,1)}, u32[]{:S(2)}, u32[]{:S(2)}) %collective-permute-start.4) | collective-permute-done | bytes 163872 | tf_op jit(solution)/shard_map/ppermute | solution.py:240
  52.1 1.0 add_select_fusion.1
  53.0 0.7 collective-permute-start.5
  53.8 1.3 collective-permute-start.8
  55.1 1.3 collective-permute-start.6
  56.4 2.0 %collective-permute-start.7 = (bf16[128,640]{1,0:T(8,128)(2,1)S(1)}, bf16[128,640]{1,0:T(8,128)(2,1)}, u32[]{:S(2)}, u32[]{:S(2)}) collective-permute-start(bf16[128,640]{1,0:T(8,128)(2,1)S(1)} %broadcast_select_fusion), channel_id=1, source_target_pairs={{0,32},{96,128},{192,224},{320,352},{416,448},{1,33},{97,129},{193... | collective-permute-start | bytes 491528 | tf_op jit(solution)/shard_map/ppermute | solution.py:252
  58.4 0.1 constant_dynamic-slice_fusion
  58.4 2.2 %collective-permute-done.7 = bf16[128,640]{1,0:T(8,128)(2,1)} collective-permute-done((bf16[128,640]{1,0:T(8,128)(2,1)S(1)}, bf16[128,640]{1,0:T(8,128)(2,1)}, u32[]{:S(2)}, u32[]{:S(2)}) %collective-permute-start.7) | collective-permute-done | bytes 163872 | tf_op jit(solution)/shard_map/ppermute | solution.py:252
  60.6 1.0 add_select_fusion.refs_0_
  61.7 4.1 %collective-permute-start.9 = (bf16[128,640]{1,0:T(8,128)(2,1)S(1)}, bf16[128,640]{1,0:T(8,128)(2,1)S(1)}, u32[]{:S(2)}, u32[]{:S(2)}) collective-permute-start(bf16[128,640]{1,0:T(8,128)(2,1)S(1)} %add_select_fusion.refs_0_), channel_id=1, source_target_pairs={{0,16},{8,24},{16,0},{24,8},{1,17},{9,25},{17,1},{25,9},{2,18},{10... | collective-permute-start | bytes 491528 | tf_op jit(solution)/shard_map/ppermute | solution.py:256
  65.8 4.5 %collective-permute-start.10 = (bf16[128,640]{1,0:T(8,128)(2,1)S(1)}, bf16[128,640]{1,0:T(8,128)(2,1)S(1)}, u32[]{:S(2)}, u32[]{:S(2)}) collective-permute-start(bf16[128,640]{1,0:T(8,128)(2,1)S(1)} %add_select_fusion.refs_0_), channel_id=1, source_target_pairs={{0,8},{8,0},{16,24},{24,16},{1,9},{9,1},{17,25},{25,17},{2,10},{10... | collective-permute-start | bytes 491528 | tf_op jit(solution)/shard_map/ppermute | solution.py:256
  70.3 1.9 %collective-permute-start.11 = (bf16[128,640]{1,0:T(8,128)(2,1)S(1)}, bf16[128,640]{1,0:T(8,128)(2,1)}, u32[]{:S(2)}, u32[]{:S(2)}) collective-permute-start(bf16[128,640]{1,0:T(8,128)(2,1)S(1)} %add_select_fusion.refs_0_), channel_id=1, source_target_pairs={{0,24},{8,16},{16,8},{24,0},{1,25},{9,17},{17,9},{25,1},{2,26},{10... | collective-permute-start | bytes 491528 | tf_op jit(solution)/shard_map/ppermute | solution.py:256
  72.3 0.1 dynamic-slice_subtract_fusion.swap_ref
  72.3 0.1 copy.7.pairs_ref
  72.4 0.1 pad_add_fusion.place_ref
  72.5 2.9 %collective-permute-done.10.refs_2_ = bf16[128,640]{1,0:T(8,128)(2,1)S(1)} collective-permute-done((bf16[128,640]{1,0:T(8,128)(2,1)S(1)}, bf16[128,640]{1,0:T(8,128)(2,1)S(1)}, u32[]{:S(2)}, u32[]{:S(2)}) %collective-permute-start.10) | collective-permute-done | bytes 163872 | tf_op jit(solution)/shard_map/ppermute | solution.py:256
  75.4 3.0 %collective-permute-done.11.refs_3_ = bf16[128,640]{1,0:T(8,128)(2,1)} collective-permute-done((bf16[128,640]{1,0:T(8,128)(2,1)S(1)}, bf16[128,640]{1,0:T(8,128)(2,1)}, u32[]{:S(2)}, u32[]{:S(2)}) %collective-permute-start.11) | collective-permute-done | bytes 163872 | tf_op jit(solution)/shard_map/ppermute | solution.py:256
  78.4 4.5 %shard_map.47 = bf16[32,4,1024]{2,1,0:T(4,128)(2,1)S(1)} custom-call(s32[3]{0:T(128)S(1)} %pad_add_fusion.place_ref, bf16[4,288,640]{2,1,0:T(8,128)(2,1)S(1)} %all-to-all-done.near_ref, bf16[4,288,640]{2,1,0:T(8,128)(2,1)S(1)} %collective-permute-done.1.far_ref, bf16[128,640]{1,0:T(8,128)(2,1)S(1)} %add_select_fusion.refs_0_, ...), custom_call_target="tpu_custom_call" | custom-call | flops 1509949440 | bytes 2949120 | tf_op jit(solution)/shard_map/pallas_call | solution.py:86
  82.8 35.5 %all_to_all.15.parts_ref = bf16[32,4,1024]{2,1,0:T(4,128)(2,1)S(1)} all-to-all(bf16[32,4,1024]{2,1,0:T(4,128)(2,1)S(1)} %shard_map.47), channel_id=1, replica_groups=mesh['z'=16,'yl'=2,'yh'=2,'x'=4,'core'=2] {'z','yl'}, dimensions={0} | all-to-all | bytes 524288 | tf_op jit(solution)/shard_map/all_to_all | solution.py:21
  118.4 15.1 %all_to_all.16.every_ref = bf16[16,4,1024]{2,1,0:T(4,128)(2,1)S(1)} all-to-all(bf16[16,4,1024]{2,1,0:T(4,128)(2,1)S(1)} %shard_map.48), channel_id=1, replica_groups=mesh['z'=16,'yl'=2,'yh'=2,'x'=4,'core'=2] {'yh','x','core'}, dimensions={0} | all-to-all | bytes 262144 | tf_op jit(solution)/shard_map/all_to_all | solution.py:21
  133.5 1.6 %shard_map.49 = f32[4,4,256]{2,1,0:T(4,128)} custom-call(s32[4,2]{1,0:T(4,128)S(1)} %copy.7.pairs_ref, s32[4]{0:T(128)S(1)} %dynamic-slice_subtract_fusion.swap_ref, bf16[16,4,1024]{2,1,0:T(4,128)(2,1)S(1)} %all_to_all.16.every_ref), custom_call_target="tpu_custom_call" | custom-call | flops 6553600 | bytes 262144 | tf_op jit(solution)/shard_map/pallas_call | solution.py:211
  (18 shorter events, 0.2 us)
Async XLA Ops:
  0.0 58.4 %copy-start = (s32[64,2]{0,1:T(2,128)S(1)}, s32[64,2]{0,1:T(2,128)}, u32[]{:S(2)}) copy-start(s32[64,2]{0,1:T(2,128)} %param.7) | copy-start | bytes 1540
  0.0 7.1 %collective-permute-start = (bf16[8,1024]{1,0:T(8,128)(2,1)}, bf16[8,1024]{1,0:T(8,128)(2,1)S(1)}, u32[]{:S(2)}, u32[]{:S(2)}) collective-permute-start(bf16[8,1024]{1,0:T(8,128)(2,1)} %amps_ref.1), channel_id=1, source_target_pairs={{0,8},{8,0},{1,9},{9,1},{2,10},{10,2},{3,11},{11,3},{4,12},{12,4},... | collective-permute-start | bytes 49160 | tf_op jit(solution)/shard_map/ppermute | solution.py:231
  7.1 0.7 copy-start.1
  9.1 4.2 %copy-start.2 = (bf16[8,32,640]{2,1,0:T(8,128)(2,1)S(1)}, bf16[8,32,640]{2,1,0:T(8,128)(2,1)}, u32[]{:S(2)}) copy-start(bf16[8,32,640]{2,1,0:T(8,128)(2,1)} %param.5) | copy-start | bytes 983044
  9.1 17.0 %all-to-all-start = ((bf16[4,288,640]{2,1,0:T(8,128)(2,1)}), bf16[4,288,640]{2,1,0:T(8,128)(2,1)S(1)}, u32[]{:S(2)}, u32[]{:S(2)}) async-start(bf16[4,288,640]{2,1,0:T(8,128)(2,1)} %shard_map.46), calls=%async_computation | async-start | bytes 2949120 | tf_op jit(solution)/shard_map/all_to_all | solution.py:21
  13.3 59.0 %copy-start.3 = (s32[128]{0:T(128)S(1)}, s32[128]{0:T(128)}, u32[]{:S(2)}) copy-start(s32[128]{0:T(128)} %param.8) | copy-start | bytes 1540
  13.3 22.5 %collective-permute-start.2 = (bf16[128,640]{1,0:T(8,128)(2,1)S(1)}, bf16[128,640]{1,0:T(8,128)(2,1)}, u32[]{:S(2)}, u32[]{:S(2)}) collective-permute-start(bf16[128,640]{1,0:T(8,128)(2,1)S(1)} %bitcast.12), channel_id=1, source_target_pairs={{0,16},{1,17},{2,18},{3,19},{4,20},{5,21},{6,22},{7,23},{8,24},{9,... | collective-permute-start | bytes 491528 | tf_op jit(solution)/shard_map/ppermute | solution.py:239
  26.0 46.5 %collective-permute-start.1 = (bf16[4,288,640]{2,1,0:T(8,128)(2,1)S(1)}, bf16[4,288,640]{2,1,0:T(8,128)(2,1)S(1)}, u32[]{:S(2)}, u32[]{:S(2)}) collective-permute-start(bf16[4,288,640]{2,1,0:T(8,128)(2,1)S(1)} %all-to-all-done.near_ref), channel_id=1, source_target_pairs={{0,1},{1,0},{2,3},{3,2},{4,5},{5,4},{6,7},{7,6},{8,9},{9,8},{10,11... | collective-permute-start | bytes 4423688 | tf_op jit(solution)/shard_map/ppermute | solution.py:259
  35.8 13.4 %collective-permute-start.3 = (bf16[128,640]{1,0:T(8,128)(2,1)S(1)}, bf16[128,640]{1,0:T(8,128)(2,1)S(1)}, u32[]{:S(2)}, u32[]{:S(2)}) collective-permute-start(bf16[128,640]{1,0:T(8,128)(2,1)S(1)} %bitcast_select_fusion), channel_id=1, source_target_pairs={{0,96},{1,97},{2,98},{3,99},{4,100},{5,101},{6,102},{7,103},{8,104... | collective-permute-start | bytes 491528 | tf_op jit(solution)/shard_map/ppermute | solution.py:240
  42.1 10.0 %collective-permute-start.4 = (bf16[128,640]{1,0:T(8,128)(2,1)S(1)}, bf16[128,640]{1,0:T(8,128)(2,1)}, u32[]{:S(2)}, u32[]{:S(2)}) collective-permute-start(bf16[128,640]{1,0:T(8,128)(2,1)S(1)} %bitcast_select_fusion), channel_id=1, source_target_pairs={{0,416},{1,417},{2,418},{3,419},{4,420},{5,421},{6,422},{7,423},{8... | collective-permute-start | bytes 491528 | tf_op jit(solution)/shard_map/ppermute | solution.py:240
  53.0 0.7 collective-permute-start.5
  53.8 4.7 %collective-permute-start.8 = (bf16[128,640]{1,0:T(8,128)(2,1)S(1)}, bf16[128,640]{1,0:T(8,128)(2,1)S(1)}, u32[]{:S(2)}, u32[]{:S(2)}) collective-permute-start(bf16[128,640]{1,0:T(8,128)(2,1)S(1)} %broadcast_select_fusion), channel_id=1, source_target_pairs={{96,64},{192,160},{320,288},{416,384},{0,480},{97,65},{193,161},{3... | collective-permute-start | bytes 491528 | tf_op jit(solution)/shard_map/ppermute | solution.py:252
  55.1 3.4 %collective-permute-start.6 = (bf16[128,640]{1,0:T(8,128)(2,1)S(1)}, bf16[128,640]{1,0:T(8,128)(2,1)}, u32[]{:S(2)}, u32[]{:S(2)}) collective-permute-start(bf16[128,640]{1,0:T(8,128)(2,1)S(1)} %broadcast_select_fusion), channel_id=1, source_target_pairs={{192,256},{193,257},{194,258},{195,259},{196,260},{197,261},{198,2... | collective-permute-start | bytes 491528 | tf_op jit(solution)/shard_map/ppermute | solution.py:251
  56.4 4.2 %collective-permute-start.7 = (bf16[128,640]{1,0:T(8,128)(2,1)S(1)}, bf16[128,640]{1,0:T(8,128)(2,1)}, u32[]{:S(2)}, u32[]{:S(2)}) collective-permute-start(bf16[128,640]{1,0:T(8,128)(2,1)S(1)} %broadcast_select_fusion), channel_id=1, source_target_pairs={{0,32},{96,128},{192,224},{320,352},{416,448},{1,33},{97,129},{193... | collective-permute-start | bytes 491528 | tf_op jit(solution)/shard_map/ppermute | solution.py:252
  61.7 10.8 %collective-permute-start.9 = (bf16[128,640]{1,0:T(8,128)(2,1)S(1)}, bf16[128,640]{1,0:T(8,128)(2,1)S(1)}, u32[]{:S(2)}, u32[]{:S(2)}) collective-permute-start(bf16[128,640]{1,0:T(8,128)(2,1)S(1)} %add_select_fusion.refs_0_), channel_id=1, source_target_pairs={{0,16},{8,24},{16,0},{24,8},{1,17},{9,25},{17,1},{25,9},{2,18},{10... | collective-permute-start | bytes 491528 | tf_op jit(solution)/shard_map/ppermute | solution.py:256
  65.8 9.6 %collective-permute-start.10 = (bf16[128,640]{1,0:T(8,128)(2,1)S(1)}, bf16[128,640]{1,0:T(8,128)(2,1)S(1)}, u32[]{:S(2)}, u32[]{:S(2)}) collective-permute-start(bf16[128,640]{1,0:T(8,128)(2,1)S(1)} %add_select_fusion.refs_0_), channel_id=1, source_target_pairs={{0,8},{8,0},{16,24},{24,16},{1,9},{9,1},{17,25},{25,17},{2,10},{10... | collective-permute-start | bytes 491528 | tf_op jit(solution)/shard_map/ppermute | solution.py:256
  70.3 8.0 %collective-permute-start.11 = (bf16[128,640]{1,0:T(8,128)(2,1)S(1)}, bf16[128,640]{1,0:T(8,128)(2,1)}, u32[]{:S(2)}, u32[]{:S(2)}) collective-permute-start(bf16[128,640]{1,0:T(8,128)(2,1)S(1)} %add_select_fusion.refs_0_), channel_id=1, source_target_pairs={{0,24},{8,16},{16,8},{24,0},{1,25},{9,17},{17,9},{25,1},{2,26},{10... | collective-permute-start | bytes 491528 | tf_op jit(solution)/shard_map/ppermute | solution.py:256

commit v12 on v11

--- a/solution.py
+++ b/solution.py
@@ -22,57 +22,67 @@
 
 
 def ladder_kernel(place_ref, near_ref, far_ref, *refs):
-    *quarter_refs, last_ref, out_ref, stack_ref, right_ref, amps_ref, landing_ref, rows_ref, landed = refs
+    *quarter_refs, last_ref, out_ref, stack_ref, landing_ref, landed = refs
     core, yh, own = place_ref[0], place_ref[1], place_ref[2]
     landing = pltpu.make_async_copy(last_ref, landing_ref, landed)
     landing.start()
+    quarter_refs = [*quarter_refs, landing_ref]
     b_count, depth, _ = stack_ref.shape
     ring, pair_rows = near_ref.shape[0], b_count
     c_pairs = near_ref.shape[1] // pair_rows - 2
     a_dev = pair_rows // 2
-    d_count = right_ref.shape[0] // b_count
-    for m in range(2):
-        for rc, ref in enumerate((near_ref, far_ref)):
-            for x in range(ring):
-                place = (lax.rem(yh + m, 2) * ring + x) * 2 + lax.rem(core + rc, 2)
-                first = (c_pairs + m) * pair_rows
-                block = ref[x, first : first + pair_rows, :depth].astype(jnp.float32)
-                for g in range(2):
-                    amps_ref[g, place] = block[g * a_dev : (g + 1) * a_dev]
-    i_count = amps_ref.shape[1] * a_dev
-    rows_ref[...] = amps_ref[...].reshape(2 * i_count, depth).astype(rows_ref.dtype)
-    landing.wait()
-    size = landing_ref.shape[0]
-    for q, ref in enumerate((*quarter_refs, landing_ref)):
-        right_ref[pl.ds(pl.multiple_of((own ^ q) * size, size), size), :] = ref[...]
-    for n in range(0, c_pairs, 2):
-        left = jnp.concatenate(
-            [
-                ref[x, m * pair_rows : (m + 1) * pair_rows, :]
-                for m in (n, n + 1)
-                for x in range(ring)
-                for ref in (near_ref, far_ref)
-            ],
-            axis=0,
-        )
-        part = lax.dot_general(
-            right_ref[...], left, (((1,), (1,)), ((), ())), preferred_element_type=jnp.float32
-        ).astype(jnp.bfloat16)
-        part = part.reshape(b_count, d_count, 2 * LANES)
-        for h in range(2):
-            rows = (n + h) * d_count
-            stack_ref[:, rows : rows + d_count, :] = part[:, :, h * LANES : (h + 1) * LANES]
-    odd = lax.rem(lax.broadcasted_iota(jnp.int32, (1, LANES), 1) // a_dev, 2) == 1
-    rows = out_ref.shape[1]
-    for q in range(b_count // 2):
-        sums = []
-        for b, step in ((2 * q, LANES - a_dev), (2 * q + 1, a_dev)):
-            full = jnp.dot(rows_ref[...], stack_ref[b], preferred_element_type=jnp.float32)
-            mixed = jnp.where(odd, full[i_count:], full[:i_count])
-            sums.append(mixed + pltpu.roll(mixed, step, 1))
-        found = jnp.where(odd, sums[1], sums[0]).astype(out_ref.dtype)
-        for k in range(out_ref.shape[0]):
-            out_ref[k, :, q * LANES : (q + 1) * LANES] = found[k * rows : (k + 1) * rows]
+    some = b_count // len(quarter_refs)
+    d_count = landing_ref.shape[0] // some
+    odd = lax.rem(lax.broadcasted_iota(jnp.int32, (1, 1, LANES), 2) // a_dev, 2) == 1
+    blocks = 4 * ring
+    for first in range(0, len(quarter_refs), 2):
+        if first + 2 == len(quarter_refs):
+            landing.wait()
+        for n in range(0, c_pairs, 2):
+            left = jnp.concatenate(
+                [
+                    ref[x, m * pair_rows : (m + 1) * pair_rows, :]
+                    for m in (n, n + 1)
+                    for x in range(ring)
+                    for ref in (near_ref, far_ref)
+                ],
+                axis=0,
+            )
+            right = jnp.concatenate([ref[...] for ref in quarter_refs[first : first + 2]], axis=0)
+            part = lax.dot_general(
+                right, left, (((1,), (1,)), ((), ())), preferred_element_type=jnp.float32
+            ).astype(jnp.bfloat16)
+            part = part.reshape(2 * some, d_count, 2 * LANES)
+            for h in range(2):
+                rows = (n + h) * d_count
+                stack_ref[first * some : (first + 2) * some, rows : rows + d_count, :] = part[
+                    :, :, h * LANES : (h + 1) * LANES
+                ]
+        for q in range(first * some // 2, (first + 2) * some // 2):
+            amps = jnp.concatenate(
+                [
+                    ref[x, m * pair_rows : (m + 1) * pair_rows, :depth]
+                    for m in (c_pairs, c_pairs + 1)
+                    for ref in (near_ref, far_ref)
+                    for x in range(ring)
+                ],
+                axis=0,
+            )
+            sums = []
+            for b, step in ((2 * q, LANES - a_dev), (2 * q + 1, a_dev)):
+                full = jnp.dot(amps, stack_ref[b], preferred_element_type=jnp.float32)
+                full = full.reshape(blocks, 2, a_dev, LANES)
+                mixed = jnp.where(odd, full[:, 1], full[:, 0]).reshape(blocks * a_dev, LANES)
+                sums.append(mixed + pltpu.roll(mixed, step, 1))
+            found = jnp.where(odd[0], sums[1], sums[0]).astype(out_ref.dtype)
+            quarter, pair = own ^ (2 * q // some), q % (some // 2)
+            column = pl.multiple_of((quarter * (some // 2) + pair) * LANES, LANES)
+            for block in range(blocks):
+                other_yh, other_core, x = block // (2 * ring), block // ring % 2, block % ring
+                place = (lax.rem(yh + other_yh, 2) * ring + x) * 2 + lax.rem(core + other_core, 2)
+                for h in range(2):
+                    low = block * a_dev + h * (a_dev // 2)
+                    out_ref[2 * place + h, :, pl.ds(column, LANES)] = found[low : low + a_dev // 2]
 
 
 def in_vmem(count):
@@ -93,10 +103,7 @@
         out_specs=pl.BlockSpec(memory_space=pltpu.VMEM),
         scratch_shapes=[
             pltpu.VMEM((b_count, depth, LANES), jnp.bfloat16),
-            pltpu.VMEM(right, jnp.bfloat16),
-            pltpu.VMEM((2, 4 * near.shape[0], b_count // 2, depth), jnp.float32),
             pltpu.VMEM(quarters[-1].shape, jnp.bfloat16),
-            pltpu.VMEM((2 * i_count, depth), jnp.bfloat16),
             pltpu.SemaphoreType.DMA,
         ],
         compiler_params=pltpu.CompilerParams(vmem_limit_bytes=12 * 1024 * 1024),

time: 136 us -> 136 us (level)
  no operation moved by 1% of the time
where the time goes in v12:
time: 136 us; the launch traced here: 135 us
  starting transfers between devices  52.7 us (39%)
  blocking collectives  50.5 us (37%)
  waiting for transfers between devices  20 us (15%)
  Pallas kernels  7.41 us (5%)
  other arithmetic  2.22 us (2%)
  local copies, waits for them, and re-layouts  2 us (1%)
    all_to_all x2, blocking collectives, exchange(): return lax.all_to_all(array, axes, 0, 0, tiled=True)  50.5 us
    ppermute x2, starting transfers between devices, on_device(): got = sum((lax.ppermute(piece, 'z', [hop]) for hop in LONG))  13.4 us
    ppermute x3, starting transfers between devices, on_device(): lax.ppermute(piece, ('yl', 'yh'), [(at, at ^ q) for at in range(4)])  10.6 us
    ppermute x1, starting transfers between devices, on_device(): far = lax.ppermute(near, 'core', PAIR)  9.73 us
    all_to_all x1, waiting for transfers between devices, exchange(): return lax.all_to_all(array, axes, 0, 0, tiled=True)  8.88 us
    ppermute x3, waiting for transfers between devices, on_device(): lax.ppermute(piece, ('yl', 'yh'), [(at, at ^ q) for at in range(4)])  5.85 us
    ppermute x1, starting transfers between devices, on_device(): other_amps = lax.ppermute(amplitudes, 'yh', PAIR)  5.76 us
    pallas_call x1, Pallas kernels, ladder_partials(): pl.pallas_call(ladder_kernel, out_shape=jax.ShapeDtypeStruct((con_count,...  4.54 us
  transfers between devices with their start and end apart: 13, of which 6 were waited for; matrix products, arithmetic and copies ran while one was open for 3% of the time, Pallas kernels for 0%

profile of v12, /device:TPU:1, one launch (start us, length us, event | category | flops | bytes accessed | tf_op | source)
XLA Modules:
  0.0 135.1 jit_solution(9367841217516029251)
XLA Ops:
  0.0 5.8 %collective-permute-start = (bf16[8,1024]{1,0:T(8,128)(2,1)}, bf16[8,1024]{1,0:T(8,128)(2,1)S(1)}, u32[]{:S(2)}, u32[]{:S(2)}) collective-permute-start(bf16[8,1024]{1,0:T(8,128)(2,1)} %amps_ref.1), channel_id=1, source_target_pairs={{0,8},{8,0},{1,9},{9,1},{2,10},{10,2},{3,11},{11,3},{4,12},{12,4},... | collective-permute-start | bytes 49160 | tf_op jit(solution)/shard_map/ppermute | solution.py:238
  5.8 1.1 copy.5
  6.9 0.2 collective-permute-done.other_ref
  7.1 0.7 copy-done.1
  7.8 1.3 shard_map.46
  9.1 4.2 %all-to-all-start = ((bf16[4,288,640]{2,1,0:T(8,128)(2,1)}), bf16[4,288,640]{2,1,0:T(8,128)(2,1)S(1)}, u32[]{:S(2)}, u32[]{:S(2)}) async-start(bf16[4,288,640]{2,1,0:T(8,128)(2,1)} %shard_map.46), calls=%async_computation | async-start | bytes 2949120 | tf_op jit(solution)/shard_map/all_to_all | solution.py:21
  13.3 3.9 %collective-permute-start.2 = (bf16[128,640]{1,0:T(8,128)(2,1)S(1)}, bf16[128,640]{1,0:T(8,128)(2,1)}, u32[]{:S(2)}, u32[]{:S(2)}) collective-permute-start(bf16[128,640]{1,0:T(8,128)(2,1)S(1)} %bitcast.12), channel_id=1, source_target_pairs={{0,16},{1,17},{2,18},{3,19},{4,20},{5,21},{6,22},{7,23},{8,24},{9,... | collective-permute-start | bytes 491528 | tf_op jit(solution)/shard_map/ppermute | solution.py:246
  17.2 8.9 %all-to-all-done.near_ref = bf16[4,288,640]{2,1,0:T(8,128)(2,1)S(1)} async-done(((bf16[4,288,640]{2,1,0:T(8,128)(2,1)}), bf16[4,288,640]{2,1,0:T(8,128)(2,1)S(1)}, u32[]{:S(2)}, u32[]{:S(2)}) %all-to-all-start) | async-done | bytes 1474592 | tf_op jit(solution)/shard_map/all_to_all | solution.py:21
  26.0 9.7 %collective-permute-start.1 = (bf16[4,288,640]{2,1,0:T(8,128)(2,1)S(1)}, bf16[4,288,640]{2,1,0:T(8,128)(2,1)S(1)}, u32[]{:S(2)}, u32[]{:S(2)}) collective-permute-start(bf16[4,288,640]{2,1,0:T(8,128)(2,1)S(1)} %all-to-all-done.near_ref), channel_id=1, source_target_pairs={{0,1},{1,0},{2,3},{3,2},{4,5},{5,4},{6,7},{7,6},{8,9},{9,8},{10,11... | collective-permute-start | bytes 4423688 | tf_op jit(solution)/shard_map/ppermute | solution.py:266
  35.8 6.3 %collective-permute-start.3 = (bf16[128,640]{1,0:T(8,128)(2,1)S(1)}, bf16[128,640]{1,0:T(8,128)(2,1)S(1)}, u32[]{:S(2)}, u32[]{:S(2)}) collective-permute-start(bf16[128,640]{1,0:T(8,128)(2,1)S(1)} %bitcast_select_fusion), channel_id=1, source_target_pairs={{0,96},{1,97},{2,98},{3,99},{4,100},{5,101},{6,102},{7,103},{8,104... | collective-permute-start | bytes 491528 | tf_op jit(solution)/shard_map/ppermute | solution.py:247
  42.1 7.1 %collective-permute-start.4 = (bf16[128,640]{1,0:T(8,128)(2,1)S(1)}, bf16[128,640]{1,0:T(8,128)(2,1)}, u32[]{:S(2)}, u32[]{:S(2)}) collective-permute-start(bf16[128,640]{1,0:T(8,128)(2,1)S(1)} %bitcast_select_fusion), channel_id=1, source_target_pairs={{0,416},{1,417},{2,418},{3,419},{4,420},{5,421},{6,422},{7,423},{8... | collective-permute-start | bytes 491528 | tf_op jit(solution)/shard_map/ppermute | solution.py:247
  49.2 2.9 %collective-permute-done.4 = bf16[128,640]{1,0:T(8,128)(2,1)} collective-permute-done((bf16[128,640]{1,0:T(8,128)(2,1)S(1)}, bf16[128,640]{1,0:T(8,128)(2,1)}, u32[]{:S(2)}, u32[]{:S(2)}) %collective-permute-start.4) | collective-permute-done | bytes 163872 | tf_op jit(solution)/shard_map/ppermute | solution.py:247
  52.1 1.0 add_select_fusion.1
  53.0 0.7 collective-permute-start.5
  53.8 1.3 collective-permute-start.8
  55.1 1.3 collective-permute-start.6
  56.4 2.0 %collective-permute-start.7 = (bf16[128,640]{1,0:T(8,128)(2,1)S(1)}, bf16[128,640]{1,0:T(8,128)(2,1)}, u32[]{:S(2)}, u32[]{:S(2)}) collective-permute-start(bf16[128,640]{1,0:T(8,128)(2,1)S(1)} %broadcast_select_fusion), channel_id=1, source_target_pairs={{0,32},{96,128},{192,224},{320,352},{416,448},{1,33},{97,129},{193... | collective-permute-start | bytes 491528 | tf_op jit(solution)/shard_map/ppermute | solution.py:259
  58.4 0.1 constant_dynamic-slice_fusion
  58.4 2.2 %collective-permute-done.7 = bf16[128,640]{1,0:T(8,128)(2,1)} collective-permute-done((bf16[128,640]{1,0:T(8,128)(2,1)S(1)}, bf16[128,640]{1,0:T(8,128)(2,1)}, u32[]{:S(2)}, u32[]{:S(2)}) %collective-permute-start.7) | collective-permute-done | bytes 163872 | tf_op jit(solution)/shard_map/ppermute | solution.py:259
  60.6 1.0 add_select_fusion.refs_0_
  61.7 4.1 %collective-permute-start.9 = (bf16[128,640]{1,0:T(8,128)(2,1)S(1)}, bf16[128,640]{1,0:T(8,128)(2,1)S(1)}, u32[]{:S(2)}, u32[]{:S(2)}) collective-permute-start(bf16[128,640]{1,0:T(8,128)(2,1)S(1)} %add_select_fusion.refs_0_), channel_id=1, source_target_pairs={{0,16},{8,24},{16,0},{24,8},{1,17},{9,25},{17,1},{25,9},{2,18},{10... | collective-permute-start | bytes 491528 | tf_op jit(solution)/shard_map/ppermute | solution.py:263
  65.8 4.5 %collective-permute-start.10 = (bf16[128,640]{1,0:T(8,128)(2,1)S(1)}, bf16[128,640]{1,0:T(8,128)(2,1)S(1)}, u32[]{:S(2)}, u32[]{:S(2)}) collective-permute-start(bf16[128,640]{1,0:T(8,128)(2,1)S(1)} %add_select_fusion.refs_0_), channel_id=1, source_target_pairs={{0,8},{8,0},{16,24},{24,16},{1,9},{9,1},{17,25},{25,17},{2,10},{10... | collective-permute-start | bytes 491528 | tf_op jit(solution)/shard_map/ppermute | solution.py:263
  70.3 1.9 %collective-permute-start.11 = (bf16[128,640]{1,0:T(8,128)(2,1)S(1)}, bf16[128,640]{1,0:T(8,128)(2,1)}, u32[]{:S(2)}, u32[]{:S(2)}) collective-permute-start(bf16[128,640]{1,0:T(8,128)(2,1)S(1)} %add_select_fusion.refs_0_), channel_id=1, source_target_pairs={{0,24},{8,16},{16,8},{24,0},{1,25},{9,17},{17,9},{25,1},{2,26},{10... | collective-permute-start | bytes 491528 | tf_op jit(solution)/shard_map/ppermute | solution.py:263
  72.3 0.1 dynamic-slice_subtract_fusion.swap_ref
  72.3 0.1 copy.7.pairs_ref
  72.4 0.1 pad_add_fusion.place_ref
  72.5 2.9 %collective-permute-done.10.refs_2_ = bf16[128,640]{1,0:T(8,128)(2,1)S(1)} collective-permute-done((bf16[128,640]{1,0:T(8,128)(2,1)S(1)}, bf16[128,640]{1,0:T(8,128)(2,1)S(1)}, u32[]{:S(2)}, u32[]{:S(2)}) %collective-permute-start.10) | collective-permute-done | bytes 163872 | tf_op jit(solution)/shard_map/ppermute | solution.py:263
  75.4 3.0 %collective-permute-done.11.refs_3_ = bf16[128,640]{1,0:T(8,128)(2,1)} collective-permute-done((bf16[128,640]{1,0:T(8,128)(2,1)S(1)}, bf16[128,640]{1,0:T(8,128)(2,1)}, u32[]{:S(2)}, u32[]{:S(2)}) %collective-permute-start.11) | collective-permute-done | bytes 163872 | tf_op jit(solution)/shard_map/ppermute | solution.py:263
  78.4 4.5 %shard_map.47 = bf16[32,4,1024]{2,1,0:T(4,128)(2,1)S(1)} custom-call(s32[3]{0:T(128)S(1)} %pad_add_fusion.place_ref, bf16[4,288,640]{2,1,0:T(8,128)(2,1)S(1)} %all-to-all-done.near_ref, bf16[4,288,640]{2,1,0:T(8,128)(2,1)S(1)} %collective-permute-done.1.far_ref, bf16[128,640]{1,0:T(8,128)(2,1)S(1)} %add_select_fusion.refs_0_, ...), custom_call_target="tpu_custom_call" | custom-call | flops 1509949440 | bytes 2949120 | tf_op jit(solution)/shard_map/pallas_call | solution.py:96
  82.9 35.5 %all_to_all.15.parts_ref = bf16[32,4,1024]{2,1,0:T(4,128)(2,1)S(1)} all-to-all(bf16[32,4,1024]{2,1,0:T(4,128)(2,1)S(1)} %shard_map.47), channel_id=1, replica_groups=mesh['z'=16,'yl'=2,'yh'=2,'x'=4,'core'=2] {'z','yl'}, dimensions={0} | all-to-all | bytes 524288 | tf_op jit(solution)/shard_map/all_to_all | solution.py:21
  118.4 15.1 %all_to_all.16.every_ref = bf16[16,4,1024]{2,1,0:T(4,128)(2,1)S(1)} all-to-all(bf16[16,4,1024]{2,1,0:T(4,128)(2,1)S(1)} %shard_map.48), channel_id=1, replica_groups=mesh['z'=16,'yl'=2,'yh'=2,'x'=4,'core'=2] {'yh','x','core'}, dimensions={0} | all-to-all | bytes 262144 | tf_op jit(solution)/shard_map/all_to_all | solution.py:21
  133.5 1.6 %shard_map.49 = f32[4,4,256]{2,1,0:T(4,128)} custom-call(s32[4,2]{1,0:T(4,128)S(1)} %copy.7.pairs_ref, s32[4]{0:T(128)S(1)} %dynamic-slice_subtract_fusion.swap_ref, bf16[16,4,1024]{2,1,0:T(4,128)(2,1)S(1)} %all_to_all.16.every_ref), custom_call_target="tpu_custom_call" | custom-call | flops 6553600 | bytes 262144 | tf_op jit(solution)/shard_map/pallas_call | solution.py:218
  (18 shorter events, 0.2 us)
Async XLA Ops:
  0.0 58.4 %copy-start = (s32[64,2]{0,1:T(2,128)S(1)}, s32[64,2]{0,1:T(2,128)}, u32[]{:S(2)}) copy-start(s32[64,2]{0,1:T(2,128)} %param.7) | copy-start | bytes 1540
  0.0 7.1 %collective-permute-start = (bf16[8,1024]{1,0:T(8,128)(2,1)}, bf16[8,1024]{1,0:T(8,128)(2,1)S(1)}, u32[]{:S(2)}, u32[]{:S(2)}) collective-permute-start(bf16[8,1024]{1,0:T(8,128)(2,1)} %amps_ref.1), channel_id=1, source_target_pairs={{0,8},{8,0},{1,9},{9,1},{2,10},{10,2},{3,11},{11,3},{4,12},{12,4},... | collective-permute-start | bytes 49160 | tf_op jit(solution)/shard_map/ppermute | solution.py:238
  7.1 0.7 copy-start.1
  9.1 4.2 %copy-start.2 = (bf16[8,32,640]{2,1,0:T(8,128)(2,1)S(1)}, bf16[8,32,640]{2,1,0:T(8,128)(2,1)}, u32[]{:S(2)}) copy-start(bf16[8,32,640]{2,1,0:T(8,128)(2,1)} %param.5) | copy-start | bytes 983044
  9.1 17.0 %all-to-all-start = ((bf16[4,288,640]{2,1,0:T(8,128)(2,1)}), bf16[4,288,640]{2,1,0:T(8,128)(2,1)S(1)}, u32[]{:S(2)}, u32[]{:S(2)}) async-start(bf16[4,288,640]{2,1,0:T(8,128)(2,1)} %shard_map.46), calls=%async_computation | async-start | bytes 2949120 | tf_op jit(solution)/shard_map/all_to_all | solution.py:21
  13.3 59.0 %copy-start.3 = (s32[128]{0:T(128)S(1)}, s32[128]{0:T(128)}, u32[]{:S(2)}) copy-start(s32[128]{0:T(128)} %param.8) | copy-start | bytes 1540
  13.3 22.5 %collective-permute-start.2 = (bf16[128,640]{1,0:T(8,128)(2,1)S(1)}, bf16[128,640]{1,0:T(8,128)(2,1)}, u32[]{:S(2)}, u32[]{:S(2)}) collective-permute-start(bf16[128,640]{1,0:T(8,128)(2,1)S(1)} %bitcast.12), channel_id=1, source_target_pairs={{0,16},{1,17},{2,18},{3,19},{4,20},{5,21},{6,22},{7,23},{8,24},{9,... | collective-permute-start | bytes 491528 | tf_op jit(solution)/shard_map/ppermute | solution.py:246
  26.0 46.5 %collective-permute-start.1 = (bf16[4,288,640]{2,1,0:T(8,128)(2,1)S(1)}, bf16[4,288,640]{2,1,0:T(8,128)(2,1)S(1)}, u32[]{:S(2)}, u32[]{:S(2)}) collective-permute-start(bf16[4,288,640]{2,1,0:T(8,128)(2,1)S(1)} %all-to-all-done.near_ref), channel_id=1, source_target_pairs={{0,1},{1,0},{2,3},{3,2},{4,5},{5,4},{6,7},{7,6},{8,9},{9,8},{10,11... | collective-permute-start | bytes 4423688 | tf_op jit(solution)/shard_map/ppermute | solution.py:266
  35.8 13.4 %collective-permute-start.3 = (bf16[128,640]{1,0:T(8,128)(2,1)S(1)}, bf16[128,640]{1,0:T(8,128)(2,1)S(1)}, u32[]{:S(2)}, u32[]{:S(2)}) collective-permute-start(bf16[128,640]{1,0:T(8,128)(2,1)S(1)} %bitcast_select_fusion), channel_id=1, source_target_pairs={{0,96},{1,97},{2,98},{3,99},{4,100},{5,101},{6,102},{7,103},{8,104... | collective-permute-start | bytes 491528 | tf_op jit(solution)/shard_map/ppermute | solution.py:247
  42.1 10.0 %collective-permute-start.4 = (bf16[128,640]{1,0:T(8,128)(2,1)S(1)}, bf16[128,640]{1,0:T(8,128)(2,1)}, u32[]{:S(2)}, u32[]{:S(2)}) collective-permute-start(bf16[128,640]{1,0:T(8,128)(2,1)S(1)} %bitcast_select_fusion), channel_id=1, source_target_pairs={{0,416},{1,417},{2,418},{3,419},{4,420},{5,421},{6,422},{7,423},{8... | collective-permute-start | bytes 491528 | tf_op jit(solution)/shard_map/ppermute | solution.py:247
  53.0 0.7 collective-permute-start.5
  53.8 4.7 %collective-permute-start.8 = (bf16[128,640]{1,0:T(8,128)(2,1)S(1)}, bf16[128,640]{1,0:T(8,128)(2,1)S(1)}, u32[]{:S(2)}, u32[]{:S(2)}) collective-permute-start(bf16[128,640]{1,0:T(8,128)(2,1)S(1)} %broadcast_select_fusion), channel_id=1, source_target_pairs={{96,64},{192,160},{320,288},{416,384},{0,480},{97,65},{193,161},{3... | collective-permute-start | bytes 491528 | tf_op jit(solution)/shard_map/ppermute | solution.py:259
  55.1 3.4 %collective-permute-start.6 = (bf16[128,640]{1,0:T(8,128)(2,1)S(1)}, bf16[128,640]{1,0:T(8,128)(2,1)}, u32[]{:S(2)}, u32[]{:S(2)}) collective-permute-start(bf16[128,640]{1,0:T(8,128)(2,1)S(1)} %broadcast_select_fusion), channel_id=1, source_target_pairs={{192,256},{193,257},{194,258},{195,259},{196,260},{197,261},{198,2... | collective-permute-start | bytes 491528 | tf_op jit(solution)/shard_map/ppermute | solution.py:258
  56.4 4.2 %collective-permute-start.7 = (bf16[128,640]{1,0:T(8,128)(2,1)S(1)}, bf16[128,640]{1,0:T(8,128)(2,1)}, u32[]{:S(2)}, u32[]{:S(2)}) collective-permute-start(bf16[128,640]{1,0:T(8,128)(2,1)S(1)} %broadcast_select_fusion), channel_id=1, source_target_pairs={{0,32},{96,128},{192,224},{320,352},{416,448},{1,33},{97,129},{193... | collective-permute-start | bytes 491528 | tf_op jit(solution)/shard_map/ppermute | solution.py:259
  61.7 10.8 %collective-permute-start.9 = (bf16[128,640]{1,0:T(8,128)(2,1)S(1)}, bf16[128,640]{1,0:T(8,128)(2,1)S(1)}, u32[]{:S(2)}, u32[]{:S(2)}) collective-permute-start(bf16[128,640]{1,0:T(8,128)(2,1)S(1)} %add_select_fusion.refs_0_), channel_id=1, source_target_pairs={{0,16},{8,24},{16,0},{24,8},{1,17},{9,25},{17,1},{25,9},{2,18},{10... | collective-permute-start | bytes 491528 | tf_op jit(solution)/shard_map/ppermute | solution.py:263
  65.8 9.6 %collective-permute-start.10 = (bf16[128,640]{1,0:T(8,128)(2,1)S(1)}, bf16[128,640]{1,0:T(8,128)(2,1)S(1)}, u32[]{:S(2)}, u32[]{:S(2)}) collective-permute-start(bf16[128,640]{1,0:T(8,128)(2,1)S(1)} %add_select_fusion.refs_0_), channel_id=1, source_target_pairs={{0,8},{8,0},{16,24},{24,16},{1,9},{9,1},{17,25},{25,17},{2,10},{10... | collective-permute-start | bytes 491528 | tf_op jit(solution)/shard_map/ppermute | solution.py:263
  70.3 8.0 %collective-permute-start.11 = (bf16[128,640]{1,0:T(8,128)(2,1)S(1)}, bf16[128,640]{1,0:T(8,128)(2,1)}, u32[]{:S(2)}, u32[]{:S(2)}) collective-permute-start(bf16[128,640]{1,0:T(8,128)(2,1)S(1)} %add_select_fusion.refs_0_), channel_id=1, source_target_pairs={{0,24},{8,16},{16,8},{24,0},{1,25},{9,17},{17,9},{25,1},{2,26},{10... | collective-permute-start | bytes 491528 | tf_op jit(solution)/shard_map/ppermute | solution.py:263

commit v13 on v12

--- a/solution.py
+++ b/solution.py
@@ -22,22 +22,18 @@
 
 
 def ladder_kernel(place_ref, near_ref, far_ref, *refs):
-    *quarter_refs, last_ref, out_ref, stack_ref, landing_ref, landed = refs
+    *quarter_refs, out_ref, stack_ref = refs
     core, yh, own = place_ref[0], place_ref[1], place_ref[2]
-    landing = pltpu.make_async_copy(last_ref, landing_ref, landed)
-    landing.start()
-    quarter_refs = [*quarter_refs, landing_ref]
     b_count, depth, _ = stack_ref.shape
     ring, pair_rows = near_ref.shape[0], b_count
     c_pairs = near_ref.shape[1] // pair_rows - 2
     a_dev = pair_rows // 2
     some = b_count // len(quarter_refs)
-    d_count = landing_ref.shape[0] // some
+    d_count = quarter_refs[0].shape[0] // some
+    together = len(quarter_refs)
     odd = lax.rem(lax.broadcasted_iota(jnp.int32, (1, 1, LANES), 2) // a_dev, 2) == 1
     blocks = 4 * ring
-    for first in range(0, len(quarter_refs), 2):
-        if first + 2 == len(quarter_refs):
-            landing.wait()
+    for first in range(0, len(quarter_refs), together):
         for n in range(0, c_pairs, 2):
             left = jnp.concatenate(
                 [
@@ -48,17 +44,17 @@
                 ],
                 axis=0,
             )
-            right = jnp.concatenate([ref[...] for ref in quarter_refs[first : first + 2]], axis=0)
+            right = jnp.concatenate([ref[...] for ref in quarter_refs[first : first + together]], axis=0)
             part = lax.dot_general(
                 right, left, (((1,), (1,)), ((), ())), preferred_element_type=jnp.float32
             ).astype(jnp.bfloat16)
-            part = part.reshape(2 * some, d_count, 2 * LANES)
+            part = part.reshape(together * some, d_count, 2 * LANES)
             for h in range(2):
                 rows = (n + h) * d_count
-                stack_ref[first * some : (first + 2) * some, rows : rows + d_count, :] = part[
+                stack_ref[first * some : (first + together) * some, rows : rows + d_count, :] = part[
                     :, :, h * LANES : (h + 1) * LANES
                 ]
-        for q in range(first * some // 2, (first + 2) * some // 2):
+        for q in range(first * some // 2, (first + together) * some // 2):
             amps = jnp.concatenate(
                 [
                     ref[x, m * pair_rows : (m + 1) * pair_rows, :depth]
@@ -98,13 +94,10 @@
         out_shape=jax.ShapeDtypeStruct(
             (con_count, i_count // con_count, b_count * LANES // 2), jnp.bfloat16
         ),
-        in_specs=[pl.BlockSpec(memory_space=pltpu.SMEM)] + in_vmem(1 + len(quarters))
-        + [pl.BlockSpec(memory_space=pl.ANY)],
+        in_specs=[pl.BlockSpec(memory_space=pltpu.SMEM)] + in_vmem(2 + len(quarters)),
         out_specs=pl.BlockSpec(memory_space=pltpu.VMEM),
         scratch_shapes=[
             pltpu.VMEM((b_count, depth, LANES), jnp.bfloat16),
-            pltpu.VMEM(quarters[-1].shape, jnp.bfloat16),
-            pltpu.SemaphoreType.DMA,
         ],
         compiler_params=pltpu.CompilerParams(vmem_limit_bytes=12 * 1024 * 1024),
         cost_estimate=pl.CostEstimate(
@@ -260,8 +253,9 @@
     sender = functools.reduce(jnp.logical_or, [z == at for at in SENDERS])
     piece = jnp.where(sender, piece, got)
     quarters = [piece] + [
-        lax.ppermute(piece, ("yl", "yh"), [(at, at ^ q) for at in range(4)]) for q in (2, 1, 3)
+        lax.ppermute(piece, ("yl", "yh"), [(at, at ^ q) for at in range(4)]) for q in (2, 1)
     ]
+    quarters.append(lax.ppermute(piece, ("yl", "yh"), [(at, at ^ 3) for at in range(4)]))
 
     far = lax.ppermute(near, "core", PAIR)
     slot_count, occ_dev = tile_pairs.shape[0] // out_count, i_count // con_count

time: 136 us -> 135 us (level)
    ppermute x0 -> x1, waiting for transfers between devices: none -> 2.96 us  [on_device(): lax.ppermute(piece, ('yl', 'yh'), [(at, at ^ 3) for at in range(4)])]
    ppermute x3 -> x2, waiting for transfers between devices: 5.85 us -> 2.89 us  [on_device(): lax.ppermute(piece, ('yl', 'yh'), [(at, at ^ q) for at in range(4)])]
    ppermute x0 -> x1, starting transfers between devices: none -> 1.92 us  [on_device(): lax.ppermute(piece, ('yl', 'yh'), [(at, at ^ 3) for at in range(4)])]
    ppermute x3 -> x2, starting transfers between devices: 10.6 us -> 8.63 us  [on_device(): lax.ppermute(piece, ('yl', 'yh'), [(at, at ^ q) for at in range(4)])]
where the time goes in v13:
time: 135 us
  starting transfers between devices  52.7 us (39%)
  blocking collectives  50.6 us (37%)
  waiting for transfers between devices  20 us (15%)
  Pallas kernels  6.86 us (5%)
  other arithmetic  2.22 us (2%)
  local copies, waits for them, and re-layouts  2 us (1%)
    all_to_all x2, blocking collectives, exchange(): return lax.all_to_all(array, axes, 0, 0, tiled=True)  50.6 us
    ppermute x2, starting transfers between devices, on_device(): got = sum((lax.ppermute(piece, 'z', [hop]) for hop in LONG))  13.4 us
    ppermute x1, starting transfers between devices, on_device(): far = lax.ppermute(near, 'core', PAIR)  9.73 us
    all_to_all x1, waiting for transfers between devices, exchange(): return lax.all_to_all(array, axes, 0, 0, tiled=True)  8.88 us
    ppermute x2, starting transfers between devices, on_device(): lax.ppermute(piece, ('yl', 'yh'), [(at, at ^ q) for at in range(4)])  8.63 us
    ppermute x1, starting transfers between devices, on_device(): other_amps = lax.ppermute(amplitudes, 'yh', PAIR)  5.76 us
    all_to_all x1, starting transfers between devices, exchange(): return lax.all_to_all(array, axes, 0, 0, tiled=True)  4.19 us
    pallas_call x1, Pallas kernels, ladder_partials(): pl.pallas_call(ladder_kernel, out_shape=jax.ShapeDtypeStruct((con_count,...  3.99 us
  transfers between devices with their start and end apart: 13, of which 6 were waited for; matrix products, arithmetic and copies ran while one was open for 3% of the time, Pallas kernels for 0%

profile of v13, /device:TPU:1, one launch (start us, length us, event | category | flops | bytes accessed | tf_op | source)
XLA Modules:
  0.0 134.5 jit_solution(5223934489095258262)
XLA Ops:
  0.0 5.8 %collective-permute-start = (bf16[8,1024]{1,0:T(8,128)(2,1)}, bf16[8,1024]{1,0:T(8,128)(2,1)S(1)}, u32[]{:S(2)}, u32[]{:S(2)}) collective-permute-start(bf16[8,1024]{1,0:T(8,128)(2,1)} %amps_ref.1), channel_id=1, source_target_pairs={{0,8},{8,0},{1,9},{9,1},{2,10},{10,2},{3,11},{11,3},{4,12},{12,4},... | collective-permute-start | bytes 49160 | tf_op jit(solution)/shard_map/ppermute | solution.py:231
  5.8 1.1 copy.5
  6.9 0.2 collective-permute-done.other_ref
  7.1 0.7 copy-done.1
  7.8 1.3 shard_map.46
  9.1 4.2 %all-to-all-start = ((bf16[4,288,640]{2,1,0:T(8,128)(2,1)}), bf16[4,288,640]{2,1,0:T(8,128)(2,1)S(1)}, u32[]{:S(2)}, u32[]{:S(2)}) async-start(bf16[4,288,640]{2,1,0:T(8,128)(2,1)} %shard_map.46), calls=%async_computation | async-start | bytes 2949120 | tf_op jit(solution)/shard_map/all_to_all | solution.py:21
  13.3 3.9 %collective-permute-start.2 = (bf16[128,640]{1,0:T(8,128)(2,1)S(1)}, bf16[128,640]{1,0:T(8,128)(2,1)}, u32[]{:S(2)}, u32[]{:S(2)}) collective-permute-start(bf16[128,640]{1,0:T(8,128)(2,1)S(1)} %bitcast.12), channel_id=1, source_target_pairs={{0,16},{1,17},{2,18},{3,19},{4,20},{5,21},{6,22},{7,23},{8,24},{9,... | collective-permute-start | bytes 491528 | tf_op jit(solution)/shard_map/ppermute | solution.py:239
  17.2 8.9 %all-to-all-done.near_ref = bf16[4,288,640]{2,1,0:T(8,128)(2,1)S(1)} async-done(((bf16[4,288,640]{2,1,0:T(8,128)(2,1)}), bf16[4,288,640]{2,1,0:T(8,128)(2,1)S(1)}, u32[]{:S(2)}, u32[]{:S(2)}) %all-to-all-start) | async-done | bytes 1474592 | tf_op jit(solution)/shard_map/all_to_all | solution.py:21
  26.0 9.7 %collective-permute-start.1 = (bf16[4,288,640]{2,1,0:T(8,128)(2,1)S(1)}, bf16[4,288,640]{2,1,0:T(8,128)(2,1)S(1)}, u32[]{:S(2)}, u32[]{:S(2)}) collective-permute-start(bf16[4,288,640]{2,1,0:T(8,128)(2,1)S(1)} %all-to-all-done.near_ref), channel_id=1, source_target_pairs={{0,1},{1,0},{2,3},{3,2},{4,5},{5,4},{6,7},{7,6},{8,9},{9,8},{10,11... | collective-permute-start | bytes 4423688 | tf_op jit(solution)/shard_map/ppermute | solution.py:260
  35.8 6.3 %collective-permute-start.3 = (bf16[128,640]{1,0:T(8,128)(2,1)S(1)}, bf16[128,640]{1,0:T(8,128)(2,1)S(1)}, u32[]{:S(2)}, u32[]{:S(2)}) collective-permute-start(bf16[128,640]{1,0:T(8,128)(2,1)S(1)} %bitcast_select_fusion), channel_id=1, source_target_pairs={{0,96},{1,97},{2,98},{3,99},{4,100},{5,101},{6,102},{7,103},{8,104... | collective-permute-start | bytes 491528 | tf_op jit(solution)/shard_map/ppermute | solution.py:240
  42.1 7.1 %collective-permute-start.4 = (bf16[128,640]{1,0:T(8,128)(2,1)S(1)}, bf16[128,640]{1,0:T(8,128)(2,1)}, u32[]{:S(2)}, u32[]{:S(2)}) collective-permute-start(bf16[128,640]{1,0:T(8,128)(2,1)S(1)} %bitcast_select_fusion), channel_id=1, source_target_pairs={{0,416},{1,417},{2,418},{3,419},{4,420},{5,421},{6,422},{7,423},{8... | collective-permute-start | bytes 491528 | tf_op jit(solution)/shard_map/ppermute | solution.py:240
  49.2 2.9 %collective-permute-done.4 = bf16[128,640]{1,0:T(8,128)(2,1)} collective-permute-done((bf16[128,640]{1,0:T(8,128)(2,1)S(1)}, bf16[128,640]{1,0:T(8,128)(2,1)}, u32[]{:S(2)}, u32[]{:S(2)}) %collective-permute-start.4) | collective-permute-done | bytes 163872 | tf_op jit(solution)/shard_map/ppermute | solution.py:240
  52.1 1.0 add_select_fusion.1
  53.0 0.7 collective-permute-start.5
  53.8 1.3 collective-permute-start.8
  55.1 1.3 collective-permute-start.6
  56.4 2.0 %collective-permute-start.7 = (bf16[128,640]{1,0:T(8,128)(2,1)S(1)}, bf16[128,640]{1,0:T(8,128)(2,1)}, u32[]{:S(2)}, u32[]{:S(2)}) collective-permute-start(bf16[128,640]{1,0:T(8,128)(2,1)S(1)} %broadcast_select_fusion), channel_id=1, source_target_pairs={{0,32},{96,128},{192,224},{320,352},{416,448},{1,33},{97,129},{193... | collective-permute-start | bytes 491528 | tf_op jit(solution)/shard_map/ppermute | solution.py:252
  58.4 0.1 constant_dynamic-slice_fusion
  58.4 2.2 %collective-permute-done.7 = bf16[128,640]{1,0:T(8,128)(2,1)} collective-permute-done((bf16[128,640]{1,0:T(8,128)(2,1)S(1)}, bf16[128,640]{1,0:T(8,128)(2,1)}, u32[]{:S(2)}, u32[]{:S(2)}) %collective-permute-start.7) | collective-permute-done | bytes 163872 | tf_op jit(solution)/shard_map/ppermute | solution.py:252
  60.6 1.0 add_select_fusion.refs_0_
  61.7 4.1 %collective-permute-start.9 = (bf16[128,640]{1,0:T(8,128)(2,1)S(1)}, bf16[128,640]{1,0:T(8,128)(2,1)S(1)}, u32[]{:S(2)}, u32[]{:S(2)}) collective-permute-start(bf16[128,640]{1,0:T(8,128)(2,1)S(1)} %add_select_fusion.refs_0_), channel_id=1, source_target_pairs={{0,16},{8,24},{16,0},{24,8},{1,17},{9,25},{17,1},{25,9},{2,18},{10... | collective-permute-start | bytes 491528 | tf_op jit(solution)/shard_map/ppermute | solution.py:256
  65.8 4.5 %collective-permute-start.10 = (bf16[128,640]{1,0:T(8,128)(2,1)S(1)}, bf16[128,640]{1,0:T(8,128)(2,1)S(1)}, u32[]{:S(2)}, u32[]{:S(2)}) collective-permute-start(bf16[128,640]{1,0:T(8,128)(2,1)S(1)} %add_select_fusion.refs_0_), channel_id=1, source_target_pairs={{0,8},{8,0},{16,24},{24,16},{1,9},{9,1},{17,25},{25,17},{2,10},{10... | collective-permute-start | bytes 491528 | tf_op jit(solution)/shard_map/ppermute | solution.py:256
  70.3 1.9 %collective-permute-start.11 = (bf16[128,640]{1,0:T(8,128)(2,1)S(1)}, bf16[128,640]{1,0:T(8,128)(2,1)}, u32[]{:S(2)}, u32[]{:S(2)}) collective-permute-start(bf16[128,640]{1,0:T(8,128)(2,1)S(1)} %add_select_fusion.refs_0_), channel_id=1, source_target_pairs={{0,24},{8,16},{16,8},{24,0},{1,25},{9,17},{17,9},{25,1},{2,26},{10... | collective-permute-start | bytes 491528 | tf_op jit(solution)/shard_map/ppermute | solution.py:258
  72.3 0.1 dynamic-slice_subtract_fusion.swap_ref
  72.3 0.1 copy.7.pairs_ref
  72.4 0.1 pad_add_fusion.place_ref
  72.5 2.9 %collective-permute-done.10.refs_2_ = bf16[128,640]{1,0:T(8,128)(2,1)S(1)} collective-permute-done((bf16[128,640]{1,0:T(8,128)(2,1)S(1)}, bf16[128,640]{1,0:T(8,128)(2,1)S(1)}, u32[]{:S(2)}, u32[]{:S(2)}) %collective-permute-start.10) | collective-permute-done | bytes 163872 | tf_op jit(solution)/shard_map/ppermute | solution.py:256
  75.4 3.0 %collective-permute-done.11.refs_3_ = bf16[128,640]{1,0:T(8,128)(2,1)} collective-permute-done((bf16[128,640]{1,0:T(8,128)(2,1)S(1)}, bf16[128,640]{1,0:T(8,128)(2,1)}, u32[]{:S(2)}, u32[]{:S(2)}) %collective-permute-start.11) | collective-permute-done | bytes 163872 | tf_op jit(solution)/shard_map/ppermute | solution.py:258
  78.4 4.0 %shard_map.47 = bf16[32,4,1024]{2,1,0:T(4,128)(2,1)S(1)} custom-call(s32[3]{0:T(128)S(1)} %pad_add_fusion.place_ref, bf16[4,288,640]{2,1,0:T(8,128)(2,1)S(1)} %all-to-all-done.near_ref, bf16[4,288,640]{2,1,0:T(8,128)(2,1)S(1)} %collective-permute-done.1.far_ref, bf16[128,640]{1,0:T(8,128)(2,1)S(1)} %add_select_fusion.refs_0_, ...), custom_call_target="tpu_custom_call" | custom-call | flops 1509949440 | bytes 2949120 | tf_op jit(solution)/shard_map/pallas_call | solution.py:92
  82.3 35.5 %all_to_all.15.parts_ref = bf16[32,4,1024]{2,1,0:T(4,128)(2,1)S(1)} all-to-all(bf16[32,4,1024]{2,1,0:T(4,128)(2,1)S(1)} %shard_map.47), channel_id=1, replica_groups=mesh['z'=16,'yl'=2,'yh'=2,'x'=4,'core'=2] {'z','yl'}, dimensions={0} | all-to-all | bytes 524288 | tf_op jit(solution)/shard_map/all_to_all | solution.py:21
  117.9 15.1 %all_to_all.16.every_ref = bf16[16,4,1024]{2,1,0:T(4,128)(2,1)S(1)} all-to-all(bf16[16,4,1024]{2,1,0:T(4,128)(2,1)S(1)} %shard_map.48), channel_id=1, replica_groups=mesh['z'=16,'yl'=2,'yh'=2,'x'=4,'core'=2] {'yh','x','core'}, dimensions={0} | all-to-all | bytes 262144 | tf_op jit(solution)/shard_map/all_to_all | solution.py:21
  133.0 1.6 %shard_map.49 = f32[4,4,256]{2,1,0:T(4,128)} custom-call(s32[4,2]{1,0:T(4,128)S(1)} %copy.7.pairs_ref, s32[4]{0:T(128)S(1)} %dynamic-slice_subtract_fusion.swap_ref, bf16[16,4,1024]{2,1,0:T(4,128)(2,1)S(1)} %all_to_all.16.every_ref), custom_call_target="tpu_custom_call" | custom-call | flops 6553600 | bytes 262144 | tf_op jit(solution)/shard_map/pallas_call | solution.py:211
  (18 shorter events, 0.2 us)
Async XLA Ops:
  0.0 58.4 %copy-start = (s32[64,2]{0,1:T(2,128)S(1)}, s32[64,2]{0,1:T(2,128)}, u32[]{:S(2)}) copy-start(s32[64,2]{0,1:T(2,128)} %param.7) | copy-start | bytes 1540
  0.0 7.1 %collective-permute-start = (bf16[8,1024]{1,0:T(8,128)(2,1)}, bf16[8,1024]{1,0:T(8,128)(2,1)S(1)}, u32[]{:S(2)}, u32[]{:S(2)}) collective-permute-start(bf16[8,1024]{1,0:T(8,128)(2,1)} %amps_ref.1), channel_id=1, source_target_pairs={{0,8},{8,0},{1,9},{9,1},{2,10},{10,2},{3,11},{11,3},{4,12},{12,4},... | collective-permute-start | bytes 49160 | tf_op jit(solution)/shard_map/ppermute | solution.py:231
  7.1 0.7 copy-start.1
  9.1 4.2 %copy-start.2 = (bf16[8,32,640]{2,1,0:T(8,128)(2,1)S(1)}, bf16[8,32,640]{2,1,0:T(8,128)(2,1)}, u32[]{:S(2)}) copy-start(bf16[8,32,640]{2,1,0:T(8,128)(2,1)} %param.5) | copy-start | bytes 983044
  9.1 17.0 %all-to-all-start = ((bf16[4,288,640]{2,1,0:T(8,128)(2,1)}), bf16[4,288,640]{2,1,0:T(8,128)(2,1)S(1)}, u32[]{:S(2)}, u32[]{:S(2)}) async-start(bf16[4,288,640]{2,1,0:T(8,128)(2,1)} %shard_map.46), calls=%async_computation | async-start | bytes 2949120 | tf_op jit(solution)/shard_map/all_to_all | solution.py:21
  13.3 59.0 %copy-start.3 = (s32[128]{0:T(128)S(1)}, s32[128]{0:T(128)}, u32[]{:S(2)}) copy-start(s32[128]{0:T(128)} %param.8) | copy-start | bytes 1540
  13.3 22.5 %collective-permute-start.2 = (bf16[128,640]{1,0:T(8,128)(2,1)S(1)}, bf16[128,640]{1,0:T(8,128)(2,1)}, u32[]{:S(2)}, u32[]{:S(2)}) collective-permute-start(bf16[128,640]{1,0:T(8,128)(2,1)S(1)} %bitcast.12), channel_id=1, source_target_pairs={{0,16},{1,17},{2,18},{3,19},{4,20},{5,21},{6,22},{7,23},{8,24},{9,... | collective-permute-start | bytes 491528 | tf_op jit(solution)/shard_map/ppermute | solution.py:239
  26.0 46.5 %collective-permute-start.1 = (bf16[4,288,640]{2,1,0:T(8,128)(2,1)S(1)}, bf16[4,288,640]{2,1,0:T(8,128)(2,1)S(1)}, u32[]{:S(2)}, u32[]{:S(2)}) collective-permute-start(bf16[4,288,640]{2,1,0:T(8,128)(2,1)S(1)} %all-to-all-done.near_ref), channel_id=1, source_target_pairs={{0,1},{1,0},{2,3},{3,2},{4,5},{5,4},{6,7},{7,6},{8,9},{9,8},{10,11... | collective-permute-start | bytes 4423688 | tf_op jit(solution)/shard_map/ppermute | solution.py:260
  35.8 13.4 %collective-permute-start.3 = (bf16[128,640]{1,0:T(8,128)(2,1)S(1)}, bf16[128,640]{1,0:T(8,128)(2,1)S(1)}, u32[]{:S(2)}, u32[]{:S(2)}) collective-permute-start(bf16[128,640]{1,0:T(8,128)(2,1)S(1)} %bitcast_select_fusion), channel_id=1, source_target_pairs={{0,96},{1,97},{2,98},{3,99},{4,100},{5,101},{6,102},{7,103},{8,104... | collective-permute-start | bytes 491528 | tf_op jit(solution)/shard_map/ppermute | solution.py:240
  42.1 10.0 %collective-permute-start.4 = (bf16[128,640]{1,0:T(8,128)(2,1)S(1)}, bf16[128,640]{1,0:T(8,128)(2,1)}, u32[]{:S(2)}, u32[]{:S(2)}) collective-permute-start(bf16[128,640]{1,0:T(8,128)(2,1)S(1)} %bitcast_select_fusion), channel_id=1, source_target_pairs={{0,416},{1,417},{2,418},{3,419},{4,420},{5,421},{6,422},{7,423},{8... | collective-permute-start | bytes 491528 | tf_op jit(solution)/shard_map/ppermute | solution.py:240
  53.0 0.7 collective-permute-start.5
  53.8 4.7 %collective-permute-start.8 = (bf16[128,640]{1,0:T(8,128)(2,1)S(1)}, bf16[128,640]{1,0:T(8,128)(2,1)S(1)}, u32[]{:S(2)}, u32[]{:S(2)}) collective-permute-start(bf16[128,640]{1,0:T(8,128)(2,1)S(1)} %broadcast_select_fusion), channel_id=1, source_target_pairs={{96,64},{192,160},{320,288},{416,384},{0,480},{97,65},{193,161},{3... | collective-permute-start | bytes 491528 | tf_op jit(solution)/shard_map/ppermute | solution.py:252
  55.1 3.4 %collective-permute-start.6 = (bf16[128,640]{1,0:T(8,128)(2,1)S(1)}, bf16[128,640]{1,0:T(8,128)(2,1)}, u32[]{:S(2)}, u32[]{:S(2)}) collective-permute-start(bf16[128,640]{1,0:T(8,128)(2,1)S(1)} %broadcast_select_fusion), channel_id=1, source_target_pairs={{192,256},{193,257},{194,258},{195,259},{196,260},{197,261},{198,2... | collective-permute-start | bytes 491528 | tf_op jit(solution)/shard_map/ppermute | solution.py:251
  56.4 4.2 %collective-permute-start.7 = (bf16[128,640]{1,0:T(8,128)(2,1)S(1)}, bf16[128,640]{1,0:T(8,128)(2,1)}, u32[]{:S(2)}, u32[]{:S(2)}) collective-permute-start(bf16[128,640]{1,0:T(8,128)(2,1)S(1)} %broadcast_select_fusion), channel_id=1, source_target_pairs={{0,32},{96,128},{192,224},{320,352},{416,448},{1,33},{97,129},{193... | collective-permute-start | bytes 491528 | tf_op jit(solution)/shard_map/ppermute | solution.py:252
  61.7 10.8 %collective-permute-start.9 = (bf16[128,640]{1,0:T(8,128)(2,1)S(1)}, bf16[128,640]{1,0:T(8,128)(2,1)S(1)}, u32[]{:S(2)}, u32[]{:S(2)}) collective-permute-start(bf16[128,640]{1,0:T(8,128)(2,1)S(1)} %add_select_fusion.refs_0_), channel_id=1, source_target_pairs={{0,16},{8,24},{16,0},{24,8},{1,17},{9,25},{17,1},{25,9},{2,18},{10... | collective-permute-start | bytes 491528 | tf_op jit(solution)/shard_map/ppermute | solution.py:256
  65.8 9.6 %collective-permute-start.10 = (bf16[128,640]{1,0:T(8,128)(2,1)S(1)}, bf16[128,640]{1,0:T(8,128)(2,1)S(1)}, u32[]{:S(2)}, u32[]{:S(2)}) collective-permute-start(bf16[128,640]{1,0:T(8,128)(2,1)S(1)} %add_select_fusion.refs_0_), channel_id=1, source_target_pairs={{0,8},{8,0},{16,24},{24,16},{1,9},{9,1},{17,25},{25,17},{2,10},{10... | collective-permute-start | bytes 491528 | tf_op jit(solution)/shard_map/ppermute | solution.py:256
  70.3 8.0 %collective-permute-start.11 = (bf16[128,640]{1,0:T(8,128)(2,1)S(1)}, bf16[128,640]{1,0:T(8,128)(2,1)}, u32[]{:S(2)}, u32[]{:S(2)}) collective-permute-start(bf16[128,640]{1,0:T(8,128)(2,1)S(1)} %add_select_fusion.refs_0_), channel_id=1, source_target_pairs={{0,24},{8,16},{16,8},{24,0},{1,25},{9,17},{17,9},{25,1},{2,26},{10... | collective-permute-start | bytes 491528 | tf_op jit(solution)/shard_map/ppermute | solution.py:258
